TPU v7x, 32 devices: a whole 2x2x4 slice. The times are simulated.
32 devices in a mesh: groups: 2 (over x), ep: 8 (over z, y), rep: 2 (over core).
Axes of the slice: x: 2, y: 2, z: 4, core: 2. Of those that a mesh axis runs over, the one named last changes fastest.
Arguments:
- tokens: bfloat16 [512, 3584], P(('groups', 'ep'), 'rep'), parts along dimension 0, may hold values from -6 to 6
- expert_ids: int32 [512, 1], P(('groups', 'ep')), parts along dimension 0, may hold values from 0 to 3; in each aligned block of 32 rows (0 to 31, 32 to 63, ...) at most 10 rows name the same one
- gate_values: float32 [512, 1], P(('groups', 'ep')), parts along dimension 0, may hold values from 0.1 to 0.6
- slot_expert: int32 [8], replicated, may hold values from 0 to 3, as said below
- gate_weight: bfloat16 [8, 3584, 1024], P('ep', None, 'rep'), as said below
- up_weight: bfloat16 [8, 3584, 1024], P('ep', None, 'rep'), as said below
- down_weight: bfloat16 [8, 1024, 3584], P('ep', 'rep'), as said below
Outputs:
- combined: bfloat16 [512, 3584], P(('groups', 'ep'), 'rep'), parts along dimension 0
There are 2 independent parts, one for each index of `groups`. A program takes and returns all parts, laid end to end along the dimension named above; an argument that names none is the same for every part. Nothing has to cross between parts.
Inputs may be any that keep to these rules, and one draw needn't show every extreme that they name: `expert_ids`: each row names 1 different experts. Among the 32 rows of one index of ep (aligned blocks) no expert is named more than 10 times, and in some blocks one expert is named exactly 10 times. `slot_expert`: every expert is held by 1 to 4 slots, and some experts by 4. gate_weight[s] equals gate_weight[r] whenever slot_expert[s] equals slot_expert[r]. up_weight[s] equals up_weight[r] whenever slot_expert[s] equals slot_expert[r]. down_weight[s] equals down_weight[r] whenever slot_expert[s] equals slot_expert[r].
All inputs are finite; a program needn't handle non-finite values.
Results may differ from a plain program's by a relative error of at most 0.0057.
Values may be sent and summed in bfloat16 or wider, within the bound.
No kernel may reach another device: no remote copies, remote signals or barrier semaphores. Data moves between devices by JAX's collectives and lax.ppermute only.
A program may use at most 128 MiB of HBM per device.

v0:
```python
import jax
import jax.numpy as jnp
from jax import lax
from jax.sharding import PartitionSpec as P


def tile_apply(source, out_type, worker):
    return worker(source).astype(out_type)


def exclusive_count(onehot):
    return jnp.sum((jnp.cumsum(onehot, axis=0) - onehot) * onehot, axis=1)


def body(tokens, expert_ids, gate_values, slot_expert, gate_weight, up_weight, down_weight):
    tok_rows, choices_per = expert_ids.shape
    feat_half = tokens.shape[1]
    slot_total = slot_expert.shape[0]
    experts = slot_total // 2
    capacity = tok_rows * choices_per * 5 // (4 * experts)
    pair_count = tok_rows * choices_per
    expert_iota = jnp.arange(experts, dtype=jnp.int32)
    slot_iota = jnp.arange(slot_total, dtype=jnp.int32)
    holding = (slot_expert[:, None] == expert_iota[None, :]).astype(jnp.int32)
    copies = jnp.sum(holding, axis=0)
    copy_rank = exclusive_count(holding)
    pair_expert = expert_ids.reshape(pair_count)
    picked = (pair_expert[:, None] == expert_iota[None, :]).astype(jnp.int32)
    pair_copies = jnp.sum(picked * copies[None, :], axis=1)
    chosen = lax.axis_index("ep") % pair_copies
    matched = (slot_expert[None, :] == pair_expert[:, None]) & (
        copy_rank[None, :] == chosen[:, None]
    )
    target = jnp.sum(jnp.where(matched, slot_iota[None, :], 0), axis=1)
    to_target = (target[:, None] == slot_iota[None, :]).astype(jnp.int32)
    position = exclusive_count(to_target)
    flat_slot = target * capacity + position
    filler = (
        jnp.full((slot_total * capacity,), pair_count, jnp.int32)
        .at[flat_slot]
        .set(jnp.arange(pair_count, dtype=jnp.int32))
    )
    padded = jnp.concatenate([tokens, jnp.zeros((1, feat_half), tokens.dtype)], axis=0)
    send_rows = padded[filler // choices_per].reshape(slot_total, capacity, feat_half)
    send_live = (filler < pair_count).astype(jnp.bfloat16).reshape(slot_total, capacity)
    gate_local = gate_weight[0]
    up_local = up_weight[0]
    down_local = down_weight[0]
    down_cols = lax.all_to_all(down_local, "rep", split_axis=1, concat_axis=0, tiled=True)
    arrived_rows = lax.all_to_all(send_rows, "ep", split_axis=0, concat_axis=0, tiled=True)
    live_flags = lax.all_to_all(send_live, "ep", split_axis=0, concat_axis=0, tiled=True)
    senders, per_sender = live_flags.shape
    row_total = senders * per_sender
    full_rows = lax.all_gather(arrived_rows, "rep", axis=2, tiled=True).reshape(row_total, -1)
    gate_proj = jnp.dot(full_rows, gate_local, preferred_element_type=jnp.float32)
    up_proj = jnp.dot(full_rows, up_local, preferred_element_type=jnp.float32)
    gathered = lax.all_gather(
        (jax.nn.silu(gate_proj) * up_proj).astype(jnp.bfloat16), "rep", axis=1, tiled=True
    )
    result = tile_apply(
        gathered,
        jnp.bfloat16,
        lambda tile_block: jnp.dot(tile_block, down_cols, preferred_element_type=jnp.float32),
    )
    outbound = result.reshape(senders, per_sender, result.shape[1])
    returned = lax.all_to_all(outbound, "ep", split_axis=0, concat_axis=0, tiled=True)
    arrived = returned.reshape(slot_total * capacity, feat_half)[flat_slot].reshape(
        tok_rows, choices_per, feat_half
    )
    combined = jnp.sum(gate_values[:, :, None] * arrived.astype(jnp.float32), axis=1)
    return combined.astype(jnp.bfloat16)


def solution(mesh):
    return jax.shard_map(
        body,
        mesh=mesh,
        in_specs=(
            P(("groups", "ep"), "rep"),
            P(("groups", "ep"), None),
            P(("groups", "ep"), None),
            P(),
            P("ep", None, "rep"),
            P("ep", None, "rep"),
            P("ep", "rep", None),
        ),
        out_specs=P(("groups", "ep"), "rep"),
        check_vma=False,
    )
```

profile of v0, /device:TPU:0, one launch (start us, length us, event | category | flops | bytes accessed | tf_op | source)
XLA Modules:
  0.0 66.9 jit_solution(18184998266238128169)
XLA Ops:
  0.0 6.0 %copy.10 = bf16[1,512,3584]{1,2,0:T(8,128)(2,1)} copy(bf16[1,512,3584]{2,1,0:T(8,128)(2,1)} %param.13) | data formatting | bytes 7340032 | tf_op args[6]
  6.0 0.0 copy-start.2
  6.0 0.0 copy-start.4
  6.0 0.0 copy-start.1
  6.0 5.5 %all-to-all-start.1 = ((bf16[512,2,1792]{0,2,1:T(8,128)(2,1)}), bf16[512,2,1792]{0,2,1:T(8,128)(2,1)}, u32[]{:S(2)}, u32[]{:S(2)}) async-start(bf16[512,2,1792]{0,2,1:T(8,128)(2,1)} %bitcast.23), calls=%async_computation.1 | async-start | bytes 7340032 | tf_op jit(solution)/shard_map/all_to_all | solution.py:49
  11.5 0.0 copy-done.2
  11.5 0.2 reduce_window_sum.22
  11.7 0.1 fusion.12
  11.8 0.0 copy-done.4
  11.8 0.1 select_reduce_fusion.2
  11.9 0.1 and_select_fusion
  12.1 0.2 select_reduce_fusion.1
  12.2 0.1 fusion.10
  12.3 0.1 reduce_window_sum.23
  12.4 0.2 select_reduce_fusion
  12.6 0.7 %scatter_custom_fusion = s32[80]{0:T(128)S(1)} fusion(s32[32]{0:T(128)S(1)} %fusion.13, s32[32]{0:T(128)S(1)} %iota.12, s32[]{:T(128)} %constant.40.clone.1), kind=kCustom, calls=%fused_computation.29 | custom fusion | bytes 324 | tf_op jit(solution)/shard_map/scatter | solution.py:41
  13.3 0.0 copy-done.1
  13.3 0.8 %gather_fusion = bf16[80,1792]{1,0:T(8,128)(2,1)S(1)} fusion(bf16[33,1792]{1,0:T(8,128)(2,1)S(1)} %concatenate.3, s32[1024]{0:T(1024)S(1)} %pad_clamp_fusion.1), kind=kCustom, calls=%fused_computation | custom fusion | bytes 573760 | tf_op jit(solution)/shard_map/gather | solution.py:44
  14.1 0.9 %reshape.73 = bf16[8,10,1792]{2,1,0:T(8,128)(2,1)} reshape(bf16[80,1792]{1,0:T(8,128)(2,1)S(1)} %gather_fusion) | data formatting | bytes 573440 | tf_op jit(solution)/shard_map/reshape | solution.py:44
  15.0 0.7 all-to-all-done.1
  15.6 7.3 %all-to-all-start = ((bf16[8,10,1792]{2,1,0:T(8,128)(2,1)}), bf16[8,10,1792]{2,1,0:T(8,128)(2,1)S(1)}, u32[]{:S(2)}, u32[]{:S(2)}) async-start(bf16[8,10,1792]{2,1,0:T(8,128)(2,1)} %reshape.73), calls=%async_computation | async-start | bytes 917504 | tf_op jit(solution)/shard_map/all_to_all | solution.py:50
  22.9 6.0 %copy.11 = bf16[2,512,1792]{2,1,0:T(8,128)(2,1)} copy(bf16[2,512,1792]{1,2,0:T(8,128)(2,1)} %bitcast.7) | data formatting | bytes 7340032 | tf_op jit(solution)/shard_map/all_to_all | solution.py:49
  28.9 7.4 %all-to-all-done = bf16[8,10,1792]{2,1,0:T(8,128)(2,1)S(1)} async-done(((bf16[8,10,1792]{2,1,0:T(8,128)(2,1)}), bf16[8,10,1792]{2,1,0:T(8,128)(2,1)S(1)}, u32[]{:S(2)}, u32[]{:S(2)}) %all-to-all-start) | async-done | bytes 286752 | tf_op jit(solution)/shard_map/all_to_all | solution.py:50
  36.3 2.5 %all_gather.6 = bf16[8,10,3584]{2,1,0:T(8,128)(2,1)S(1)} all-gather(bf16[8,10,1792]{2,1,0:T(8,128)(2,1)S(1)} %all-to-all-done), channel_id=1, replica_groups=mesh['groups'=2,'ep'=8,'rep'=2] {'rep'}, dimensions={2}, use_global_device_ids=true | all-gather | bytes 860160 | tf_op jit(solution)/shard_map/all_gather | solution.py:54
  38.8 0.2 reshape.74
  39.0 0.0 copy-start
  39.0 2.9 %fusion.2 = f32[80,512]{1,0:T(8,128)S(1)} fusion(bf16[80,3584]{1,0:T(8,128)(2,1)S(1)} %reshape.74, bf16[1,3584,512]{2,1,0:T(8,128)(2,1)} %param.11), kind=kOutput, calls=%fused_computation.5 | convolution fusion | flops 293601280 | bytes 4407296 | tf_op jit(solution)/shard_map/dot_general | solution.py:55
  41.9 2.8 %fusion.7 = bf16[80,512]{1,0:T(8,128)(2,1)S(1)} fusion(bf16[80,3584]{1,0:T(8,128)(2,1)S(1)} %reshape.74, bf16[1,3584,512]{2,1,0:T(8,128)(2,1)} %param.12, f32[80,512]{1,0:T(8,128)S(1)} %fusion.2), kind=kOutput, calls=%fused_computation.9 | convolution fusion | flops 293847040 | bytes 4489216 | tf_op jit(solution)/shard_map/dot_general | solution.py:56
  44.7 1.9 %all_gather.7 = bf16[80,1024]{1,0:T(8,128)(2,1)S(1)} all-gather(bf16[80,512]{1,0:T(8,128)(2,1)S(1)} %fusion.7), channel_id=1, replica_groups=mesh['groups'=2,'ep'=8,'rep'=2] {'rep'}, dimensions={1}, use_global_device_ids=true | all-gather | bytes 245760 | tf_op jit(solution)/shard_map/all_gather | solution.py:57
  46.6 0.0 copy-done
  46.6 0.0 copy-start.3
  46.6 0.8 %convolution_convert_fusion = bf16[80,1792]{1,0:T(8,128)(2,1)S(1)} fusion(bf16[80,1024]{1,0:T(8,128)(2,1)S(1)} %all_gather.7, bf16[1024,1792]{1,0:T(8,128)(2,1)S(1)} %bitcast.24), kind=kOutput, calls=%fused_computation.7 | convolution fusion | flops 293744640 | bytes 4120576 | tf_op jit(solution)/shard_map/dot_general | solution.py:63
  47.4 0.9 %reshape.75 = bf16[8,10,1792]{2,1,0:T(8,128)(2,1)} reshape(bf16[80,1792]{1,0:T(8,128)(2,1)S(1)} %convolution_convert_fusion) | data formatting | bytes 573440 | tf_op jit(solution)/shard_map/reshape | solution.py:65
  48.3 3.6 %all-to-all-start.2 = ((bf16[8,10,1792]{2,1,0:T(8,128)(2,1)}), bf16[8,10,1792]{2,1,0:T(8,128)(2,1)S(1)}, u32[]{:S(2)}, u32[]{:S(2)}) async-start(bf16[8,10,1792]{2,1,0:T(8,128)(2,1)} %reshape.75), calls=%async_computation.2 | async-start | bytes 917504 | tf_op jit(solution)/shard_map/all_to_all | solution.py:66
  51.9 13.4 %all-to-all-done.2 = bf16[8,10,1792]{2,1,0:T(8,128)(2,1)S(1)} async-done(((bf16[8,10,1792]{2,1,0:T(8,128)(2,1)}), bf16[8,10,1792]{2,1,0:T(8,128)(2,1)S(1)}, u32[]{:S(2)}, u32[]{:S(2)}) %all-to-all-start.2) | async-done | bytes 286752 | tf_op jit(solution)/shard_map/all_to_all | solution.py:66
  65.4 0.1 reshape.76
  65.5 0.6 gather_fusion.1
  66.1 0.0 copy-done.3
  66.1 0.7 %multiply_convert_fusion = bf16[32,1792]{1,0:T(8,128)(2,1)} fusion(bf16[32,1792]{1,0:T(8,128)(2,1)S(1)} %gather_fusion.1, f32[32]{0:T(128)S(1)} %bitcast.25), kind=kLoop, calls=%fused_computation.10 | loop fusion | flops 172032 | bytes 229504 | tf_op jit(solution)/shard_map/convert_element_type | solution.py:71
  (7 shorter events, 0.0 us)
Async XLA Ops:
  6.0 5.6 %copy-start.2 = (s32[8]{0:T(128)S(1)}, s32[8]{0:T(128)}, u32[]{:S(2)}) copy-start(s32[8]{0:T(128)} %param.10) | copy-start | bytes 100
  6.0 5.9 %copy-start.4 = (s32[32,1]{0,1:T(1,128)S(1)}, s32[32,1]{0,1:T(1,128)}, u32[]{:S(2)}) copy-start(s32[32,1]{0,1:T(1,128)} %param.8) | copy-start | bytes 388
  6.0 7.3 %copy-start.1 = (bf16[32,1792]{1,0:T(8,128)(2,1)S(1)}, bf16[32,1792]{1,0:T(8,128)(2,1)}, u32[]{:S(2)}) copy-start(bf16[32,1792]{1,0:T(8,128)(2,1)} %param.7) | copy-start | bytes 344068
  6.0 9.7 %all-to-all-start.1 = ((bf16[512,2,1792]{0,2,1:T(8,128)(2,1)}), bf16[512,2,1792]{0,2,1:T(8,128)(2,1)}, u32[]{:S(2)}, u32[]{:S(2)}) async-start(bf16[512,2,1792]{0,2,1:T(8,128)(2,1)} %bitcast.23), calls=%async_computation.1 | async-start | bytes 7340032 | tf_op jit(solution)/shard_map/all_to_all | solution.py:49
  15.6 20.7 %all-to-all-start = ((bf16[8,10,1792]{2,1,0:T(8,128)(2,1)}), bf16[8,10,1792]{2,1,0:T(8,128)(2,1)S(1)}, u32[]{:S(2)}, u32[]{:S(2)}) async-start(bf16[8,10,1792]{2,1,0:T(8,128)(2,1)} %reshape.73), calls=%async_computation | async-start | bytes 917504 | tf_op jit(solution)/shard_map/all_to_all | solution.py:50
  39.0 7.7 %copy-start = (bf16[2,512,1792]{2,1,0:T(8,128)(2,1)S(1)}, bf16[2,512,1792]{2,1,0:T(8,128)(2,1)}, u32[]{:S(2)}) copy-start(bf16[2,512,1792]{2,1,0:T(8,128)(2,1)} %copy.11) | copy-start | bytes 11010052
  46.6 19.5 %copy-start.3 = (f32[32,1]{0,1:T(1,128)S(1)}, f32[32,1]{0,1:T(1,128)}, u32[]{:S(2)}) copy-start(f32[32,1]{0,1:T(1,128)} %param.9) | copy-start | bytes 388
  48.3 17.1 %all-to-all-start.2 = ((bf16[8,10,1792]{2,1,0:T(8,128)(2,1)}), bf16[8,10,1792]{2,1,0:T(8,128)(2,1)S(1)}, u32[]{:S(2)}, u32[]{:S(2)}) async-start(bf16[8,10,1792]{2,1,0:T(8,128)(2,1)} %reshape.75), calls=%async_computation.2 | async-start | bytes 917504 | tf_op jit(solution)/shard_map/all_to_all | solution.py:66
where the time goes:
time: 67.5 us; the launch traced here: 66.9 us
  waiting for transfers between devices  21.5 us (32%)
  starting transfers between devices  16.5 us (24%)
  local copies, waits for them, and re-layouts  16.1 us (24%)
  matrix products  6.5 us (10%)
  blocking collectives  4.37 us (6%)
  other arithmetic  1.77 us (3%)
    all_to_all x1, waiting for transfers between devices, body(): lax.all_to_all(outbound, 'ep', split_axis=0, concat_axis=0, tiled=True)  13.4 us
    all_to_all x1, waiting for transfers between devices, body(): lax.all_to_all(send_rows, 'ep', split_axis=0, concat_axis=0, tiled=True)  7.41 us
    all_to_all x1, starting transfers between devices, body(): lax.all_to_all(send_rows, 'ep', split_axis=0, concat_axis=0, tiled=True)  7.31 us
    all_to_all x1, local copies, waits for them, and re-layouts, body(): lax.all_to_all(down_local, 'rep', split_axis=1, concat_axis=0, tiled=True)  5.98 us
    unnamed x11, local copies, waits for them, and re-layouts  5.97 us
    all_to_all x1, starting transfers between devices, body(): lax.all_to_all(down_local, 'rep', split_axis=1, concat_axis=0, tiled=True)  5.55 us
    all_to_all x1, starting transfers between devices, body(): lax.all_to_all(outbound, 'ep', split_axis=0, concat_axis=0, tiled=True)  3.63 us
    dot_general x1, matrix products, body(): jnp.dot(full_rows, gate_local, preferred_element_type=jnp.float32)  2.94 us
  transfers between devices with their start and end apart: 3, of which 3 were waited for; matrix products, arithmetic and copies ran while one was open for 14% of the time, Pallas kernels for 0%

commit v1 on v0

v1 whole, which is shorter than its diff:
```python
import functools

import jax
import jax.numpy as jnp
from jax import lax
from jax.experimental import pallas as pl
from jax.experimental.pallas import tpu as pltpu
from jax.sharding import PartitionSpec as P

LANES = 128
SUBLANES = 8
MIB = 1 << 20
F32 = jnp.float32
BF16 = jnp.bfloat16
TRANS_LHS = (((0,), (0,)), ((), ()))


class Plan:
    def __init__(self, tok, choices, feat, slots):
        experts = slots // 2
        self.tok, self.choices, self.feat, self.slots = tok, choices, feat, slots
        self.capacity = tok * choices * 5 // (4 * experts)
        assert feat % LANES == 0
        self.blocks = feat // LANES
        self.full = self.capacity // SUBLANES
        self.main = self.full * SUBLANES
        self.tail = self.capacity - self.main
        self.group = SUBLANES // self.tail if self.tail else 0
        self.tail_tiles = -(-self.blocks // self.group) if self.tail else 0
        self.tiles = self.full * self.blocks + self.tail_tiles
        self.main_rows = slots * self.main
        self.tail_rows = slots * self.tail
        self.rows = self.main_rows + self.tail_rows
        self.tail_wide = slots * SUBLANES if self.tail else 0
        self.wide = self.main_rows + self.tail_wide
        self.packed = (slots, self.tiles, SUBLANES, LANES)


def iota(shape, dim):
    return lax.broadcasted_iota(jnp.int32, shape, dim)


def floor_div(values, divisor):
    return jnp.floor((values.astype(F32) + 0.5) * (1.0 / divisor)).astype(jnp.int32)


def route(plan, member, slot_row, ids):
    slots, tok = plan.slots, plan.tok
    square = (slots, slots)
    down, across = iota(square, 0), iota(square, 1)
    row = jnp.broadcast_to(slot_row.astype(F32), square)
    col = jnp.sum(jnp.where(down == across, row, 0.0), axis=1, keepdims=True)
    same = jnp.where(col == row, 1.0, 0.0)
    copies = jnp.sum(same, axis=0, keepdims=True)
    rank = jnp.sum(jnp.where(down < across, same, 0.0), axis=0, keepdims=True)
    want = jnp.zeros((1, slots), F32)
    for number in (2, 3, 4):
        want = jnp.where(copies == number, lax.rem(member, number).astype(F32), want)
    chosen = rank == want
    hits = [
        jnp.where((ids[:, k : k + 1] == slot_row) & chosen, 1.0, 0.0) for k in range(plan.choices)
    ]
    before = jnp.where(iota((tok, tok), 1) < iota((tok, tok), 0), 1.0, 0.0).astype(BF16)
    counts = jnp.dot(before, sum(hits).astype(BF16), preferred_element_type=F32)
    lane = iota((tok, slots), 1).astype(F32)
    found = []
    for hit in hits:
        slot = jnp.sum(hit * lane, axis=1, keepdims=True).astype(jnp.int32)
        place = jnp.sum(hit * counts, axis=1, keepdims=True).astype(jnp.int32)
        found.append((slot, place))
    return found


def main_hot(plan, slot, place):
    code = jnp.where(place < plan.main, slot * plan.main + place, -1)
    return jnp.where(code == iota((plan.tok, plan.main_rows), 1), 1.0, 0.0)


def tail_hot(plan, slot, place, part):
    code = jnp.where(
        place < plan.main, -1, slot * SUBLANES + place - plan.main + part * plan.tail
    )
    return jnp.where(code == iota((plan.tok, plan.tail_wide), 1), 1.0, 0.0)


def lane_block(index):
    return slice(index * LANES, (index + 1) * LANES)


def pack_kernel(plan, member_ref, slot_ref, ids_ref, tokens_ref, send_ref):
    found = route(plan, member_ref[0], slot_ref[...], ids_ref[...])
    if plan.full:
        hot = sum(main_hot(plan, *pair) for pair in found).astype(BF16)
        main = lax.dot_general(hot, tokens_ref[...], TRANS_LHS, preferred_element_type=F32)
        for block in range(plan.blocks):
            tile = main[:, lane_block(block)].reshape(plan.slots, plan.full, SUBLANES, LANES)
            for index in range(plan.full):
                send_ref[:, index * plan.blocks + block] = tile[:, index].astype(BF16)
    if plan.tail:
        hot = jnp.concatenate(
            [sum(tail_hot(plan, *pair, part) for pair in found) for part in range(plan.group)],
            axis=0,
        ).astype(BF16)
        for index in range(plan.tail_tiles):
            stack = []
            for part in range(plan.group):
                block = index * plan.group + part
                if block < plan.blocks:
                    stack.append(tokens_ref[:, lane_block(block)])
                else:
                    stack.append(jnp.zeros((plan.tok, LANES), BF16))
            tile = lax.dot_general(
                hot, jnp.concatenate(stack, axis=0), TRANS_LHS, preferred_element_type=F32
            )
            send_ref[:, plan.full * plan.blocks + index] = tile.reshape(
                plan.slots, SUBLANES, LANES
            ).astype(BF16)


def flat_tile(tile):
    return tile.astype(F32).reshape(-1, LANES).astype(BF16)


def unpack_rows(plan, packed_ref, rows_ref):
    for block in range(plan.blocks):
        for index in range(plan.full):
            tile = packed_ref[:, index * plan.blocks + block]
            if plan.full == 1:
                rows_ref[0 : plan.main_rows, lane_block(block)] = flat_tile(tile)
            else:
                for sender in range(plan.slots):
                    first = sender * plan.main + index * SUBLANES
                    rows_ref[first : first + SUBLANES, lane_block(block)] = tile[sender]
    if plan.tail:
        shape = (plan.group * plan.tail_rows, plan.tail_wide)
        line = iota(shape, 0)
        part = floor_div(line, plan.tail_rows)
        inner = line - part * plan.tail_rows
        sender = floor_div(inner, plan.tail)
        spot = sender * SUBLANES + part * plan.tail + inner - sender * plan.tail
        hot = jnp.where(spot == iota(shape, 1), 1.0, 0.0).astype(BF16)
        for index in range(plan.tail_tiles):
            tile = flat_tile(packed_ref[:, plan.full * plan.blocks + index])
            moved = jnp.dot(hot, tile, preferred_element_type=F32).astype(BF16)
            for part in range(plan.group):
                block = index * plan.group + part
                if block < plan.blocks:
                    rows_ref[plan.main_rows : plan.rows, lane_block(block)] = moved[
                        part * plan.tail_rows : (part + 1) * plan.tail_rows
                    ]


def own_kernel(plan, core_ref, packed_ref, gate_ref, up_ref, acc_ref, rows_ref):
    unpack_rows(plan, packed_ref, rows_ref)
    first = pl.multiple_of(core_ref[0] * plan.feat, LANES)
    hid = gate_ref.shape[1]
    rows = rows_ref[...]
    acc_ref[:, :hid] = jnp.dot(
        rows, gate_ref[pl.ds(first, plan.feat), :], preferred_element_type=F32
    )
    acc_ref[:, hid:] = jnp.dot(
        rows, up_ref[pl.ds(first, plan.feat), :], preferred_element_type=F32
    )


def emit_packed(plan, product, out_ref):
    for block in range(plan.blocks):
        tile = product[: plan.main_rows, lane_block(block)].reshape(
            plan.slots, plan.full, SUBLANES, LANES
        )
        for index in range(plan.full):
            out_ref[:, index * plan.blocks + block] = tile[:, index].astype(out_ref.dtype)
    for index in range(plan.tail_tiles):
        spot = iota((plan.tail_wide, LANES), 0)
        spot = spot - floor_div(spot, SUBLANES) * SUBLANES
        tile = jnp.zeros((plan.tail_wide, LANES), F32)
        for part in range(plan.group):
            block = index * plan.group + part
            if block < plan.blocks:
                here = (spot >= part * plan.tail) & (spot < (part + 1) * plan.tail)
                tile = jnp.where(here, product[plan.main_rows :, lane_block(block)], tile)
        out_ref[:, plan.full * plan.blocks + index] = tile.reshape(
            plan.slots, SUBLANES, LANES
        ).astype(out_ref.dtype)


def other_kernel(
    plan, core_ref, packed_ref, acc_ref, gate_ref, up_ref, down_ref, hidden_ref, out_ref, rows_ref
):
    unpack_rows(plan, packed_ref, rows_ref)
    first = pl.multiple_of((1 - core_ref[0]) * plan.feat, LANES)
    hid = gate_ref.shape[1]
    rows = rows_ref[...]
    gate = acc_ref[:, :hid] + jnp.dot(
        rows, gate_ref[pl.ds(first, plan.feat), :], preferred_element_type=F32
    )
    up = acc_ref[:, hid:] + jnp.dot(
        rows, up_ref[pl.ds(first, plan.feat), :], preferred_element_type=F32
    )
    hidden = (gate / (1.0 + jnp.exp(-gate)) * up).astype(BF16)
    if plan.full:
        hidden_ref[: plan.main_rows] = hidden[: plan.main_rows]
    if plan.tail:
        shape = (plan.tail_wide, plan.tail_rows)
        line, col = iota(shape, 0), iota(shape, 1)
        sender = floor_div(line, SUBLANES)
        spot = line - sender * SUBLANES
        spot = spot - floor_div(spot, plan.tail) * plan.tail
        hot = jnp.where(sender * plan.tail + spot == col, 1.0, 0.0).astype(BF16)
        hidden_ref[plan.main_rows :] = jnp.dot(
            hot, hidden[plan.main_rows :], preferred_element_type=F32
        ).astype(BF16)
    product = jnp.dot(
        hidden_ref[...], down_ref[:, pl.ds(first, plan.feat)], preferred_element_type=F32
    )
    emit_packed(plan, product, out_ref)


def down_kernel(plan, core_ref, hidden_ref, down_ref, out_ref):
    first = pl.multiple_of(core_ref[0] * plan.feat, LANES)
    product = jnp.dot(
        hidden_ref[...], down_ref[:, pl.ds(first, plan.feat)], preferred_element_type=F32
    )
    emit_packed(plan, product, out_ref)


def combine_kernel(plan, member_ref, slot_ref, ids_ref, gates_ref, packed_ref, out_ref):
    found = route(plan, member_ref[0], slot_ref[...], ids_ref[...])
    hots = []
    for slot, place in found:
        main = [main_hot(plan, slot, place)] if plan.full else []
        parts = range(plan.group) if plan.tail else range(1)
        hots.append(
            [
                jnp.concatenate(
                    main + ([tail_hot(plan, slot, place, part)] if plan.tail else []), axis=1
                ).astype(BF16)
                for part in parts
            ]
        )
    for block in range(plan.blocks):
        stack = []
        if plan.full == 1:
            stack.append(packed_ref[:, block].astype(F32).reshape(plan.main_rows, LANES))
        elif plan.full:
            tiles = [
                packed_ref[:, index * plan.blocks + block].astype(F32)[:, None]
                for index in range(plan.full)
            ]
            stack.append(jnp.concatenate(tiles, axis=1).reshape(plan.main_rows, LANES))
        part = 0
        if plan.tail:
            index, part = divmod(block, plan.group)
            tile = packed_ref[:, plan.full * plan.blocks + index]
            stack.append(tile.astype(F32).reshape(plan.tail_wide, LANES))
        table = jnp.concatenate(stack, axis=0).astype(BF16)
        total = jnp.zeros((plan.tok, LANES), F32)
        for k in range(plan.choices):
            picked = jnp.dot(hots[k][part], table, preferred_element_type=F32)
            total = total + gates_ref[:, k : k + 1] * picked
        out_ref[:, lane_block(block)] = total.astype(BF16)


SMEM = pl.BlockSpec(memory_space=pltpu.SMEM)
VMEM = pl.BlockSpec(memory_space=pltpu.VMEM)


def call(kernel, name, in_specs, out_shape, flops, moved, limit, scratch=()):
    single = not isinstance(out_shape, (list, tuple))
    return pl.pallas_call(
        kernel,
        name=name,
        in_specs=in_specs,
        out_specs=VMEM if single else [VMEM] * len(out_shape),
        out_shape=out_shape,
        scratch_shapes=list(scratch),
        cost_estimate=pl.CostEstimate(flops=flops, bytes_accessed=moved, transcendentals=0),
        compiler_params=pltpu.CompilerParams(vmem_limit_bytes=limit),
    )


def body(tokens, expert_ids, gate_values, slot_expert, gate_weight, up_weight, down_weight):
    tok, choices = expert_ids.shape
    feat = tokens.shape[1]
    slots = slot_expert.shape[0]
    plan = Plan(tok, choices, feat, slots)
    gate_local, up_local, down_local = gate_weight[0], up_weight[0], down_weight[0]
    hid = gate_local.shape[1]
    member = lax.axis_index("ep").astype(jnp.int32).reshape(1)
    core = lax.axis_index("rep").astype(jnp.int32).reshape(1)
    slot_row = slot_expert.reshape(1, slots)
    swap = [(0, 1), (1, 0)]
    packed_bytes = 2 * slots * plan.tiles * SUBLANES * LANES
    half_flops = 4 * plan.rows * feat * hid
    rows_scratch = pltpu.VMEM((plan.rows, feat), BF16)

    send = call(
        functools.partial(pack_kernel, plan),
        "pack",
        [SMEM, VMEM, VMEM, VMEM],
        jax.ShapeDtypeStruct(plan.packed, BF16),
        4 * tok * feat * plan.wide,
        2 * packed_bytes,
        16 * MIB,
    )(member, slot_row, expert_ids, tokens)
    arrived = lax.all_to_all(send, "ep", split_axis=0, concat_axis=0, tiled=True)
    partner = lax.ppermute(arrived, "rep", swap)
    acc = call(
        functools.partial(own_kernel, plan),
        "own_half",
        [SMEM, VMEM, VMEM, VMEM],
        jax.ShapeDtypeStruct((plan.rows, 2 * hid), F32),
        half_flops,
        packed_bytes + 8 * plan.rows * hid,
        24 * MIB,
        [rows_scratch],
    )(core, arrived, gate_local, up_local)
    hidden, outbound = call(
        functools.partial(other_kernel, plan),
        "other_half",
        [SMEM, VMEM, VMEM, VMEM, VMEM, VMEM],
        [
            jax.ShapeDtypeStruct((plan.wide, hid), BF16),
            jax.ShapeDtypeStruct(plan.packed, BF16),
        ],
        half_flops + 2 * plan.wide * hid * feat,
        2 * packed_bytes + 8 * plan.rows * hid,
        24 * MIB,
        [rows_scratch],
    )(core, partner, acc, gate_local, up_local, down_local)
    received = lax.ppermute(outbound, "rep", swap)
    mine = call(
        functools.partial(down_kernel, plan),
        "down_own",
        [SMEM, VMEM, VMEM],
        jax.ShapeDtypeStruct(plan.packed, F32),
        2 * plan.wide * hid * feat,
        2 * packed_bytes,
        16 * MIB,
    )(core, hidden, down_local)
    result = (mine + received.astype(F32)).astype(BF16)
    returned = lax.all_to_all(result, "ep", split_axis=0, concat_axis=0, tiled=True)
    return call(
        functools.partial(combine_kernel, plan),
        "combine",
        [SMEM, VMEM, VMEM, VMEM, VMEM],
        jax.ShapeDtypeStruct((tok, feat), BF16),
        2 * tok * feat * plan.wide * choices,
        2 * packed_bytes,
        16 * MIB,
    )(member, slot_row, expert_ids, gate_values, returned)


def solution(mesh):
    assert mesh.shape["rep"] == 2
    return jax.shard_map(
        body,
        mesh=mesh,
        in_specs=(
            P(("groups", "ep"), "rep"),
            P(("groups", "ep"), None),
            P(("groups", "ep"), None),
            P(),
            P("ep", None, "rep"),
            P("ep", None, "rep"),
            P("ep", "rep", None),
        ),
        out_specs=P(("groups", "ep"), "rep"),
        check_vma=False,
    )
```

time: 67.5 us -> 48.9 us (0.72)
  blocking collectives: 4.37 us -> 17.4 us
  starting transfers between devices: 16.5 us -> 3.99 us
  waiting for transfers between devices: 21.5 us -> 11 us
  matrix products: 6.5 us -> 0 us
  local copies, waits for them, and re-layouts: 16.1 us -> 10.8 us
  Pallas kernels: 0 us -> 4.38 us
  other arithmetic: 1.77 us -> 0.77 us
    all_to_all x0 -> x1, blocking collectives: none -> 17.4 us  [body(): lax.all_to_all(send, 'ep', split_axis=0, concat_axis=0, tiled=True)]
    all_to_all x3 -> x1, starting transfers between devices: 16.5 us -> 3.42 us  [body(): lax.all_to_all(result, 'ep', split_axis=0, concat_axis=0, tiled=True)]
    all_to_all x3 -> x1, waiting for transfers between devices: 21.5 us -> 10.2 us  [body(): lax.all_to_all(result, 'ep', split_axis=0, concat_axis=0, tiled=True)]
    dot_general x3 -> x0, matrix products: 6.5 us -> none  [the longest x1 2.94 us: body(): jnp.dot(full_rows, gate_local, preferred_element_type=jnp.float32)]
    all_to_all x1 -> x0, local copies, waits for them, and re-layouts: 5.98 us -> none  [body(): lax.all_to_all(down_local, 'rep', split_axis=1, concat_axis=0, tiled=True)]
    unnamed x11 -> x20, local copies, waits for them, and re-layouts: 5.97 us -> 10.8 us
    pallas_call x0 -> x5, Pallas kernels: none -> 4.38 us  [the longest x1 1.32 us: body(): call(functools.partial(other_kernel, plan), 'other_half', [SMEM, VMEM, VM...]
    all_gather x2 -> x0, blocking collectives: 4.37 us -> none  [the longest x1 2.45 us: body(): lax.all_gather(arrived_rows, 'rep', axis=2, tiled=True)]
  transfers between devices with their start and end apart: 3 -> 3, of which waited for: 3 -> 2; matrix products, arithmetic and copies ran while one was open for 14% -> 0% of each run, Pallas kernels for 0% -> 3%
where the time goes in v1:
time: 48.9 us; the launch traced here: 48.5 us
  blocking collectives  17.4 us (36%)
  waiting for transfers between devices  11 us (22%)
  local copies, waits for them, and re-layouts  10.8 us (22%)
  Pallas kernels  4.38 us (9%)
  starting transfers between devices  3.99 us (8%)
  other arithmetic  0.77 us (2%)
    all_to_all x1, blocking collectives, body(): lax.all_to_all(send, 'ep', split_axis=0, concat_axis=0, tiled=True)  17.4 us
    unnamed x20, local copies, waits for them, and re-layouts  10.8 us
    all_to_all x1, waiting for transfers between devices, body(): lax.all_to_all(result, 'ep', split_axis=0, concat_axis=0, tiled=True)  10.2 us
    all_to_all x1, starting transfers between devices, body(): lax.all_to_all(result, 'ep', split_axis=0, concat_axis=0, tiled=True)  3.42 us
    pallas_call x1, Pallas kernels, body(): call(functools.partial(other_kernel, plan), 'other_half', [SMEM, VMEM, VM...  1.32 us
    pallas_call x1, Pallas kernels, body(): call(functools.partial(combine_kernel, plan), 'combine', [SMEM, VMEM, VME...  1.25 us
  transfers between devices with their start and end apart: 3, of which 2 were waited for; matrix products, arithmetic and copies ran while one was open for 0% of the time, Pallas kernels for 3%

profile of v1, /device:TPU:0, one launch (start us, length us, event | category | flops | bytes accessed | tf_op | source)
XLA Modules:
  0.0 48.5 jit_solution(5536613108698547242)
XLA Ops:
  0.0 0.7 %copy.9.ids_ref = s32[32,1]{1,0:T(8,128)S(1)} copy(s32[32,1]{0,1:T(1,128)} %param.8) | data formatting | bytes 256 | tf_op args[1]
  0.7 0.0 copy-start.5
  0.7 0.9 %copy-done.5 = bf16[32,1792]{1,0:T(8,128)(2,1)S(1)} copy-done((bf16[32,1792]{1,0:T(8,128)(2,1)S(1)}, bf16[32,1792]{1,0:T(8,128)(2,1)}, u32[]{:S(2)}) %copy-start.5) | copy-done | bytes 114712
  1.6 0.0 copy-start.6
  1.6 0.7 %copy-done.6 = s32[8]{0:T(128)S(1)} copy-done((s32[8]{0:T(128)S(1)}, s32[8]{0:T(128)}, u32[]{:S(2)}) %copy-start.6) | copy-done | bytes 56
  2.3 0.6 %pack.1 = bf16[8,18,8,128]{3,2,1,0:T(8,128)(2,1)S(1)} custom-call(s32[1]{0:T(128)} %bitcast.member_ref, s32[1,8]{1,0:T(1,128)S(1)} %bitcast.12, s32[32,1]{1,0:T(8,128)S(1)} %copy.9.ids_ref, bf16[32,1792]{1,0:T(8,128)(2,1)S(1)} %copy-done.5), custom_call_target="tpu_custom_call" | custom-call | flops 29360128 | bytes 589824 | tf_op jit(solution)/shard_map/pack/pallas_call | solution.py:297
  2.9 17.4 %all_to_all.10.packed_ref = bf16[8,18,8,128]{3,2,1,0:T(8,128)(2,1)S(1)} all-to-all(bf16[8,18,8,128]{3,2,1,0:T(8,128)(2,1)S(1)} %pack.1), channel_id=1, replica_groups=mesh['groups'=2,'ep'=8,'rep'=2] {'ep'}, dimensions={0} | all-to-all | bytes 589824 | tf_op jit(solution)/shard_map/all_to_all | solution.py:306
  20.3 0.0 collective-permute-start
  20.3 0.0 copy-start
  20.3 2.0 %copy-done = bf16[1,3584,512]{2,1,0:T(8,128)(2,1)S(1)} copy-done((bf16[1,3584,512]{2,1,0:T(8,128)(2,1)S(1)}, bf16[1,3584,512]{2,1,0:T(8,128)(2,1)}, u32[]{:S(2)}) %copy-start) | copy-done | bytes 3670040
  22.4 0.0 copy-start.2
  22.4 2.0 %copy-done.2 = bf16[1,3584,512]{2,1,0:T(8,128)(2,1)S(1)} copy-done((bf16[1,3584,512]{2,1,0:T(8,128)(2,1)S(1)}, bf16[1,3584,512]{2,1,0:T(8,128)(2,1)}, u32[]{:S(2)}) %copy-start.2) | copy-done | bytes 3670040
  24.4 0.0 copy-start.1
  24.4 0.0 copy-start.3
  24.4 0.8 %own_half.1.acc_ref = f32[80,1024]{1,0:T(8,128)S(1)} custom-call(s32[1]{0:T(128)} %bitcast.2.core_ref, bf16[8,18,8,128]{3,2,1,0:T(8,128)(2,1)S(1)} %all_to_all.10.packed_ref, bf16[3584,512]{1,0:T(8,128)(2,1)S(1)} %bitcast.6, bf16[3584,512]{1,0:T(8,128)(2,1)S(1)} %bitcast.8), custom_call_target="tpu_custom_call" | custom-call | flops 293601280 | bytes 622592 | tf_op jit(solution)/shard_map/own_half/pallas_call | solution.py:308
  25.2 0.0 collective-permute-done.packed_ref
  25.2 1.2 %copy-done.1 = bf16[1,3584,512]{2,1,0:T(8,128)(2,1)S(1)} copy-done((bf16[1,3584,512]{2,1,0:T(8,128)(2,1)S(1)}, bf16[1,3584,512]{2,1,0:T(8,128)(2,1)}, u32[]{:S(2)}) %copy-start.1) | copy-done | bytes 3670040
  26.4 1.1 %copy-done.3 = bf16[1,3584,512]{2,1,0:T(8,128)(2,1)S(1)} copy-done((bf16[1,3584,512]{2,1,0:T(8,128)(2,1)S(1)}, bf16[1,3584,512]{2,1,0:T(8,128)(2,1)}, u32[]{:S(2)}) %copy-start.3) | copy-done | bytes 3670040
  27.6 0.0 copy-start.4
  27.6 2.0 %copy-done.4 = bf16[1,512,3584]{2,1,0:T(8,128)(2,1)S(1)} copy-done((bf16[1,512,3584]{2,1,0:T(8,128)(2,1)S(1)}, bf16[1,512,3584]{2,1,0:T(8,128)(2,1)}, u32[]{:S(2)}) %copy-start.4) | copy-done | bytes 3670040
  29.6 1.3 %other_half.1 = (bf16[128,512]{1,0:T(8,128)(2,1)S(1)}, bf16[8,18,8,128]{3,2,1,0:T(8,128)(2,1)S(1)}) custom-call(s32[1]{0:T(128)} %bitcast.2.core_ref, bf16[8,18,8,128]{3,2,1,0:T(8,128)(2,1)S(1)} %collective-permute-done.packed_ref, f32[80,1024]{1,0:T(8,128)S(1)} %own_half.1.acc_ref, bf16[3584,512]{1,0:T(8,128)(2,1)S(1)} %bitcast.7, ...), custom_call_target="tpu_custom_call" | custom-call | flops 528482304 | bytes 917504 | tf_op jit(solution)/shard_map/other_half/pallas_call | solution.py:318
  30.9 0.0 copy-start.8
  30.9 0.0 copy-start.7
  30.9 0.6 %collective-permute-start.1 = (bf16[8,18,8,128]{3,2,1,0:T(8,128)(2,1)S(1)}, bf16[8,18,8,128]{3,2,1,0:T(8,128)(2,1)S(1)}, u32[]{:S(2)}, u32[]{:S(2)}) collective-permute-start(bf16[8,18,8,128]{3,2,1,0:T(8,128)(2,1)S(1)} %get-tuple-element.8), channel_id=1, source_target_pairs={{0,1},{1,0},{2,3},{3,2},{4,5},{5,4},{6,7},{7,6},{8,9},{9,8},{10,11... | collective-permute-start | bytes 884744 | tf_op jit(solution)/shard_map/ppermute | solution.py:331
  31.5 0.4 down_own.1
  31.9 0.8 %collective-permute-done.1 = bf16[8,18,8,128]{3,2,1,0:T(8,128)(2,1)S(1)} collective-permute-done((bf16[8,18,8,128]{3,2,1,0:T(8,128)(2,1)S(1)}, bf16[8,18,8,128]{3,2,1,0:T(8,128)(2,1)S(1)}, u32[]{:S(2)}, u32[]{:S(2)}) %collective-permute-start.1) | collective-permute-done | bytes 294944 | tf_op jit(solution)/shard_map/ppermute | solution.py:331
  32.7 0.8 %add_convert_fusion = bf16[8,18,8,128]{3,2,1,0:T(8,128)(2,1)} fusion(f32[8,18,8,128]{3,2,1,0:T(8,128)S(1)} %down_own.1, bf16[8,18,8,128]{3,2,1,0:T(8,128)(2,1)S(1)} %collective-permute-done.1), kind=kLoop, calls=%fused_computation | loop fusion | flops 442368 | bytes 1179648 | tf_op jit(solution)/shard_map/convert_element_type | solution.py:341
  33.5 3.4 %all-to-all-start.1 = ((bf16[8,18,8,128]{3,2,1,0:T(8,128)(2,1)}), bf16[8,18,8,128]{3,2,1,0:T(8,128)(2,1)S(1)}, u32[]{:S(2)}, u32[]{:S(2)}) async-start(bf16[8,18,8,128]{3,2,1,0:T(8,128)(2,1)} %add_convert_fusion), calls=%async_computation.1 | async-start | bytes 589824 | tf_op jit(solution)/shard_map/all_to_all | solution.py:342
  36.9 0.0 copy-done.8
  36.9 0.1 copy.10.gates_ref
  37.0 10.2 %all-to-all-done.1.packed_ref = bf16[8,18,8,128]{3,2,1,0:T(8,128)(2,1)S(1)} async-done(((bf16[8,18,8,128]{3,2,1,0:T(8,128)(2,1)}), bf16[8,18,8,128]{3,2,1,0:T(8,128)(2,1)S(1)}, u32[]{:S(2)}, u32[]{:S(2)}) %all-to-all-start.1) | async-done | bytes 294944 | tf_op jit(solution)/shard_map/all_to_all | solution.py:342
  47.2 0.0 copy-done.7
  47.2 1.2 %combine.1 = bf16[32,1792]{1,0:T(8,128)(2,1)} custom-call(s32[1]{0:T(128)} %bitcast.member_ref, s32[1,8]{1,0:T(1,128)S(1)} %bitcast.13, s32[32,1]{1,0:T(8,128)S(1)} %copy.9.ids_ref, f32[32,1]{1,0:T(8,128)S(1)} %copy.10.gates_ref, bf16[8,18,8,128]{3,2,1,0:T(8,128)(2,1)S(1)} %all-to-all-done.1.packed_ref), custom_call_target="tpu_custom_call" | custom-call | flops 14680064 | bytes 589824 | tf_op jit(solution)/shard_map/combine/pallas_call | solution.py:343
Async XLA Ops:
  0.7 0.9 %copy-start.5 = (bf16[32,1792]{1,0:T(8,128)(2,1)S(1)}, bf16[32,1792]{1,0:T(8,128)(2,1)}, u32[]{:S(2)}) copy-start(bf16[32,1792]{1,0:T(8,128)(2,1)} %tokens_ref.1) | copy-start | bytes 344068
  1.6 0.7 %copy-start.6 = (s32[8]{0:T(128)S(1)}, s32[8]{0:T(128)}, u32[]{:S(2)}) copy-start(s32[8]{0:T(128)} %param.10) | copy-start | bytes 100
  20.3 4.9 %collective-permute-start = (bf16[8,18,8,128]{3,2,1,0:T(8,128)(2,1)S(1)}, bf16[8,18,8,128]{3,2,1,0:T(8,128)(2,1)S(1)}, u32[]{:S(2)}, u32[]{:S(2)}) collective-permute-start(bf16[8,18,8,128]{3,2,1,0:T(8,128)(2,1)S(1)} %all_to_all.10.packed_ref), channel_id=1, source_target_pairs={{0,1},{1,0},{2,3},{3,2},{4,5},{5,4},{6,7},{7,6},{8,9},{9,8},{10,11... | collective-permute-start | bytes 884744 | tf_op jit(solution)/shard_map/ppermute | solution.py:307
  20.3 2.0 %copy-start = (bf16[1,3584,512]{2,1,0:T(8,128)(2,1)S(1)}, bf16[1,3584,512]{2,1,0:T(8,128)(2,1)}, u32[]{:S(2)}) copy-start(bf16[1,3584,512]{2,1,0:T(8,128)(2,1)} %param.11) | copy-start | bytes 11010052
  22.4 2.0 %copy-start.2 = (bf16[1,3584,512]{2,1,0:T(8,128)(2,1)S(1)}, bf16[1,3584,512]{2,1,0:T(8,128)(2,1)}, u32[]{:S(2)}) copy-start(bf16[1,3584,512]{2,1,0:T(8,128)(2,1)} %param.12) | copy-start | bytes 11010052
  24.4 2.0 %copy-start.1 = (bf16[1,3584,512]{2,1,0:T(8,128)(2,1)S(1)}, bf16[1,3584,512]{2,1,0:T(8,128)(2,1)}, u32[]{:S(2)}) copy-start(bf16[1,3584,512]{2,1,0:T(8,128)(2,1)} %param.11) | copy-start | bytes 11010052
  24.4 3.2 %copy-start.3 = (bf16[1,3584,512]{2,1,0:T(8,128)(2,1)S(1)}, bf16[1,3584,512]{2,1,0:T(8,128)(2,1)}, u32[]{:S(2)}) copy-start(bf16[1,3584,512]{2,1,0:T(8,128)(2,1)} %param.12) | copy-start | bytes 11010052
  27.6 2.0 %copy-start.4 = (bf16[1,512,3584]{2,1,0:T(8,128)(2,1)S(1)}, bf16[1,512,3584]{2,1,0:T(8,128)(2,1)}, u32[]{:S(2)}) copy-start(bf16[1,512,3584]{2,1,0:T(8,128)(2,1)} %param.13) | copy-start | bytes 11010052
  30.9 6.0 %copy-start.8 = (f32[32,1]{0,1:T(1,128)S(1)}, f32[32,1]{0,1:T(1,128)}, u32[]{:S(2)}) copy-start(f32[32,1]{0,1:T(1,128)} %param.9) | copy-start | bytes 388
  30.9 16.3 %copy-start.7 = (s32[8]{0:T(128)S(1)}, s32[8]{0:T(128)}, u32[]{:S(2)}) copy-start(s32[8]{0:T(128)} %param.10) | copy-start | bytes 100
  30.9 1.8 %collective-permute-start.1 = (bf16[8,18,8,128]{3,2,1,0:T(8,128)(2,1)S(1)}, bf16[8,18,8,128]{3,2,1,0:T(8,128)(2,1)S(1)}, u32[]{:S(2)}, u32[]{:S(2)}) collective-permute-start(bf16[8,18,8,128]{3,2,1,0:T(8,128)(2,1)S(1)} %get-tuple-element.8), channel_id=1, source_target_pairs={{0,1},{1,0},{2,3},{3,2},{4,5},{5,4},{6,7},{7,6},{8,9},{9,8},{10,11... | collective-permute-start | bytes 884744 | tf_op jit(solution)/shard_map/ppermute | solution.py:331
  33.5 13.7 %all-to-all-start.1 = ((bf16[8,18,8,128]{3,2,1,0:T(8,128)(2,1)}), bf16[8,18,8,128]{3,2,1,0:T(8,128)(2,1)S(1)}, u32[]{:S(2)}, u32[]{:S(2)}) async-start(bf16[8,18,8,128]{3,2,1,0:T(8,128)(2,1)} %add_convert_fusion), calls=%async_computation.1 | async-start | bytes 589824 | tf_op jit(solution)/shard_map/all_to_all | solution.py:342

commit v2 on v1

--- a/solution.py
+++ b/solution.py
@@ -7,12 +7,14 @@
 from jax.experimental.pallas import tpu as pltpu
 from jax.sharding import PartitionSpec as P
 
+
 LANES = 128
 SUBLANES = 8
 MIB = 1 << 20
 F32 = jnp.float32
 BF16 = jnp.bfloat16
-TRANS_LHS = (((0,), (0,)), ((), ()))
+COVER_FLOPS = 1 << 34
+COVER_BYTES = 1 << 25
 
 
 class Plan:
@@ -33,6 +35,7 @@
         self.rows = self.main_rows + self.tail_rows
         self.tail_wide = slots * SUBLANES if self.tail else 0
         self.wide = self.main_rows + self.tail_wide
+        self.parts = max(1, self.group)
         self.packed = (slots, self.tiles, SUBLANES, LANES)
 
 
@@ -42,65 +45,83 @@
 
 def floor_div(values, divisor):
     return jnp.floor((values.astype(F32) + 0.5) * (1.0 / divisor)).astype(jnp.int32)
+
+
+def to_column(row):
+    size = row.shape[1]
+    diagonal = iota((size, size), 0) == iota((size, size), 1)
+    return jnp.sum(jnp.where(diagonal, jnp.broadcast_to(row, (size, size)), 0), axis=1, keepdims=True)
 
 
 def route(plan, member, slot_row, ids):
     slots, tok = plan.slots, plan.tok
     square = (slots, slots)
-    down, across = iota(square, 0), iota(square, 1)
-    row = jnp.broadcast_to(slot_row.astype(F32), square)
-    col = jnp.sum(jnp.where(down == across, row, 0.0), axis=1, keepdims=True)
+    row = slot_row.astype(F32)
+    col = to_column(row)
     same = jnp.where(col == row, 1.0, 0.0)
-    copies = jnp.sum(same, axis=0, keepdims=True)
-    rank = jnp.sum(jnp.where(down < across, same, 0.0), axis=0, keepdims=True)
-    want = jnp.zeros((1, slots), F32)
+    copies = jnp.sum(same, axis=1, keepdims=True)
+    rank = jnp.sum(jnp.where(iota(square, 1) < iota(square, 0), same, 0.0), axis=1, keepdims=True)
+    want = jnp.zeros((slots, 1), F32)
     for number in (2, 3, 4):
         want = jnp.where(copies == number, lax.rem(member, number).astype(F32), want)
     chosen = rank == want
     hits = [
-        jnp.where((ids[:, k : k + 1] == slot_row) & chosen, 1.0, 0.0) for k in range(plan.choices)
+        jnp.where((ids[k : k + 1].astype(F32) == col) & chosen, 1.0, 0.0)
+        for k in range(plan.choices)
     ]
-    before = jnp.where(iota((tok, tok), 1) < iota((tok, tok), 0), 1.0, 0.0).astype(BF16)
-    counts = jnp.dot(before, sum(hits).astype(BF16), preferred_element_type=F32)
-    lane = iota((tok, slots), 1).astype(F32)
+    before = jnp.where(iota((tok, tok), 0) < iota((tok, tok), 1), 1.0, 0.0).astype(BF16)
+    counts = jnp.dot(sum(hits).astype(BF16), before, preferred_element_type=F32)
+    line = iota((slots, tok), 0).astype(F32)
     found = []
     for hit in hits:
-        slot = jnp.sum(hit * lane, axis=1, keepdims=True).astype(jnp.int32)
-        place = jnp.sum(hit * counts, axis=1, keepdims=True).astype(jnp.int32)
+        slot = jnp.sum(hit * line, axis=0, keepdims=True).astype(jnp.int32)
+        place = jnp.sum(hit * counts, axis=0, keepdims=True).astype(jnp.int32)
         found.append((slot, place))
     return found
 
 
-def main_hot(plan, slot, place):
-    code = jnp.where(place < plan.main, slot * plan.main + place, -1)
-    return jnp.where(code == iota((plan.tok, plan.main_rows), 1), 1.0, 0.0)
-
-
-def tail_hot(plan, slot, place, part):
-    code = jnp.where(
-        place < plan.main, -1, slot * SUBLANES + place - plan.main + part * plan.tail
-    )
-    return jnp.where(code == iota((plan.tok, plan.tail_wide), 1), 1.0, 0.0)
+def main_code(plan, slot, place):
+    return jnp.where(place < plan.main, slot * plan.main + place, -1)
+
+
+def tail_code(plan, slot, place, part):
+    spot = slot * SUBLANES + place - plan.main + part * plan.tail
+    return jnp.where(place < plan.main, -1, spot)
 
 
 def lane_block(index):
     return slice(index * LANES, (index + 1) * LANES)
 
 
-def pack_kernel(plan, member_ref, slot_ref, ids_ref, tokens_ref, send_ref):
-    found = route(plan, member_ref[0], slot_ref[...], ids_ref[...])
+def warm_kernel(out_ref):
+    out_ref[...] = jnp.zeros_like(out_ref)
+
+
+def read_found(plan, found_ref):
+    lines = [found_ref[index : index + 1] for index in range(2 * plan.choices)]
+    return list(zip(lines[: plan.choices], lines[plan.choices :], strict=True))
+
+
+def pack_kernel(plan, warm_ref, slot_ref, ids_ref, tokens_ref, send_ref, found_ref):
+    found = route(plan, lax.axis_index("ep"), slot_ref[...], ids_ref[...])
+    for k, (slot, place) in enumerate(found):
+        found_ref[k : k + 1] = slot
+        found_ref[plan.choices + k : plan.choices + k + 1] = place
     if plan.full:
-        hot = sum(main_hot(plan, *pair) for pair in found).astype(BF16)
-        main = lax.dot_general(hot, tokens_ref[...], TRANS_LHS, preferred_element_type=F32)
+        line = iota((plan.main_rows, plan.tok), 0)
+        hot = sum(jnp.where(line == main_code(plan, *pair), 1.0, 0.0) for pair in found)
+        main = jnp.dot(hot.astype(BF16), tokens_ref[...], preferred_element_type=F32)
         for block in range(plan.blocks):
             tile = main[:, lane_block(block)].reshape(plan.slots, plan.full, SUBLANES, LANES)
             for index in range(plan.full):
                 send_ref[:, index * plan.blocks + block] = tile[:, index].astype(BF16)
     if plan.tail:
-        hot = jnp.concatenate(
-            [sum(tail_hot(plan, *pair, part) for pair in found) for part in range(plan.group)],
-            axis=0,
-        ).astype(BF16)
+        line = iota((plan.tail_wide, plan.tok * plan.group), 0)
+        hot = jnp.zeros(line.shape, F32)
+        for pair in found:
+            codes = [tail_code(plan, *pair, part) for part in range(plan.group)]
+            hot += jnp.where(line == jnp.concatenate(codes, axis=1), 1.0, 0.0)
+        hot = hot.astype(BF16)
         for index in range(plan.tail_tiles):
             stack = []
             for part in range(plan.group):
@@ -109,12 +130,21 @@
                     stack.append(tokens_ref[:, lane_block(block)])
                 else:
                     stack.append(jnp.zeros((plan.tok, LANES), BF16))
-            tile = lax.dot_general(
-                hot, jnp.concatenate(stack, axis=0), TRANS_LHS, preferred_element_type=F32
-            )
+            tile = jnp.dot(hot, jnp.concatenate(stack, axis=0), preferred_element_type=F32)
             send_ref[:, plan.full * plan.blocks + index] = tile.reshape(
                 plan.slots, SUBLANES, LANES
             ).astype(BF16)
+
+
+def select_kernel(plan, found_ref, gates_ref, pick_ref, column_ref):
+    lane = iota((plan.tok, plan.wide), 1).astype(F32)
+    for k, (slot, place) in enumerate(read_found(plan, found_ref)):
+        column_ref[:, k : k + 1] = to_column(gates_ref[k : k + 1])
+        for part in range(plan.parts):
+            tail = plan.main_rows + tail_code(plan, slot, place, part)
+            code = jnp.where(place < plan.main, main_code(plan, slot, place), tail)
+            pick = jnp.where(to_column(code.astype(F32)) == lane, 1.0, 0.0)
+            pick_ref[k * plan.parts + part] = pick.astype(BF16)
 
 
 def flat_tile(tile):
@@ -150,9 +180,9 @@
                     ]
 
 
-def own_kernel(plan, core_ref, packed_ref, gate_ref, up_ref, acc_ref, rows_ref):
+def own_kernel(plan, packed_ref, gate_ref, up_ref, down_ref, acc_ref, rows_ref):
     unpack_rows(plan, packed_ref, rows_ref)
-    first = pl.multiple_of(core_ref[0] * plan.feat, LANES)
+    first = pl.multiple_of(lax.axis_index("rep") * plan.feat, LANES)
     hid = gate_ref.shape[1]
     rows = rows_ref[...]
     acc_ref[:, :hid] = jnp.dot(
@@ -185,10 +215,10 @@
 
 
 def other_kernel(
-    plan, core_ref, packed_ref, acc_ref, gate_ref, up_ref, down_ref, hidden_ref, out_ref, rows_ref
+    plan, packed_ref, acc_ref, gate_ref, up_ref, down_ref, hidden_ref, out_ref, rows_ref
 ):
     unpack_rows(plan, packed_ref, rows_ref)
-    first = pl.multiple_of((1 - core_ref[0]) * plan.feat, LANES)
+    first = pl.multiple_of((1 - lax.axis_index("rep")) * plan.feat, LANES)
     hid = gate_ref.shape[1]
     rows = rows_ref[...]
     gate = acc_ref[:, :hid] + jnp.dot(
@@ -216,28 +246,19 @@
     emit_packed(plan, product, out_ref)
 
 
-def down_kernel(plan, core_ref, hidden_ref, down_ref, out_ref):
-    first = pl.multiple_of(core_ref[0] * plan.feat, LANES)
+def down_kernel(plan, hidden_ref, down_ref, out_ref):
+    first = pl.multiple_of(lax.axis_index("rep") * plan.feat, LANES)
     product = jnp.dot(
         hidden_ref[...], down_ref[:, pl.ds(first, plan.feat)], preferred_element_type=F32
     )
     emit_packed(plan, product, out_ref)
 
 
-def combine_kernel(plan, member_ref, slot_ref, ids_ref, gates_ref, packed_ref, out_ref):
-    found = route(plan, member_ref[0], slot_ref[...], ids_ref[...])
-    hots = []
-    for slot, place in found:
-        main = [main_hot(plan, slot, place)] if plan.full else []
-        parts = range(plan.group) if plan.tail else range(1)
-        hots.append(
-            [
-                jnp.concatenate(
-                    main + ([tail_hot(plan, slot, place, part)] if plan.tail else []), axis=1
-                ).astype(BF16)
-                for part in parts
-            ]
-        )
+def sum_kernel(mine_ref, other_ref, out_ref):
+    out_ref[...] = (mine_ref[...] + other_ref[...].astype(F32)).astype(BF16)
+
+
+def combine_kernel(plan, pick_ref, column_ref, packed_ref, out_ref):
     for block in range(plan.blocks):
         stack = []
         if plan.full == 1:
@@ -256,20 +277,21 @@
         table = jnp.concatenate(stack, axis=0).astype(BF16)
         total = jnp.zeros((plan.tok, LANES), F32)
         for k in range(plan.choices):
-            picked = jnp.dot(hots[k][part], table, preferred_element_type=F32)
-            total = total + gates_ref[:, k : k + 1] * picked
+            picked = jnp.dot(
+                pick_ref[k * plan.parts + part], table, preferred_element_type=F32
+            )
+            total = total + column_ref[:, k : k + 1] * picked
         out_ref[:, lane_block(block)] = total.astype(BF16)
 
 
-SMEM = pl.BlockSpec(memory_space=pltpu.SMEM)
 VMEM = pl.BlockSpec(memory_space=pltpu.VMEM)
-
-
-def call(kernel, name, in_specs, out_shape, flops, moved, limit, scratch=()):
+ANY = pl.BlockSpec(memory_space=pltpu.HBM)
+
+
+def call(kernel, in_specs, out_shape, flops, moved, limit, scratch=()):
     single = not isinstance(out_shape, (list, tuple))
     return pl.pallas_call(
         kernel,
-        name=name,
         in_specs=in_specs,
         out_specs=VMEM if single else [VMEM] * len(out_shape),
         out_shape=out_shape,
@@ -284,71 +306,85 @@
     feat = tokens.shape[1]
     slots = slot_expert.shape[0]
     plan = Plan(tok, choices, feat, slots)
-    gate_local, up_local, down_local = gate_weight[0], up_weight[0], down_weight[0]
-    hid = gate_local.shape[1]
-    member = lax.axis_index("ep").astype(jnp.int32).reshape(1)
-    core = lax.axis_index("rep").astype(jnp.int32).reshape(1)
-    slot_row = slot_expert.reshape(1, slots)
+    weights = [gate_weight[0], up_weight[0], down_weight[0]]
+    hid = weights[0].shape[1]
+    gate_local, up_local, down_local = weights
     swap = [(0, 1), (1, 0)]
     packed_bytes = 2 * slots * plan.tiles * SUBLANES * LANES
     half_flops = 4 * plan.rows * feat * hid
     rows_scratch = pltpu.VMEM((plan.rows, feat), BF16)
-
-    send = call(
+    packed = jax.ShapeDtypeStruct(plan.packed, BF16)
+
+    slot_row, ids, gates = slot_expert.reshape(1, slots), expert_ids.T, gate_values.T
+
+    warm = call(
+        warm_kernel,
+        [],
+        jax.ShapeDtypeStruct((SUBLANES, LANES), F32),
+        COVER_FLOPS,
+        COVER_BYTES,
+        1 * MIB,
+    )()
+    send, found = call(
         functools.partial(pack_kernel, plan),
-        "pack",
-        [SMEM, VMEM, VMEM, VMEM],
-        jax.ShapeDtypeStruct(plan.packed, BF16),
-        4 * tok * feat * plan.wide,
-        2 * packed_bytes,
-        16 * MIB,
-    )(member, slot_row, expert_ids, tokens)
+        [VMEM] * 4,
+        [packed, jax.ShapeDtypeStruct((2 * choices, tok), jnp.int32)],
+        COVER_FLOPS,
+        COVER_BYTES,
+        8 * MIB,
+    )(warm, slot_row, ids, tokens)
     arrived = lax.all_to_all(send, "ep", split_axis=0, concat_axis=0, tiled=True)
     partner = lax.ppermute(arrived, "rep", swap)
     acc = call(
         functools.partial(own_kernel, plan),
-        "own_half",
-        [SMEM, VMEM, VMEM, VMEM],
+        [VMEM] * 4,
         jax.ShapeDtypeStruct((plan.rows, 2 * hid), F32),
-        half_flops,
-        packed_bytes + 8 * plan.rows * hid,
-        24 * MIB,
+        1 << 10,
+        1 << 10,
+        8 * MIB,
         [rows_scratch],
-    )(core, arrived, gate_local, up_local)
+    )(arrived, gate_local, up_local, down_local)
+    picks, columns = call(
+        functools.partial(select_kernel, plan),
+        [VMEM, VMEM],
+        [
+            jax.ShapeDtypeStruct((choices * plan.parts, tok, plan.wide), BF16),
+            jax.ShapeDtypeStruct((tok, choices), F32),
+        ],
+        1 << 10,
+        1 << 10,
+        4 * MIB,
+    )(found, gates)
     hidden, outbound = call(
         functools.partial(other_kernel, plan),
-        "other_half",
-        [SMEM, VMEM, VMEM, VMEM, VMEM, VMEM],
-        [
-            jax.ShapeDtypeStruct((plan.wide, hid), BF16),
-            jax.ShapeDtypeStruct(plan.packed, BF16),
-        ],
+        [VMEM, VMEM, VMEM, VMEM, VMEM],
+        [jax.ShapeDtypeStruct((plan.wide, hid), BF16), packed],
         half_flops + 2 * plan.wide * hid * feat,
         2 * packed_bytes + 8 * plan.rows * hid,
-        24 * MIB,
+        8 * MIB,
         [rows_scratch],
-    )(core, partner, acc, gate_local, up_local, down_local)
+    )(partner, acc, gate_local, up_local, down_local)
     received = lax.ppermute(outbound, "rep", swap)
     mine = call(
         functools.partial(down_kernel, plan),
-        "down_own",
-        [SMEM, VMEM, VMEM],
+        [VMEM, VMEM],
         jax.ShapeDtypeStruct(plan.packed, F32),
         2 * plan.wide * hid * feat,
         2 * packed_bytes,
-        16 * MIB,
-    )(core, hidden, down_local)
-    result = (mine + received.astype(F32)).astype(BF16)
+        8 * MIB,
+    )(hidden, down_local)
+    result = call(
+        sum_kernel, [VMEM, VMEM], packed, packed_bytes, 4 * packed_bytes, 4 * MIB
+    )(mine, received)
     returned = lax.all_to_all(result, "ep", split_axis=0, concat_axis=0, tiled=True)
     return call(
         functools.partial(combine_kernel, plan),
-        "combine",
-        [SMEM, VMEM, VMEM, VMEM, VMEM],
+        [VMEM, VMEM, VMEM],
         jax.ShapeDtypeStruct((tok, feat), BF16),
         2 * tok * feat * plan.wide * choices,
         2 * packed_bytes,
-        16 * MIB,
-    )(member, slot_row, expert_ids, gate_values, returned)
+        8 * MIB,
+    )(picks, columns, returned)
 
 
 def solution(mesh):

time: 48.9 us -> 39.1 us (0.80)
  local copies, waits for them, and re-layouts: 10.8 us -> 0.94 us
  other arithmetic: 0.77 us -> 0 us
  waiting for transfers between devices: 11 us -> 11.7 us
    unnamed x20 -> x14, local copies, waits for them, and re-layouts: 10.8 us -> 0.94 us
    convert_element_type x1 -> x0, other arithmetic: 0.77 us -> none  [body(): result = (mine + received.astype(F32)).astype(BF16)]
    ppermute x1, waiting for transfers between devices: 0.01 us -> 0.73 us  [body(): partner = lax.ppermute(arrived, 'rep', swap)]
    pallas_call x5 -> x8, Pallas kernels: 4.38 us -> 4.81 us  [the longest x1 1.32 us: body(): call(functools.partial(other_kernel, plan), [VMEM, VMEM, VMEM, VMEM, VMEM...]
  transfers between devices with their start and end apart: 3 -> 3, of which waited for: 2 -> 3; matrix products, arithmetic and copies ran while one was open for 0% -> 0% of each run, Pallas kernels for 3% -> 3%
where the time goes in v2:
time: 39.1 us; the launch traced here: 38.9 us
  blocking collectives  17.7 us (45%)
  waiting for transfers between devices  11.7 us (30%)
  Pallas kernels  4.81 us (12%)
  starting transfers between devices  3.62 us (9%)
  local copies, waits for them, and re-layouts  0.94 us (2%)
    all_to_all x1, blocking collectives, body(): lax.all_to_all(send, 'ep', split_axis=0, concat_axis=0, tiled=True)  17.7 us
    all_to_all x1, waiting for transfers between devices, body(): lax.all_to_all(result, 'ep', split_axis=0, concat_axis=0, tiled=True)  9.95 us
    all_to_all x1, starting transfers between devices, body(): lax.all_to_all(result, 'ep', split_axis=0, concat_axis=0, tiled=True)  3.42 us
    pallas_call x1, Pallas kernels, body(): call(functools.partial(other_kernel, plan), [VMEM, VMEM, VMEM, VMEM, VMEM...  1.32 us
    ppermute x1, waiting for transfers between devices, body(): received = lax.ppermute(outbound, 'rep', swap)  1.03 us
    unnamed x14, local copies, waits for them, and re-layouts  0.94 us
    pallas_call x1, Pallas kernels, body(): call(functools.partial(combine_kernel, plan), [VMEM, VMEM, VMEM], jax.Sha...  0.88 us
    pallas_call x1, Pallas kernels, body(): call(functools.partial(own_kernel, plan), [VMEM] * 4, jax.ShapeDtypeStruc...  0.83 us
  transfers between devices with their start and end apart: 3, of which 3 were waited for; matrix products, arithmetic and copies ran while one was open for 0% of the time, Pallas kernels for 3%

profile of v2, /device:TPU:0, one launch (start us, length us, event | category | flops | bytes accessed | tf_op | source)
XLA Modules:
  0.0 38.9 jit_solution(4786456270021922982)
XLA Ops:
  0.0 0.0 copy-start.4
  0.0 0.0 copy-start.5
  0.0 0.0 copy-start.3
  0.0 0.6 %copy-done.4 = s32[8]{0:T(128)S(1)} copy-done((s32[8]{0:T(128)S(1)}, s32[8]{0:T(128)}, u32[]{:S(2)}) %copy-start.4) | copy-done | bytes 56
  0.7 0.0 copy-done.5
  0.7 0.3 copy-done.3
  0.9 0.0 copy-start
  0.9 0.0 copy-start.1
  0.9 0.0 copy-start.2
  0.9 0.5 %shard_map.74 = (bf16[8,18,8,128]{3,2,1,0:T(8,128)(2,1)S(1)}, s32[2,32]{1,0:T(2,128)S(1)}) custom-call(f32[8,128]{1,0:T(8,128)S(1)} %shard_map.73.warm_ref, s32[1,8]{1,0:T(1,128)S(1)} %bitcast.13, s32[1,32]{1,0:T(1,128)S(1)} %bitcast.14, bf16[32,1792]{1,0:T(8,128)(2,1)S(1)} %copy-done.3), custom_call_target="tpu_custom_call" | custom-call | flops 17179869184 | bytes 33554432 | tf_op jit(solution)/shard_map/pallas_call | solution.py:328
  1.5 17.7 %all_to_all.10.packed_ref = bf16[8,18,8,128]{3,2,1,0:T(8,128)(2,1)S(1)} all-to-all(bf16[8,18,8,128]{3,2,1,0:T(8,128)(2,1)S(1)} %get-tuple-element.14), channel_id=1, replica_groups=mesh['groups'=2,'ep'=8,'rep'=2] {'ep'}, dimensions={0} | all-to-all | bytes 589824 | tf_op jit(solution)/shard_map/all_to_all | solution.py:336
  19.2 0.0 collective-permute-start
  19.2 0.0 copy-done
  19.2 0.0 copy-done.1
  19.2 0.0 copy-done.2
  19.2 0.8 %shard_map.76.acc_ref = f32[80,1024]{1,0:T(8,128)S(1)} custom-call(bf16[8,18,8,128]{3,2,1,0:T(8,128)(2,1)S(1)} %all_to_all.10.packed_ref, bf16[3584,512]{1,0:T(8,128)(2,1)S(1)} %bitcast.9, bf16[3584,512]{1,0:T(8,128)(2,1)S(1)} %bitcast.11, bf16[512,3584]{1,0:T(8,128)(2,1)S(1)} %bitcast.6), custom_call_target="tpu_custom_call" | custom-call | flops 1024 | bytes 1024 | tf_op jit(solution)/shard_map/pallas_call | solution.py:338
  20.0 0.7 %collective-permute-done.packed_ref = bf16[8,18,8,128]{3,2,1,0:T(8,128)(2,1)S(1)} collective-permute-done((bf16[8,18,8,128]{3,2,1,0:T(8,128)(2,1)S(1)}, bf16[8,18,8,128]{3,2,1,0:T(8,128)(2,1)S(1)}, u32[]{:S(2)}, u32[]{:S(2)}) %collective-permute-start) | collective-permute-done | bytes 294944 | tf_op jit(solution)/shard_map/ppermute | solution.py:337
  20.7 1.3 %shard_map.77 = (bf16[128,512]{1,0:T(8,128)(2,1)S(1)}, bf16[8,18,8,128]{3,2,1,0:T(8,128)(2,1)S(1)}) custom-call(bf16[8,18,8,128]{3,2,1,0:T(8,128)(2,1)S(1)} %collective-permute-done.packed_ref, f32[80,1024]{1,0:T(8,128)S(1)} %shard_map.76.acc_ref, bf16[3584,512]{1,0:T(8,128)(2,1)S(1)} %bitcast.10, bf16[3584,512]{1,0:T(8,128)(2,1)S(1)} %bitcast.12, ...), custom_call_target="tpu_custom_call" | custom-call | flops 528482304 | bytes 917504 | tf_op jit(solution)/shard_map/pallas_call | solution.py:358
  22.1 0.0 copy-start.6
  22.1 0.2 collective-permute-start.1
  22.3 0.4 %shard_map.78.mine_ref = f32[8,18,8,128]{3,2,1,0:T(8,128)S(1)} custom-call(bf16[128,512]{1,0:T(8,128)(2,1)S(1)} %get-tuple-element.15.hidden_ref, bf16[512,3584]{1,0:T(8,128)(2,1)S(1)} %bitcast.8), custom_call_target="tpu_custom_call" | custom-call | flops 234881024 | bytes 589824 | tf_op jit(solution)/shard_map/pallas_call | solution.py:368
  22.7 1.0 %collective-permute-done.1.other_ref = bf16[8,18,8,128]{3,2,1,0:T(8,128)(2,1)S(1)} collective-permute-done((bf16[8,18,8,128]{3,2,1,0:T(8,128)(2,1)S(1)}, bf16[8,18,8,128]{3,2,1,0:T(8,128)(2,1)S(1)}, u32[]{:S(2)}, u32[]{:S(2)}) %collective-permute-start.1) | collective-permute-done | bytes 294944 | tf_op jit(solution)/shard_map/ppermute | solution.py:367
  23.7 0.8 %shard_map.79 = bf16[8,18,8,128]{3,2,1,0:T(8,128)(2,1)} custom-call(f32[8,18,8,128]{3,2,1,0:T(8,128)S(1)} %shard_map.78.mine_ref, bf16[8,18,8,128]{3,2,1,0:T(8,128)(2,1)S(1)} %collective-permute-done.1.other_ref), custom_call_target="tpu_custom_call" | custom-call | flops 294912 | bytes 1179648 | tf_op jit(solution)/shard_map/pallas_call | solution.py:376
  24.5 3.4 %all-to-all-start.1 = ((bf16[8,18,8,128]{3,2,1,0:T(8,128)(2,1)}), bf16[8,18,8,128]{3,2,1,0:T(8,128)(2,1)S(1)}, u32[]{:S(2)}, u32[]{:S(2)}) async-start(bf16[8,18,8,128]{3,2,1,0:T(8,128)(2,1)} %shard_map.79), calls=%async_computation.1 | async-start | bytes 589824 | tf_op jit(solution)/shard_map/all_to_all | solution.py:379
  27.9 0.0 copy-done.6
  27.9 0.1 shard_map.75
  28.0 10.0 %all-to-all-done.1.packed_ref = bf16[8,18,8,128]{3,2,1,0:T(8,128)(2,1)S(1)} async-done(((bf16[8,18,8,128]{3,2,1,0:T(8,128)(2,1)}), bf16[8,18,8,128]{3,2,1,0:T(8,128)(2,1)S(1)}, u32[]{:S(2)}, u32[]{:S(2)}) %all-to-all-start.1) | async-done | bytes 294944 | tf_op jit(solution)/shard_map/all_to_all | solution.py:379
  38.0 0.9 %shard_map.80 = bf16[32,1792]{1,0:T(8,128)(2,1)} custom-call(bf16[4,32,128]{2,1,0:T(8,128)(2,1)S(1)} %get-tuple-element.12.pick_ref, f32[32,1]{1,0:T(8,128)S(1)} %get-tuple-element.13.column_ref, bf16[8,18,8,128]{3,2,1,0:T(8,128)(2,1)S(1)} %all-to-all-done.1.packed_ref), custom_call_target="tpu_custom_call" | custom-call | flops 14680064 | bytes 589824 | tf_op jit(solution)/shard_map/pallas_call | solution.py:380
  (1 shorter events, 0.0 us)
Async XLA Ops:
  0.0 0.7 %copy-start.4 = (s32[8]{0:T(128)S(1)}, s32[8]{0:T(128)}, u32[]{:S(2)}) copy-start(s32[8]{0:T(128)} %param.10) | copy-start | bytes 100
  0.0 0.7 %copy-start.5 = (s32[32,1]{0,1:T(1,128)S(1)}, s32[32,1]{0,1:T(1,128)}, u32[]{:S(2)}) copy-start(s32[32,1]{0,1:T(1,128)} %param.8) | copy-start | bytes 388
  0.0 0.9 %copy-start.3 = (bf16[32,1792]{1,0:T(8,128)(2,1)S(1)}, bf16[32,1792]{1,0:T(8,128)(2,1)}, u32[]{:S(2)}) copy-start(bf16[32,1792]{1,0:T(8,128)(2,1)} %tokens_ref.1) | copy-start | bytes 344068
  0.9 18.2 %copy-start = (bf16[1,512,3584]{2,1,0:T(8,128)(2,1)S(1)}, bf16[1,512,3584]{2,1,0:T(8,128)(2,1)}, u32[]{:S(2)}) copy-start(bf16[1,512,3584]{2,1,0:T(8,128)(2,1)} %param.13) | copy-start | bytes 11010052
  0.9 18.2 %copy-start.1 = (bf16[1,3584,512]{2,1,0:T(8,128)(2,1)S(1)}, bf16[1,3584,512]{2,1,0:T(8,128)(2,1)}, u32[]{:S(2)}) copy-start(bf16[1,3584,512]{2,1,0:T(8,128)(2,1)} %param.11) | copy-start | bytes 11010052
  0.9 18.2 %copy-start.2 = (bf16[1,3584,512]{2,1,0:T(8,128)(2,1)S(1)}, bf16[1,3584,512]{2,1,0:T(8,128)(2,1)}, u32[]{:S(2)}) copy-start(bf16[1,3584,512]{2,1,0:T(8,128)(2,1)} %param.12) | copy-start | bytes 11010052
  19.2 1.6 %collective-permute-start = (bf16[8,18,8,128]{3,2,1,0:T(8,128)(2,1)S(1)}, bf16[8,18,8,128]{3,2,1,0:T(8,128)(2,1)S(1)}, u32[]{:S(2)}, u32[]{:S(2)}) collective-permute-start(bf16[8,18,8,128]{3,2,1,0:T(8,128)(2,1)S(1)} %all_to_all.10.packed_ref), channel_id=1, source_target_pairs={{0,1},{1,0},{2,3},{3,2},{4,5},{5,4},{6,7},{7,6},{8,9},{9,8},{10,11... | collective-permute-start | bytes 884744 | tf_op jit(solution)/shard_map/ppermute | solution.py:337
  22.1 5.9 %copy-start.6 = (f32[32,1]{0,1:T(1,128)S(1)}, f32[32,1]{0,1:T(1,128)}, u32[]{:S(2)}) copy-start(f32[32,1]{0,1:T(1,128)} %param.9) | copy-start | bytes 388
  22.1 1.6 %collective-permute-start.1 = (bf16[8,18,8,128]{3,2,1,0:T(8,128)(2,1)S(1)}, bf16[8,18,8,128]{3,2,1,0:T(8,128)(2,1)S(1)}, u32[]{:S(2)}, u32[]{:S(2)}) collective-permute-start(bf16[8,18,8,128]{3,2,1,0:T(8,128)(2,1)S(1)} %get-tuple-element.16), channel_id=1, source_target_pairs={{0,1},{1,0},{2,3},{3,2},{4,5},{5,4},{6,7},{7,6},{8,9},{9,8},{10,11... | collective-permute-start | bytes 884744 | tf_op jit(solution)/shard_map/ppermute | solution.py:367
  24.5 13.5 %all-to-all-start.1 = ((bf16[8,18,8,128]{3,2,1,0:T(8,128)(2,1)}), bf16[8,18,8,128]{3,2,1,0:T(8,128)(2,1)S(1)}, u32[]{:S(2)}, u32[]{:S(2)}) async-start(bf16[8,18,8,128]{3,2,1,0:T(8,128)(2,1)} %shard_map.79), calls=%async_computation.1 | async-start | bytes 589824 | tf_op jit(solution)/shard_map/all_to_all | solution.py:379

commit v3 on v2

--- a/solution.py
+++ b/solution.py
@@ -47,6 +47,26 @@
     return jnp.floor((values.astype(F32) + 0.5) * (1.0 / divisor)).astype(jnp.int32)
 
 
+def exchange_order(members):
+    return sorted(range(members), key=lambda index: exchange_place(index, members))
+
+
+def exchange_place(index, members):
+    away = index - members // 2
+    return 2 * away if away >= 0 else -2 * away - 1
+
+
+def exchange(array, members):
+    return lax.all_to_all(
+        array,
+        "ep",
+        split_axis=0,
+        concat_axis=0,
+        tiled=True,
+        axis_index_groups=[exchange_order(members)],
+    )
+
+
 def to_column(row):
     size = row.shape[1]
     diagonal = iota((size, size), 0) == iota((size, size), 1)
@@ -71,7 +91,8 @@
     ]
     before = jnp.where(iota((tok, tok), 0) < iota((tok, tok), 1), 1.0, 0.0).astype(BF16)
     counts = jnp.dot(sum(hits).astype(BF16), before, preferred_element_type=F32)
-    line = iota((slots, tok), 0).astype(F32)
+    away = iota((slots, tok), 0) - slots // 2
+    line = jnp.where(away >= 0, 2 * away, -2 * away - 1).astype(F32)
     found = []
     for hit in hits:
         slot = jnp.sum(hit * line, axis=0, keepdims=True).astype(jnp.int32)
@@ -333,7 +354,7 @@
         COVER_BYTES,
         8 * MIB,
     )(warm, slot_row, ids, tokens)
-    arrived = lax.all_to_all(send, "ep", split_axis=0, concat_axis=0, tiled=True)
+    arrived = exchange(send, slots)
     partner = lax.ppermute(arrived, "rep", swap)
     acc = call(
         functools.partial(own_kernel, plan),
@@ -376,7 +397,7 @@
     result = call(
         sum_kernel, [VMEM, VMEM], packed, packed_bytes, 4 * packed_bytes, 4 * MIB
     )(mine, received)
-    returned = lax.all_to_all(result, "ep", split_axis=0, concat_axis=0, tiled=True)
+    returned = exchange(result, slots)
     return call(
         functools.partial(combine_kernel, plan),
         [VMEM, VMEM, VMEM],

time: 39.1 us -> 36.9 us (0.944)
  waiting for transfers between devices: 11.7 us -> 9.92 us
  blocking collectives: 17.7 us -> 16 us
  starting transfers between devices: 3.62 us -> 4.89 us
    all_to_all x1, waiting for transfers between devices: 9.95 us -> 8.15 us  [exchange(): lax.all_to_all(array, 'ep', split_axis=0, concat_axis=0, tiled=True, axis...]
    all_to_all x1, blocking collectives: 17.7 us -> 16 us  [exchange(): lax.all_to_all(array, 'ep', split_axis=0, concat_axis=0, tiled=True, axis...]
    all_to_all x1, starting transfers between devices: 3.42 us -> 4.69 us  [exchange(): lax.all_to_all(array, 'ep', split_axis=0, concat_axis=0, tiled=True, axis...]
  transfers between devices with their start and end apart: 3 -> 3, of which waited for: 3 -> 3; matrix products, arithmetic and copies ran while one was open for 0% -> 0% of each run, Pallas kernels for 3% -> 4%
where the time goes in v3:
time: 36.9 us; the launch traced here: 36.7 us
  blocking collectives  16 us (43%)
  waiting for transfers between devices  9.92 us (27%)
  starting transfers between devices  4.89 us (13%)
  Pallas kernels  4.81 us (13%)
  local copies, waits for them, and re-layouts  0.94 us (3%)
    all_to_all x1, blocking collectives, exchange(): lax.all_to_all(array, 'ep', split_axis=0, concat_axis=0, tiled=True, axis...  16 us
    all_to_all x1, waiting for transfers between devices, exchange(): lax.all_to_all(array, 'ep', split_axis=0, concat_axis=0, tiled=True, axis...  8.15 us
    all_to_all x1, starting transfers between devices, exchange(): lax.all_to_all(array, 'ep', split_axis=0, concat_axis=0, tiled=True, axis...  4.69 us
    pallas_call x1, Pallas kernels, body(): call(functools.partial(other_kernel, plan), [VMEM, VMEM, VMEM, VMEM, VMEM...  1.32 us
    ppermute x1, waiting for transfers between devices, body(): received = lax.ppermute(outbound, 'rep', swap)  1.04 us
    unnamed x14, local copies, waits for them, and re-layouts  0.94 us
    pallas_call x1, Pallas kernels, body(): call(functools.partial(combine_kernel, plan), [VMEM, VMEM, VMEM], jax.Sha...  0.88 us
    pallas_call x1, Pallas kernels, body(): call(functools.partial(own_kernel, plan), [VMEM] * 4, jax.ShapeDtypeStruc...  0.83 us
  transfers between devices with their start and end apart: 3, of which 3 were waited for; matrix products, arithmetic and copies ran while one was open for 0% of the time, Pallas kernels for 4%

profile of v3, /device:TPU:0, one launch (start us, length us, event | category | flops | bytes accessed | tf_op | source)
XLA Modules:
  0.0 36.7 jit_solution(148070006290986843)
XLA Ops:
  0.0 0.0 copy-start.4
  0.0 0.0 copy-start.5
  0.0 0.0 copy-start.3
  0.0 0.6 %copy-done.4 = s32[8]{0:T(128)S(1)} copy-done((s32[8]{0:T(128)S(1)}, s32[8]{0:T(128)}, u32[]{:S(2)}) %copy-start.4) | copy-done | bytes 56
  0.7 0.0 copy-done.5
  0.7 0.3 copy-done.3
  0.9 0.0 copy-start
  0.9 0.0 copy-start.1
  0.9 0.0 copy-start.2
  0.9 0.5 %shard_map.74 = (bf16[8,18,8,128]{3,2,1,0:T(8,128)(2,1)S(1)}, s32[2,32]{1,0:T(2,128)S(1)}) custom-call(f32[8,128]{1,0:T(8,128)S(1)} %shard_map.73.warm_ref, s32[1,8]{1,0:T(1,128)S(1)} %bitcast.13, s32[1,32]{1,0:T(1,128)S(1)} %bitcast.14, bf16[32,1792]{1,0:T(8,128)(2,1)S(1)} %copy-done.3), custom_call_target="tpu_custom_call" | custom-call | flops 17179869184 | bytes 33554432 | tf_op jit(solution)/shard_map/pallas_call | solution.py:349
  1.5 16.0 %all_to_all.10.packed_ref = bf16[8,18,8,128]{3,2,1,0:T(8,128)(2,1)S(1)} all-to-all(bf16[8,18,8,128]{3,2,1,0:T(8,128)(2,1)S(1)} %get-tuple-element.14), channel_id=1, replica_groups={{8,6,10,4,12,2,14,0},{9,7,11,5,13,3,15,1},{24,22,26,20,28,18,30,16},{25..., dimensions={0} | all-to-all | bytes 589824 | tf_op jit(solution)/shard_map/all_to_all | solution.py:60
  17.5 0.0 collective-permute-start
  17.5 0.0 copy-done
  17.5 0.0 copy-done.1
  17.5 0.0 copy-done.2
  17.5 0.8 %shard_map.76.acc_ref = f32[80,1024]{1,0:T(8,128)S(1)} custom-call(bf16[8,18,8,128]{3,2,1,0:T(8,128)(2,1)S(1)} %all_to_all.10.packed_ref, bf16[3584,512]{1,0:T(8,128)(2,1)S(1)} %bitcast.9, bf16[3584,512]{1,0:T(8,128)(2,1)S(1)} %bitcast.11, bf16[512,3584]{1,0:T(8,128)(2,1)S(1)} %bitcast.6), custom_call_target="tpu_custom_call" | custom-call | flops 1024 | bytes 1024 | tf_op jit(solution)/shard_map/pallas_call | solution.py:359
  18.3 0.7 %collective-permute-done.packed_ref = bf16[8,18,8,128]{3,2,1,0:T(8,128)(2,1)S(1)} collective-permute-done((bf16[8,18,8,128]{3,2,1,0:T(8,128)(2,1)S(1)}, bf16[8,18,8,128]{3,2,1,0:T(8,128)(2,1)S(1)}, u32[]{:S(2)}, u32[]{:S(2)}) %collective-permute-start) | collective-permute-done | bytes 294944 | tf_op jit(solution)/shard_map/ppermute | solution.py:358
  19.1 1.3 %shard_map.77 = (bf16[128,512]{1,0:T(8,128)(2,1)S(1)}, bf16[8,18,8,128]{3,2,1,0:T(8,128)(2,1)S(1)}) custom-call(bf16[8,18,8,128]{3,2,1,0:T(8,128)(2,1)S(1)} %collective-permute-done.packed_ref, f32[80,1024]{1,0:T(8,128)S(1)} %shard_map.76.acc_ref, bf16[3584,512]{1,0:T(8,128)(2,1)S(1)} %bitcast.10, bf16[3584,512]{1,0:T(8,128)(2,1)S(1)} %bitcast.12, ...), custom_call_target="tpu_custom_call" | custom-call | flops 528482304 | bytes 917504 | tf_op jit(solution)/shard_map/pallas_call | solution.py:379
  20.4 0.0 copy-start.6
  20.4 0.2 collective-permute-start.1
  20.6 0.4 %shard_map.78.mine_ref = f32[8,18,8,128]{3,2,1,0:T(8,128)S(1)} custom-call(bf16[128,512]{1,0:T(8,128)(2,1)S(1)} %get-tuple-element.15.hidden_ref, bf16[512,3584]{1,0:T(8,128)(2,1)S(1)} %bitcast.8), custom_call_target="tpu_custom_call" | custom-call | flops 234881024 | bytes 589824 | tf_op jit(solution)/shard_map/pallas_call | solution.py:389
  21.0 1.0 %collective-permute-done.1.other_ref = bf16[8,18,8,128]{3,2,1,0:T(8,128)(2,1)S(1)} collective-permute-done((bf16[8,18,8,128]{3,2,1,0:T(8,128)(2,1)S(1)}, bf16[8,18,8,128]{3,2,1,0:T(8,128)(2,1)S(1)}, u32[]{:S(2)}, u32[]{:S(2)}) %collective-permute-start.1) | collective-permute-done | bytes 294944 | tf_op jit(solution)/shard_map/ppermute | solution.py:388
  22.1 0.8 %shard_map.79 = bf16[8,18,8,128]{3,2,1,0:T(8,128)(2,1)} custom-call(f32[8,18,8,128]{3,2,1,0:T(8,128)S(1)} %shard_map.78.mine_ref, bf16[8,18,8,128]{3,2,1,0:T(8,128)(2,1)S(1)} %collective-permute-done.1.other_ref), custom_call_target="tpu_custom_call" | custom-call | flops 294912 | bytes 1179648 | tf_op jit(solution)/shard_map/pallas_call | solution.py:397
  22.8 4.7 %all-to-all-start.1 = ((bf16[8,18,8,128]{3,2,1,0:T(8,128)(2,1)}), bf16[8,18,8,128]{3,2,1,0:T(8,128)(2,1)S(1)}, u32[]{:S(2)}, u32[]{:S(2)}) async-start(bf16[8,18,8,128]{3,2,1,0:T(8,128)(2,1)} %shard_map.79), calls=%async_computation.1 | async-start | bytes 589824 | tf_op jit(solution)/shard_map/all_to_all | solution.py:60
  27.5 0.0 copy-done.6
  27.5 0.1 shard_map.75
  27.6 8.2 %all-to-all-done.1.packed_ref = bf16[8,18,8,128]{3,2,1,0:T(8,128)(2,1)S(1)} async-done(((bf16[8,18,8,128]{3,2,1,0:T(8,128)(2,1)}), bf16[8,18,8,128]{3,2,1,0:T(8,128)(2,1)S(1)}, u32[]{:S(2)}, u32[]{:S(2)}) %all-to-all-start.1) | async-done | bytes 294944 | tf_op jit(solution)/shard_map/all_to_all | solution.py:60
  35.8 0.9 %shard_map.80 = bf16[32,1792]{1,0:T(8,128)(2,1)} custom-call(bf16[4,32,128]{2,1,0:T(8,128)(2,1)S(1)} %get-tuple-element.12.pick_ref, f32[32,1]{1,0:T(8,128)S(1)} %get-tuple-element.13.column_ref, bf16[8,18,8,128]{3,2,1,0:T(8,128)(2,1)S(1)} %all-to-all-done.1.packed_ref), custom_call_target="tpu_custom_call" | custom-call | flops 14680064 | bytes 589824 | tf_op jit(solution)/shard_map/pallas_call | solution.py:401
  (1 shorter events, 0.0 us)
Async XLA Ops:
  0.0 0.7 %copy-start.4 = (s32[8]{0:T(128)S(1)}, s32[8]{0:T(128)}, u32[]{:S(2)}) copy-start(s32[8]{0:T(128)} %param.10) | copy-start | bytes 100
  0.0 0.7 %copy-start.5 = (s32[32,1]{0,1:T(1,128)S(1)}, s32[32,1]{0,1:T(1,128)}, u32[]{:S(2)}) copy-start(s32[32,1]{0,1:T(1,128)} %param.8) | copy-start | bytes 388
  0.0 0.9 %copy-start.3 = (bf16[32,1792]{1,0:T(8,128)(2,1)S(1)}, bf16[32,1792]{1,0:T(8,128)(2,1)}, u32[]{:S(2)}) copy-start(bf16[32,1792]{1,0:T(8,128)(2,1)} %tokens_ref.1) | copy-start | bytes 344068
  0.9 16.6 %copy-start = (bf16[1,512,3584]{2,1,0:T(8,128)(2,1)S(1)}, bf16[1,512,3584]{2,1,0:T(8,128)(2,1)}, u32[]{:S(2)}) copy-start(bf16[1,512,3584]{2,1,0:T(8,128)(2,1)} %param.13) | copy-start | bytes 11010052
  0.9 16.6 %copy-start.1 = (bf16[1,3584,512]{2,1,0:T(8,128)(2,1)S(1)}, bf16[1,3584,512]{2,1,0:T(8,128)(2,1)}, u32[]{:S(2)}) copy-start(bf16[1,3584,512]{2,1,0:T(8,128)(2,1)} %param.11) | copy-start | bytes 11010052
  0.9 16.6 %copy-start.2 = (bf16[1,3584,512]{2,1,0:T(8,128)(2,1)S(1)}, bf16[1,3584,512]{2,1,0:T(8,128)(2,1)}, u32[]{:S(2)}) copy-start(bf16[1,3584,512]{2,1,0:T(8,128)(2,1)} %param.12) | copy-start | bytes 11010052
  17.5 1.6 %collective-permute-start = (bf16[8,18,8,128]{3,2,1,0:T(8,128)(2,1)S(1)}, bf16[8,18,8,128]{3,2,1,0:T(8,128)(2,1)S(1)}, u32[]{:S(2)}, u32[]{:S(2)}) collective-permute-start(bf16[8,18,8,128]{3,2,1,0:T(8,128)(2,1)S(1)} %all_to_all.10.packed_ref), channel_id=1, source_target_pairs={{0,1},{1,0},{2,3},{3,2},{4,5},{5,4},{6,7},{7,6},{8,9},{9,8},{10,11... | collective-permute-start | bytes 884744 | tf_op jit(solution)/shard_map/ppermute | solution.py:358
  20.4 7.1 %copy-start.6 = (f32[32,1]{0,1:T(1,128)S(1)}, f32[32,1]{0,1:T(1,128)}, u32[]{:S(2)}) copy-start(f32[32,1]{0,1:T(1,128)} %param.9) | copy-start | bytes 388
  20.4 1.6 %collective-permute-start.1 = (bf16[8,18,8,128]{3,2,1,0:T(8,128)(2,1)S(1)}, bf16[8,18,8,128]{3,2,1,0:T(8,128)(2,1)S(1)}, u32[]{:S(2)}, u32[]{:S(2)}) collective-permute-start(bf16[8,18,8,128]{3,2,1,0:T(8,128)(2,1)S(1)} %get-tuple-element.16), channel_id=1, source_target_pairs={{0,1},{1,0},{2,3},{3,2},{4,5},{5,4},{6,7},{7,6},{8,9},{9,8},{10,11... | collective-permute-start | bytes 884744 | tf_op jit(solution)/shard_map/ppermute | solution.py:388
  22.8 13.0 %all-to-all-start.1 = ((bf16[8,18,8,128]{3,2,1,0:T(8,128)(2,1)}), bf16[8,18,8,128]{3,2,1,0:T(8,128)(2,1)S(1)}, u32[]{:S(2)}, u32[]{:S(2)}) async-start(bf16[8,18,8,128]{3,2,1,0:T(8,128)(2,1)} %shard_map.79), calls=%async_computation.1 | async-start | bytes 589824 | tf_op jit(solution)/shard_map/all_to_all | solution.py:60

commit v4 on v3

--- a/solution.py
+++ b/solution.py
@@ -47,13 +47,15 @@
     return jnp.floor((values.astype(F32) + 0.5) * (1.0 / divisor)).astype(jnp.int32)
 
 
+def exchange_place(index, members):
+    away = index - 1 - members // 2
+    away = jnp.where(index == 0, members // 2 - 1, away)
+    return jnp.where(away >= 0, 2 * away, -2 * away - 1)
+
+
 def exchange_order(members):
-    return sorted(range(members), key=lambda index: exchange_place(index, members))
-
-
-def exchange_place(index, members):
-    away = index - members // 2
-    return 2 * away if away >= 0 else -2 * away - 1
+    away = [index // 2 if index % 2 == 0 else -(index // 2) - 1 for index in range(members)]
+    return [(1 + members // 2 + step) % members for step in away]
 
 
 def exchange(array, members):
@@ -91,8 +93,7 @@
     ]
     before = jnp.where(iota((tok, tok), 0) < iota((tok, tok), 1), 1.0, 0.0).astype(BF16)
     counts = jnp.dot(sum(hits).astype(BF16), before, preferred_element_type=F32)
-    away = iota((slots, tok), 0) - slots // 2
-    line = jnp.where(away >= 0, 2 * away, -2 * away - 1).astype(F32)
+    line = exchange_place(iota((slots, tok), 0), slots).astype(F32)
     found = []
     for hit in hits:
         slot = jnp.sum(hit * line, axis=0, keepdims=True).astype(jnp.int32)
@@ -235,9 +236,7 @@
         ).astype(out_ref.dtype)
 
 
-def other_kernel(
-    plan, packed_ref, acc_ref, gate_ref, up_ref, down_ref, hidden_ref, out_ref, rows_ref
-):
+def other_kernel(plan, packed_ref, acc_ref, gate_ref, up_ref, hidden_ref, rows_ref):
     unpack_rows(plan, packed_ref, rows_ref)
     first = pl.multiple_of((1 - lax.axis_index("rep")) * plan.feat, LANES)
     hid = gate_ref.shape[1]
@@ -248,9 +247,11 @@
     up = acc_ref[:, hid:] + jnp.dot(
         rows, up_ref[pl.ds(first, plan.feat), :], preferred_element_type=F32
     )
-    hidden = (gate / (1.0 + jnp.exp(-gate)) * up).astype(BF16)
-    if plan.full:
-        hidden_ref[: plan.main_rows] = hidden[: plan.main_rows]
+    hidden_ref[...] = (gate / (1.0 + jnp.exp(-gate)) * up).astype(BF16)
+
+
+def down_product(plan, hidden_ref, down_ref):
+    rows = [hidden_ref[: plan.main_rows]] if plan.full else []
     if plan.tail:
         shape = (plan.tail_wide, plan.tail_rows)
         line, col = iota(shape, 0), iota(shape, 1)
@@ -258,25 +259,22 @@
         spot = line - sender * SUBLANES
         spot = spot - floor_div(spot, plan.tail) * plan.tail
         hot = jnp.where(sender * plan.tail + spot == col, 1.0, 0.0).astype(BF16)
-        hidden_ref[plan.main_rows :] = jnp.dot(
-            hot, hidden[plan.main_rows :], preferred_element_type=F32
-        ).astype(BF16)
-    product = jnp.dot(
-        hidden_ref[...], down_ref[:, pl.ds(first, plan.feat)], preferred_element_type=F32
-    )
-    emit_packed(plan, product, out_ref)
-
-
-def down_kernel(plan, hidden_ref, down_ref, out_ref):
+        tail = jnp.dot(hot, hidden_ref[plan.main_rows :], preferred_element_type=F32)
+        rows.append(tail.astype(BF16))
     first = pl.multiple_of(lax.axis_index("rep") * plan.feat, LANES)
-    product = jnp.dot(
-        hidden_ref[...], down_ref[:, pl.ds(first, plan.feat)], preferred_element_type=F32
-    )
-    emit_packed(plan, product, out_ref)
-
-
-def sum_kernel(mine_ref, other_ref, out_ref):
-    out_ref[...] = (mine_ref[...] + other_ref[...].astype(F32)).astype(BF16)
+    return jnp.dot(
+        jnp.concatenate(rows, axis=0),
+        down_ref[:, pl.ds(first, plan.feat)],
+        preferred_element_type=F32,
+    )
+
+
+def down_own_kernel(plan, hidden_ref, down_ref, out_ref):
+    out_ref[...] = down_product(plan, hidden_ref, down_ref)
+
+
+def down_other_kernel(plan, hidden_ref, down_ref, mine_ref, out_ref):
+    emit_packed(plan, mine_ref[...] + down_product(plan, hidden_ref, down_ref), out_ref)
 
 
 def combine_kernel(plan, pick_ref, column_ref, packed_ref, out_ref):
@@ -338,6 +336,7 @@
 
     slot_row, ids, gates = slot_expert.reshape(1, slots), expert_ids.T, gate_values.T
 
+    down_swapped = lax.ppermute(down_local, "rep", swap)
     warm = call(
         warm_kernel,
         [],
@@ -376,27 +375,32 @@
         1 << 10,
         4 * MIB,
     )(found, gates)
-    hidden, outbound = call(
+    hidden = call(
         functools.partial(other_kernel, plan),
-        [VMEM, VMEM, VMEM, VMEM, VMEM],
-        [jax.ShapeDtypeStruct((plan.wide, hid), BF16), packed],
-        half_flops + 2 * plan.wide * hid * feat,
-        2 * packed_bytes + 8 * plan.rows * hid,
+        [VMEM] * 4,
+        jax.ShapeDtypeStruct((plan.rows, hid), BF16),
+        half_flops,
+        packed_bytes + 8 * plan.rows * hid,
         8 * MIB,
         [rows_scratch],
-    )(partner, acc, gate_local, up_local, down_local)
-    received = lax.ppermute(outbound, "rep", swap)
+    )(partner, acc, gate_local, up_local)
+    received = lax.ppermute(hidden, "rep", swap)
     mine = call(
-        functools.partial(down_kernel, plan),
-        [VMEM, VMEM],
-        jax.ShapeDtypeStruct(plan.packed, F32),
+        functools.partial(down_own_kernel, plan),
+        [VMEM] * 2,
+        jax.ShapeDtypeStruct((plan.wide, feat), F32),
         2 * plan.wide * hid * feat,
         2 * packed_bytes,
         8 * MIB,
     )(hidden, down_local)
     result = call(
-        sum_kernel, [VMEM, VMEM], packed, packed_bytes, 4 * packed_bytes, 4 * MIB
-    )(mine, received)
+        functools.partial(down_other_kernel, plan),
+        [VMEM] * 3,
+        packed,
+        2 * plan.wide * hid * feat,
+        2 * packed_bytes,
+        8 * MIB,
+    )(received, down_swapped, mine)
     returned = exchange(result, slots)
     return call(
         functools.partial(combine_kernel, plan),

time: 36.9 us -> 36 us (0.976)
  starting transfers between devices: 4.89 us -> 6.44 us
  waiting for transfers between devices: 9.92 us -> 8.64 us
  blocking collectives: 16 us -> 15.4 us
  local copies, waits for them, and re-layouts: 0.94 us -> 0.36 us
    all_to_all x1, starting transfers between devices: 4.69 us -> 5.68 us  [exchange(): lax.all_to_all(array, 'ep', split_axis=0, concat_axis=0, tiled=True, axis...]
    all_to_all x1, waiting for transfers between devices: 8.15 us -> 7.29 us  [exchange(): lax.all_to_all(array, 'ep', split_axis=0, concat_axis=0, tiled=True, axis...]
    all_to_all x1, blocking collectives: 16 us -> 15.4 us  [exchange(): lax.all_to_all(array, 'ep', split_axis=0, concat_axis=0, tiled=True, axis...]
    unnamed x14, local copies, waits for them, and re-layouts: 0.94 us -> 0.36 us
    ppermute x1 -> x2, starting transfers between devices: 0.19 us -> 0.76 us  [the longest x1 0.56 us: body(): down_swapped = lax.ppermute(down_local, 'rep', swap)]
    ppermute x1 -> x2, waiting for transfers between devices: 1.04 us -> 0.62 us  [the longest x1 0.62 us: body(): received = lax.ppermute(hidden, 'rep', swap)]
  transfers between devices with their start and end apart: 3 -> 4, of which waited for: 3 -> 3; matrix products, arithmetic and copies ran while one was open for 0% -> 0% of each run, Pallas kernels for 4% -> 8%
where the time goes in v4:
time: 36 us; the launch traced here: 35.8 us
  blocking collectives  15.4 us (43%)
  waiting for transfers between devices  8.64 us (24%)
  starting transfers between devices  6.44 us (18%)
  Pallas kernels  4.89 us (14%)
  local copies, waits for them, and re-layouts  0.36 us (1%)
    all_to_all x1, blocking collectives, exchange(): lax.all_to_all(array, 'ep', split_axis=0, concat_axis=0, tiled=True, axis...  15.4 us
    all_to_all x1, waiting for transfers between devices, exchange(): lax.all_to_all(array, 'ep', split_axis=0, concat_axis=0, tiled=True, axis...  7.29 us
    all_to_all x1, starting transfers between devices, exchange(): lax.all_to_all(array, 'ep', split_axis=0, concat_axis=0, tiled=True, axis...  5.68 us
    pallas_call x1, Pallas kernels, body(): call(functools.partial(down_other_kernel, plan), [VMEM] * 3, packed, 2 *...  1.23 us
    pallas_call x1, Pallas kernels, body(): call(functools.partial(combine_kernel, plan), [VMEM, VMEM, VMEM], jax.Sha...  0.88 us
    pallas_call x1, Pallas kernels, body(): call(functools.partial(other_kernel, plan), [VMEM] * 4, jax.ShapeDtypeStr...  0.84 us
    pallas_call x1, Pallas kernels, body(): call(functools.partial(own_kernel, plan), [VMEM] * 4, jax.ShapeDtypeStruc...  0.83 us
    ppermute x1, waiting for transfers between devices, body(): partner = lax.ppermute(arrived, 'rep', swap)  0.73 us
  transfers between devices with their start and end apart: 4, of which 3 were waited for; matrix products, arithmetic and copies ran while one was open for 0% of the time, Pallas kernels for 8%

profile of v4, /device:TPU:0, one launch (start us, length us, event | category | flops | bytes accessed | tf_op | source)
XLA Modules:
  0.0 35.8 jit_solution(10541644753159404184)
XLA Ops:
  0.0 0.0 copy-start.3
  0.0 0.0 copy-start.4
  0.0 0.0 copy-start.5
  0.0 0.6 %collective-permute-start.2 = (bf16[512,3584]{1,0:T(8,128)(2,1)}, bf16[512,3584]{1,0:T(8,128)(2,1)S(1)}, u32[]{:S(2)}, u32[]{:S(2)}) collective-permute-start(bf16[512,3584]{1,0:T(8,128)(2,1)} %bitcast.10), channel_id=1, source_target_pairs={{0,1},{1,0},{2,3},{3,2},{4,5},{5,4},{6,7},{7,6},{8,9},{9,8},{10,11... | collective-permute-start | bytes 11010056 | tf_op jit(solution)/shard_map/ppermute | solution.py:339
  0.6 0.3 copy-done.3
  0.9 0.0 copy-done.4
  0.9 0.0 copy-done.5
  0.9 0.0 copy-start
  0.9 0.0 copy-start.1
  0.9 0.0 copy-start.2
  0.9 0.5 %shard_map.74 = (bf16[8,18,8,128]{3,2,1,0:T(8,128)(2,1)S(1)}, s32[2,32]{1,0:T(2,128)S(1)}) custom-call(f32[8,128]{1,0:T(8,128)S(1)} %shard_map.73.warm_ref, s32[1,8]{1,0:T(1,128)S(1)} %bitcast.13, s32[1,32]{1,0:T(1,128)S(1)} %bitcast.14, bf16[32,1792]{1,0:T(8,128)(2,1)S(1)} %copy-done.3), custom_call_target="tpu_custom_call" | custom-call | flops 17179869184 | bytes 33554432 | tf_op jit(solution)/shard_map/pallas_call | solution.py:348
  1.4 15.4 %all_to_all.10.packed_ref = bf16[8,18,8,128]{3,2,1,0:T(8,128)(2,1)S(1)} all-to-all(bf16[8,18,8,128]{3,2,1,0:T(8,128)(2,1)S(1)} %get-tuple-element.12), channel_id=1, replica_groups={{10,8,12,6,14,4,0,2},{11,9,13,7,15,5,1,3},{26,24,28,22,30,20,16,18},{27..., dimensions={0} | all-to-all | bytes 589824 | tf_op jit(solution)/shard_map/all_to_all | solution.py:62
  16.8 0.0 collective-permute-start
  16.8 0.0 copy-done
  16.8 0.0 copy-done.1
  16.8 0.0 copy-done.2
  16.8 0.8 %shard_map.76.acc_ref = f32[80,1024]{1,0:T(8,128)S(1)} custom-call(bf16[8,18,8,128]{3,2,1,0:T(8,128)(2,1)S(1)} %all_to_all.10.packed_ref, bf16[3584,512]{1,0:T(8,128)(2,1)S(1)} %bitcast.6, bf16[3584,512]{1,0:T(8,128)(2,1)S(1)} %bitcast.8, bf16[512,3584]{1,0:T(8,128)(2,1)S(1)} %bitcast.11), custom_call_target="tpu_custom_call" | custom-call | flops 1024 | bytes 1024 | tf_op jit(solution)/shard_map/pallas_call | solution.py:358
  17.7 0.7 %collective-permute-done.packed_ref = bf16[8,18,8,128]{3,2,1,0:T(8,128)(2,1)S(1)} collective-permute-done((bf16[8,18,8,128]{3,2,1,0:T(8,128)(2,1)S(1)}, bf16[8,18,8,128]{3,2,1,0:T(8,128)(2,1)S(1)}, u32[]{:S(2)}, u32[]{:S(2)}) %collective-permute-start) | collective-permute-done | bytes 294944 | tf_op jit(solution)/shard_map/ppermute | solution.py:357
  18.4 0.8 %shard_map.77.hidden_ref = bf16[80,512]{1,0:T(8,128)(2,1)S(1)} custom-call(bf16[8,18,8,128]{3,2,1,0:T(8,128)(2,1)S(1)} %collective-permute-done.packed_ref, f32[80,1024]{1,0:T(8,128)S(1)} %shard_map.76.acc_ref, bf16[3584,512]{1,0:T(8,128)(2,1)S(1)} %bitcast.7, bf16[3584,512]{1,0:T(8,128)(2,1)S(1)} %bitcast.9), custom_call_target="tpu_custom_call" | custom-call | flops 293601280 | bytes 622592 | tf_op jit(solution)/shard_map/pallas_call | solution.py:378
  19.2 0.2 collective-permute-start.1
  19.4 0.5 %shard_map.78.mine_ref = f32[128,1792]{1,0:T(8,128)S(1)} custom-call(bf16[80,512]{1,0:T(8,128)(2,1)S(1)} %shard_map.77.hidden_ref, bf16[512,3584]{1,0:T(8,128)(2,1)S(1)} %bitcast.12), custom_call_target="tpu_custom_call" | custom-call | flops 234881024 | bytes 589824 | tf_op jit(solution)/shard_map/pallas_call | solution.py:388
  19.9 0.0 copy-start.6
  19.9 0.6 %collective-permute-done.1.hidden_ref = bf16[80,512]{1,0:T(8,128)(2,1)S(1)} collective-permute-done((bf16[80,512]{1,0:T(8,128)(2,1)S(1)}, bf16[80,512]{1,0:T(8,128)(2,1)S(1)}, u32[]{:S(2)}, u32[]{:S(2)}) %collective-permute-start.1) | collective-permute-done | bytes 81952 | tf_op jit(solution)/shard_map/ppermute | solution.py:387
  20.6 0.0 collective-permute-done.2.down_ref
  20.6 1.2 %shard_map.79 = bf16[8,18,8,128]{3,2,1,0:T(8,128)(2,1)} custom-call(bf16[80,512]{1,0:T(8,128)(2,1)S(1)} %collective-permute-done.1.hidden_ref, bf16[512,3584]{1,0:T(8,128)(2,1)S(1)} %collective-permute-done.2.down_ref, f32[128,1792]{1,0:T(8,128)S(1)} %shard_map.78.mine_ref), custom_call_target="tpu_custom_call" | custom-call | flops 234881024 | bytes 589824 | tf_op jit(solution)/shard_map/pallas_call | solution.py:396
  21.8 5.7 %all-to-all-start.1 = ((bf16[8,18,8,128]{3,2,1,0:T(8,128)(2,1)}), bf16[8,18,8,128]{3,2,1,0:T(8,128)(2,1)S(1)}, u32[]{:S(2)}, u32[]{:S(2)}) async-start(bf16[8,18,8,128]{3,2,1,0:T(8,128)(2,1)} %shard_map.79), calls=%async_computation.1 | async-start | bytes 589824 | tf_op jit(solution)/shard_map/all_to_all | solution.py:62
  27.5 0.0 copy-done.6
  27.5 0.1 shard_map.75
  27.6 7.3 %all-to-all-done.1.packed_ref = bf16[8,18,8,128]{3,2,1,0:T(8,128)(2,1)S(1)} async-done(((bf16[8,18,8,128]{3,2,1,0:T(8,128)(2,1)}), bf16[8,18,8,128]{3,2,1,0:T(8,128)(2,1)S(1)}, u32[]{:S(2)}, u32[]{:S(2)}) %all-to-all-start.1) | async-done | bytes 294944 | tf_op jit(solution)/shard_map/all_to_all | solution.py:62
  34.9 0.9 %shard_map.80 = bf16[32,1792]{1,0:T(8,128)(2,1)} custom-call(bf16[4,32,128]{2,1,0:T(8,128)(2,1)S(1)} %get-tuple-element.10.pick_ref, f32[32,1]{1,0:T(8,128)S(1)} %get-tuple-element.11.column_ref, bf16[8,18,8,128]{3,2,1,0:T(8,128)(2,1)S(1)} %all-to-all-done.1.packed_ref), custom_call_target="tpu_custom_call" | custom-call | flops 14680064 | bytes 589824 | tf_op jit(solution)/shard_map/pallas_call | solution.py:405
  (1 shorter events, 0.0 us)
Async XLA Ops:
  0.0 0.9 %copy-start.3 = (bf16[32,1792]{1,0:T(8,128)(2,1)S(1)}, bf16[32,1792]{1,0:T(8,128)(2,1)}, u32[]{:S(2)}) copy-start(bf16[32,1792]{1,0:T(8,128)(2,1)} %tokens_ref.1) | copy-start | bytes 344068
  0.0 0.9 %copy-start.4 = (s32[8]{0:T(128)S(1)}, s32[8]{0:T(128)}, u32[]{:S(2)}) copy-start(s32[8]{0:T(128)} %param.10) | copy-start | bytes 100
  0.0 0.9 %copy-start.5 = (s32[32,1]{0,1:T(1,128)S(1)}, s32[32,1]{0,1:T(1,128)}, u32[]{:S(2)}) copy-start(s32[32,1]{0,1:T(1,128)} %param.8) | copy-start | bytes 388
  0.0 20.6 %collective-permute-start.2 = (bf16[512,3584]{1,0:T(8,128)(2,1)}, bf16[512,3584]{1,0:T(8,128)(2,1)S(1)}, u32[]{:S(2)}, u32[]{:S(2)}) collective-permute-start(bf16[512,3584]{1,0:T(8,128)(2,1)} %bitcast.10), channel_id=1, source_target_pairs={{0,1},{1,0},{2,3},{3,2},{4,5},{5,4},{6,7},{7,6},{8,9},{9,8},{10,11... | collective-permute-start | bytes 11010056 | tf_op jit(solution)/shard_map/ppermute | solution.py:339
  0.9 15.9 %copy-start = (bf16[1,3584,512]{2,1,0:T(8,128)(2,1)S(1)}, bf16[1,3584,512]{2,1,0:T(8,128)(2,1)}, u32[]{:S(2)}) copy-start(bf16[1,3584,512]{2,1,0:T(8,128)(2,1)} %param.11) | copy-start | bytes 11010052
  0.9 15.9 %copy-start.1 = (bf16[1,3584,512]{2,1,0:T(8,128)(2,1)S(1)}, bf16[1,3584,512]{2,1,0:T(8,128)(2,1)}, u32[]{:S(2)}) copy-start(bf16[1,3584,512]{2,1,0:T(8,128)(2,1)} %param.12) | copy-start | bytes 11010052
  0.9 15.9 %copy-start.2 = (bf16[1,512,3584]{2,1,0:T(8,128)(2,1)S(1)}, bf16[1,512,3584]{2,1,0:T(8,128)(2,1)}, u32[]{:S(2)}) copy-start(bf16[1,512,3584]{2,1,0:T(8,128)(2,1)} %param.13) | copy-start | bytes 11010052
  16.8 1.6 %collective-permute-start = (bf16[8,18,8,128]{3,2,1,0:T(8,128)(2,1)S(1)}, bf16[8,18,8,128]{3,2,1,0:T(8,128)(2,1)S(1)}, u32[]{:S(2)}, u32[]{:S(2)}) collective-permute-start(bf16[8,18,8,128]{3,2,1,0:T(8,128)(2,1)S(1)} %all_to_all.10.packed_ref), channel_id=1, source_target_pairs={{0,1},{1,0},{2,3},{3,2},{4,5},{5,4},{6,7},{7,6},{8,9},{9,8},{10,11... | collective-permute-start | bytes 884744 | tf_op jit(solution)/shard_map/ppermute | solution.py:357
  19.2 1.3 %collective-permute-start.1 = (bf16[80,512]{1,0:T(8,128)(2,1)S(1)}, bf16[80,512]{1,0:T(8,128)(2,1)S(1)}, u32[]{:S(2)}, u32[]{:S(2)}) collective-permute-start(bf16[80,512]{1,0:T(8,128)(2,1)S(1)} %shard_map.77.hidden_ref), channel_id=1, source_target_pairs={{0,1},{1,0},{2,3},{3,2},{4,5},{5,4},{6,7},{7,6},{8,9},{9,8},{10,11... | collective-permute-start | bytes 245768 | tf_op jit(solution)/shard_map/ppermute | solution.py:387
  19.9 7.5 %copy-start.6 = (f32[32,1]{0,1:T(1,128)S(1)}, f32[32,1]{0,1:T(1,128)}, u32[]{:S(2)}) copy-start(f32[32,1]{0,1:T(1,128)} %param.9) | copy-start | bytes 388
  21.8 13.1 %all-to-all-start.1 = ((bf16[8,18,8,128]{3,2,1,0:T(8,128)(2,1)}), bf16[8,18,8,128]{3,2,1,0:T(8,128)(2,1)S(1)}, u32[]{:S(2)}, u32[]{:S(2)}) async-start(bf16[8,18,8,128]{3,2,1,0:T(8,128)(2,1)} %shard_map.79), calls=%async_computation.1 | async-start | bytes 589824 | tf_op jit(solution)/shard_map/all_to_all | solution.py:62

commit v5 on v4

--- a/solution.py
+++ b/solution.py
@@ -9,7 +9,7 @@
 
 
 LANES = 128
-SUBLANES = 8
+TILE_ROWS = 4
 MIB = 1 << 20
 F32 = jnp.float32
 BF16 = jnp.bfloat16
@@ -24,19 +24,19 @@
         self.capacity = tok * choices * 5 // (4 * experts)
         assert feat % LANES == 0
         self.blocks = feat // LANES
-        self.full = self.capacity // SUBLANES
-        self.main = self.full * SUBLANES
+        self.full = self.capacity // TILE_ROWS
+        self.main = self.full * TILE_ROWS
         self.tail = self.capacity - self.main
-        self.group = SUBLANES // self.tail if self.tail else 0
+        self.group = TILE_ROWS // self.tail if self.tail else 0
         self.tail_tiles = -(-self.blocks // self.group) if self.tail else 0
         self.tiles = self.full * self.blocks + self.tail_tiles
         self.main_rows = slots * self.main
         self.tail_rows = slots * self.tail
         self.rows = self.main_rows + self.tail_rows
-        self.tail_wide = slots * SUBLANES if self.tail else 0
+        self.tail_wide = slots * TILE_ROWS if self.tail else 0
         self.wide = self.main_rows + self.tail_wide
         self.parts = max(1, self.group)
-        self.packed = (slots, self.tiles, SUBLANES, LANES)
+        self.packed = (slots, self.tiles, TILE_ROWS, LANES)
 
 
 def iota(shape, dim):
@@ -78,27 +78,24 @@
 def route(plan, member, slot_row, ids):
     slots, tok = plan.slots, plan.tok
     square = (slots, slots)
-    row = slot_row.astype(F32)
-    col = to_column(row)
-    same = jnp.where(col == row, 1.0, 0.0)
+    col = to_column(slot_row.astype(F32))
+    same = jnp.where(col == slot_row.astype(F32), 1.0, 0.0)
     copies = jnp.sum(same, axis=1, keepdims=True)
     rank = jnp.sum(jnp.where(iota(square, 1) < iota(square, 0), same, 0.0), axis=1, keepdims=True)
     want = jnp.zeros((slots, 1), F32)
     for number in (2, 3, 4):
         want = jnp.where(copies == number, lax.rem(member, number).astype(F32), want)
     chosen = rank == want
-    hits = [
-        jnp.where((ids[k : k + 1].astype(F32) == col) & chosen, 1.0, 0.0)
-        for k in range(plan.choices)
-    ]
-    before = jnp.where(iota((tok, tok), 0) < iota((tok, tok), 1), 1.0, 0.0).astype(BF16)
-    counts = jnp.dot(sum(hits).astype(BF16), before, preferred_element_type=F32)
     line = exchange_place(iota((slots, tok), 0), slots).astype(F32)
+    rows = [ids[k : k + 1].astype(F32) for k in range(plan.choices)]
+    cols = [to_column(row) for row in rows]
+    before = iota((tok, tok), 0) < iota((tok, tok), 1)
     found = []
-    for hit in hits:
-        slot = jnp.sum(hit * line, axis=0, keepdims=True).astype(jnp.int32)
-        place = jnp.sum(hit * counts, axis=0, keepdims=True).astype(jnp.int32)
-        found.append((slot, place))
+    for row in rows:
+        slot = jnp.sum(jnp.where((row == col) & chosen, line, 0.0), axis=0, keepdims=True)
+        earlier = sum(jnp.where((other == row) & before, 1.0, 0.0) for other in cols)
+        place = jnp.sum(earlier, axis=0, keepdims=True)
+        found.append((slot.astype(jnp.int32), place.astype(jnp.int32)))
     return found
 
 
@@ -107,7 +104,7 @@
 
 
 def tail_code(plan, slot, place, part):
-    spot = slot * SUBLANES + place - plan.main + part * plan.tail
+    spot = slot * TILE_ROWS + place - plan.main + part * plan.tail
     return jnp.where(place < plan.main, -1, spot)
 
 
@@ -134,7 +131,7 @@
         hot = sum(jnp.where(line == main_code(plan, *pair), 1.0, 0.0) for pair in found)
         main = jnp.dot(hot.astype(BF16), tokens_ref[...], preferred_element_type=F32)
         for block in range(plan.blocks):
-            tile = main[:, lane_block(block)].reshape(plan.slots, plan.full, SUBLANES, LANES)
+            tile = main[:, lane_block(block)].reshape(plan.slots, plan.full, TILE_ROWS, LANES)
             for index in range(plan.full):
                 send_ref[:, index * plan.blocks + block] = tile[:, index].astype(BF16)
     if plan.tail:
@@ -154,7 +151,7 @@
                     stack.append(jnp.zeros((plan.tok, LANES), BF16))
             tile = jnp.dot(hot, jnp.concatenate(stack, axis=0), preferred_element_type=F32)
             send_ref[:, plan.full * plan.blocks + index] = tile.reshape(
-                plan.slots, SUBLANES, LANES
+                plan.slots, TILE_ROWS, LANES
             ).astype(BF16)
 
 
@@ -181,15 +178,15 @@
                 rows_ref[0 : plan.main_rows, lane_block(block)] = flat_tile(tile)
             else:
                 for sender in range(plan.slots):
-                    first = sender * plan.main + index * SUBLANES
-                    rows_ref[first : first + SUBLANES, lane_block(block)] = tile[sender]
+                    first = sender * plan.main + index * TILE_ROWS
+                    rows_ref[first : first + TILE_ROWS, lane_block(block)] = tile[sender]
     if plan.tail:
         shape = (plan.group * plan.tail_rows, plan.tail_wide)
         line = iota(shape, 0)
         part = floor_div(line, plan.tail_rows)
         inner = line - part * plan.tail_rows
         sender = floor_div(inner, plan.tail)
-        spot = sender * SUBLANES + part * plan.tail + inner - sender * plan.tail
+        spot = sender * TILE_ROWS + part * plan.tail + inner - sender * plan.tail
         hot = jnp.where(spot == iota(shape, 1), 1.0, 0.0).astype(BF16)
         for index in range(plan.tail_tiles):
             tile = flat_tile(packed_ref[:, plan.full * plan.blocks + index])
@@ -218,13 +215,13 @@
 def emit_packed(plan, product, out_ref):
     for block in range(plan.blocks):
         tile = product[: plan.main_rows, lane_block(block)].reshape(
-            plan.slots, plan.full, SUBLANES, LANES
+            plan.slots, plan.full, TILE_ROWS, LANES
         )
         for index in range(plan.full):
             out_ref[:, index * plan.blocks + block] = tile[:, index].astype(out_ref.dtype)
     for index in range(plan.tail_tiles):
         spot = iota((plan.tail_wide, LANES), 0)
-        spot = spot - floor_div(spot, SUBLANES) * SUBLANES
+        spot = spot - floor_div(spot, TILE_ROWS) * TILE_ROWS
         tile = jnp.zeros((plan.tail_wide, LANES), F32)
         for part in range(plan.group):
             block = index * plan.group + part
@@ -232,7 +229,7 @@
                 here = (spot >= part * plan.tail) & (spot < (part + 1) * plan.tail)
                 tile = jnp.where(here, product[plan.main_rows :, lane_block(block)], tile)
         out_ref[:, plan.full * plan.blocks + index] = tile.reshape(
-            plan.slots, SUBLANES, LANES
+            plan.slots, TILE_ROWS, LANES
         ).astype(out_ref.dtype)
 
 
@@ -255,8 +252,8 @@
     if plan.tail:
         shape = (plan.tail_wide, plan.tail_rows)
         line, col = iota(shape, 0), iota(shape, 1)
-        sender = floor_div(line, SUBLANES)
-        spot = line - sender * SUBLANES
+        sender = floor_div(line, TILE_ROWS)
+        spot = line - sender * TILE_ROWS
         spot = spot - floor_div(spot, plan.tail) * plan.tail
         hot = jnp.where(sender * plan.tail + spot == col, 1.0, 0.0).astype(BF16)
         tail = jnp.dot(hot, hidden_ref[plan.main_rows :], preferred_element_type=F32)
@@ -329,7 +326,7 @@
     hid = weights[0].shape[1]
     gate_local, up_local, down_local = weights
     swap = [(0, 1), (1, 0)]
-    packed_bytes = 2 * slots * plan.tiles * SUBLANES * LANES
+    packed_bytes = 2 * slots * plan.tiles * TILE_ROWS * LANES
     half_flops = 4 * plan.rows * feat * hid
     rows_scratch = pltpu.VMEM((plan.rows, feat), BF16)
     packed = jax.ShapeDtypeStruct(plan.packed, BF16)
@@ -340,7 +337,7 @@
     warm = call(
         warm_kernel,
         [],
-        jax.ShapeDtypeStruct((SUBLANES, LANES), F32),
+        jax.ShapeDtypeStruct((TILE_ROWS, LANES), F32),
         COVER_FLOPS,
         COVER_BYTES,
         1 * MIB,

time: 36 us -> 35.6 us (0.989)
  no operation moved by 1% of the time
where the time goes in v5:
time: 35.6 us; the launch traced here: 35.3 us
  blocking collectives  15.2 us (43%)
  waiting for transfers between devices  8.46 us (24%)
  starting transfers between devices  6.46 us (18%)
  Pallas kernels  4.78 us (13%)
  local copies, waits for them, and re-layouts  0.36 us (1%)
    all_to_all x1, blocking collectives, exchange(): lax.all_to_all(array, 'ep', split_axis=0, concat_axis=0, tiled=True, axis...  15.2 us
    all_to_all x1, waiting for transfers between devices, exchange(): lax.all_to_all(array, 'ep', split_axis=0, concat_axis=0, tiled=True, axis...  7.12 us
    all_to_all x1, starting transfers between devices, exchange(): lax.all_to_all(array, 'ep', split_axis=0, concat_axis=0, tiled=True, axis...  5.69 us
    pallas_call x1, Pallas kernels, body(): call(functools.partial(down_other_kernel, plan), [VMEM] * 3, packed, 2 *...  1.24 us
    pallas_call x1, Pallas kernels, body(): call(functools.partial(combine_kernel, plan), [VMEM, VMEM, VMEM], jax.Sha...  0.86 us
    pallas_call x1, Pallas kernels, body(): call(functools.partial(other_kernel, plan), [VMEM] * 4, jax.ShapeDtypeStr...  0.84 us
    pallas_call x1, Pallas kernels, body(): call(functools.partial(own_kernel, plan), [VMEM] * 4, jax.ShapeDtypeStruc...  0.83 us
    ppermute x1, waiting for transfers between devices, body(): partner = lax.ppermute(arrived, 'rep', swap)  0.71 us
  transfers between devices with their start and end apart: 4, of which 3 were waited for; matrix products, arithmetic and copies ran while one was open for 0% of the time, Pallas kernels for 8%

profile of v5, /device:TPU:0, one launch (start us, length us, event | category | flops | bytes accessed | tf_op | source)
XLA Modules:
  0.0 35.3 jit_solution(5385316339591286781)
XLA Ops:
  0.0 0.0 copy-start.3
  0.0 0.0 copy-start.4
  0.0 0.0 copy-start.5
  0.0 0.6 %collective-permute-start.2 = (bf16[512,3584]{1,0:T(8,128)(2,1)}, bf16[512,3584]{1,0:T(8,128)(2,1)S(1)}, u32[]{:S(2)}, u32[]{:S(2)}) collective-permute-start(bf16[512,3584]{1,0:T(8,128)(2,1)} %bitcast.10), channel_id=1, source_target_pairs={{0,1},{1,0},{2,3},{3,2},{4,5},{5,4},{6,7},{7,6},{8,9},{9,8},{10,11... | collective-permute-start | bytes 11010056 | tf_op jit(solution)/shard_map/ppermute | solution.py:336
  0.6 0.3 copy-done.3
  0.9 0.0 copy-done.4
  0.9 0.0 copy-done.5
  0.9 0.0 copy-start
  0.9 0.0 copy-start.1
  0.9 0.0 copy-start.2
  0.9 0.4 %shard_map.74 = (bf16[8,35,4,128]{3,2,1,0:T(4,128)(2,1)S(1)}, s32[2,32]{1,0:T(2,128)S(1)}) custom-call(f32[4,128]{1,0:T(4,128)S(1)} %shard_map.73.warm_ref, s32[1,8]{1,0:T(1,128)S(1)} %bitcast.13, s32[1,32]{1,0:T(1,128)S(1)} %bitcast.14, bf16[32,1792]{1,0:T(8,128)(2,1)S(1)} %copy-done.3), custom_call_target="tpu_custom_call" | custom-call | flops 17179869184 | bytes 33554432 | tf_op jit(solution)/shard_map/pallas_call | solution.py:345
  1.3 15.2 %all_to_all.10.packed_ref = bf16[8,35,4,128]{3,2,1,0:T(4,128)(2,1)S(1)} all-to-all(bf16[8,35,4,128]{3,2,1,0:T(4,128)(2,1)S(1)} %get-tuple-element.12), channel_id=1, replica_groups={{10,8,12,6,14,4,0,2},{11,9,13,7,15,5,1,3},{26,24,28,22,30,20,16,18},{27..., dimensions={0} | all-to-all | bytes 573440 | tf_op jit(solution)/shard_map/all_to_all | solution.py:62
  16.6 0.0 collective-permute-start
  16.6 0.0 copy-done
  16.6 0.0 copy-done.1
  16.6 0.0 copy-done.2
  16.6 0.8 %shard_map.76.acc_ref = f32[80,1024]{1,0:T(8,128)S(1)} custom-call(bf16[8,35,4,128]{3,2,1,0:T(4,128)(2,1)S(1)} %all_to_all.10.packed_ref, bf16[3584,512]{1,0:T(8,128)(2,1)S(1)} %bitcast.6, bf16[3584,512]{1,0:T(8,128)(2,1)S(1)} %bitcast.8, bf16[512,3584]{1,0:T(8,128)(2,1)S(1)} %bitcast.11), custom_call_target="tpu_custom_call" | custom-call | flops 1024 | bytes 1024 | tf_op jit(solution)/shard_map/pallas_call | solution.py:355
  17.4 0.7 %collective-permute-done.packed_ref = bf16[8,35,4,128]{3,2,1,0:T(4,128)(2,1)S(1)} collective-permute-done((bf16[8,35,4,128]{3,2,1,0:T(4,128)(2,1)S(1)}, bf16[8,35,4,128]{3,2,1,0:T(4,128)(2,1)S(1)}, u32[]{:S(2)}, u32[]{:S(2)}) %collective-permute-start) | collective-permute-done | bytes 286752 | tf_op jit(solution)/shard_map/ppermute | solution.py:354
  18.1 0.8 %shard_map.77.hidden_ref = bf16[80,512]{1,0:T(8,128)(2,1)S(1)} custom-call(bf16[8,35,4,128]{3,2,1,0:T(4,128)(2,1)S(1)} %collective-permute-done.packed_ref, f32[80,1024]{1,0:T(8,128)S(1)} %shard_map.76.acc_ref, bf16[3584,512]{1,0:T(8,128)(2,1)S(1)} %bitcast.7, bf16[3584,512]{1,0:T(8,128)(2,1)S(1)} %bitcast.9), custom_call_target="tpu_custom_call" | custom-call | flops 293601280 | bytes 614400 | tf_op jit(solution)/shard_map/pallas_call | solution.py:375
  19.0 0.2 collective-permute-start.1
  19.2 0.5 %shard_map.78.mine_ref = f32[96,1792]{1,0:T(8,128)S(1)} custom-call(bf16[80,512]{1,0:T(8,128)(2,1)S(1)} %shard_map.77.hidden_ref, bf16[512,3584]{1,0:T(8,128)(2,1)S(1)} %bitcast.12), custom_call_target="tpu_custom_call" | custom-call | flops 176160768 | bytes 573440 | tf_op jit(solution)/shard_map/pallas_call | solution.py:385
  19.7 0.0 copy-start.6
  19.7 0.6 %collective-permute-done.1.hidden_ref = bf16[80,512]{1,0:T(8,128)(2,1)S(1)} collective-permute-done((bf16[80,512]{1,0:T(8,128)(2,1)S(1)}, bf16[80,512]{1,0:T(8,128)(2,1)S(1)}, u32[]{:S(2)}, u32[]{:S(2)}) %collective-permute-start.1) | collective-permute-done | bytes 81952 | tf_op jit(solution)/shard_map/ppermute | solution.py:384
  20.3 0.0 collective-permute-done.2.down_ref
  20.3 1.2 %shard_map.79 = bf16[8,35,4,128]{3,2,1,0:T(4,128)(2,1)} custom-call(bf16[80,512]{1,0:T(8,128)(2,1)S(1)} %collective-permute-done.1.hidden_ref, bf16[512,3584]{1,0:T(8,128)(2,1)S(1)} %collective-permute-done.2.down_ref, f32[96,1792]{1,0:T(8,128)S(1)} %shard_map.78.mine_ref), custom_call_target="tpu_custom_call" | custom-call | flops 176160768 | bytes 573440 | tf_op jit(solution)/shard_map/pallas_call | solution.py:393
  21.6 5.7 %all-to-all-start.1 = ((bf16[8,35,4,128]{3,2,1,0:T(4,128)(2,1)}), bf16[8,35,4,128]{3,2,1,0:T(4,128)(2,1)S(1)}, u32[]{:S(2)}, u32[]{:S(2)}) async-start(bf16[8,35,4,128]{3,2,1,0:T(4,128)(2,1)} %shard_map.79), calls=%async_computation.1 | async-start | bytes 573440 | tf_op jit(solution)/shard_map/all_to_all | solution.py:62
  27.3 0.0 copy-done.6
  27.3 0.1 shard_map.75
  27.4 7.1 %all-to-all-done.1.packed_ref = bf16[8,35,4,128]{3,2,1,0:T(4,128)(2,1)S(1)} async-done(((bf16[8,35,4,128]{3,2,1,0:T(4,128)(2,1)}), bf16[8,35,4,128]{3,2,1,0:T(4,128)(2,1)S(1)}, u32[]{:S(2)}, u32[]{:S(2)}) %all-to-all-start.1) | async-done | bytes 286752 | tf_op jit(solution)/shard_map/all_to_all | solution.py:62
  34.5 0.9 %shard_map.80 = bf16[32,1792]{1,0:T(8,128)(2,1)} custom-call(bf16[2,32,96]{2,1,0:T(8,128)(2,1)S(1)} %get-tuple-element.10.pick_ref, f32[32,1]{1,0:T(8,128)S(1)} %get-tuple-element.11.column_ref, bf16[8,35,4,128]{3,2,1,0:T(4,128)(2,1)S(1)} %all-to-all-done.1.packed_ref), custom_call_target="tpu_custom_call" | custom-call | flops 11010048 | bytes 573440 | tf_op jit(solution)/shard_map/pallas_call | solution.py:402
  (1 shorter events, 0.0 us)
Async XLA Ops:
  0.0 0.9 %copy-start.3 = (bf16[32,1792]{1,0:T(8,128)(2,1)S(1)}, bf16[32,1792]{1,0:T(8,128)(2,1)}, u32[]{:S(2)}) copy-start(bf16[32,1792]{1,0:T(8,128)(2,1)} %tokens_ref.1) | copy-start | bytes 344068
  0.0 0.9 %copy-start.4 = (s32[8]{0:T(128)S(1)}, s32[8]{0:T(128)}, u32[]{:S(2)}) copy-start(s32[8]{0:T(128)} %param.10) | copy-start | bytes 100
  0.0 0.9 %copy-start.5 = (s32[32,1]{0,1:T(1,128)S(1)}, s32[32,1]{0,1:T(1,128)}, u32[]{:S(2)}) copy-start(s32[32,1]{0,1:T(1,128)} %param.8) | copy-start | bytes 388
  0.0 20.3 %collective-permute-start.2 = (bf16[512,3584]{1,0:T(8,128)(2,1)}, bf16[512,3584]{1,0:T(8,128)(2,1)S(1)}, u32[]{:S(2)}, u32[]{:S(2)}) collective-permute-start(bf16[512,3584]{1,0:T(8,128)(2,1)} %bitcast.10), channel_id=1, source_target_pairs={{0,1},{1,0},{2,3},{3,2},{4,5},{5,4},{6,7},{7,6},{8,9},{9,8},{10,11... | collective-permute-start | bytes 11010056 | tf_op jit(solution)/shard_map/ppermute | solution.py:336
  0.9 15.7 %copy-start = (bf16[1,3584,512]{2,1,0:T(8,128)(2,1)S(1)}, bf16[1,3584,512]{2,1,0:T(8,128)(2,1)}, u32[]{:S(2)}) copy-start(bf16[1,3584,512]{2,1,0:T(8,128)(2,1)} %param.11) | copy-start | bytes 11010052
  0.9 15.7 %copy-start.1 = (bf16[1,3584,512]{2,1,0:T(8,128)(2,1)S(1)}, bf16[1,3584,512]{2,1,0:T(8,128)(2,1)}, u32[]{:S(2)}) copy-start(bf16[1,3584,512]{2,1,0:T(8,128)(2,1)} %param.12) | copy-start | bytes 11010052
  0.9 15.7 %copy-start.2 = (bf16[1,512,3584]{2,1,0:T(8,128)(2,1)S(1)}, bf16[1,512,3584]{2,1,0:T(8,128)(2,1)}, u32[]{:S(2)}) copy-start(bf16[1,512,3584]{2,1,0:T(8,128)(2,1)} %param.13) | copy-start | bytes 11010052
  16.6 1.6 %collective-permute-start = (bf16[8,35,4,128]{3,2,1,0:T(4,128)(2,1)S(1)}, bf16[8,35,4,128]{3,2,1,0:T(4,128)(2,1)S(1)}, u32[]{:S(2)}, u32[]{:S(2)}) collective-permute-start(bf16[8,35,4,128]{3,2,1,0:T(4,128)(2,1)S(1)} %all_to_all.10.packed_ref), channel_id=1, source_target_pairs={{0,1},{1,0},{2,3},{3,2},{4,5},{5,4},{6,7},{7,6},{8,9},{9,8},{10,11... | collective-permute-start | bytes 860168 | tf_op jit(solution)/shard_map/ppermute | solution.py:354
  19.0 1.3 %collective-permute-start.1 = (bf16[80,512]{1,0:T(8,128)(2,1)S(1)}, bf16[80,512]{1,0:T(8,128)(2,1)S(1)}, u32[]{:S(2)}, u32[]{:S(2)}) collective-permute-start(bf16[80,512]{1,0:T(8,128)(2,1)S(1)} %shard_map.77.hidden_ref), channel_id=1, source_target_pairs={{0,1},{1,0},{2,3},{3,2},{4,5},{5,4},{6,7},{7,6},{8,9},{9,8},{10,11... | collective-permute-start | bytes 245768 | tf_op jit(solution)/shard_map/ppermute | solution.py:384
  19.7 7.6 %copy-start.6 = (f32[32,1]{0,1:T(1,128)S(1)}, f32[32,1]{0,1:T(1,128)}, u32[]{:S(2)}) copy-start(f32[32,1]{0,1:T(1,128)} %param.9) | copy-start | bytes 388
  21.6 12.9 %all-to-all-start.1 = ((bf16[8,35,4,128]{3,2,1,0:T(4,128)(2,1)}), bf16[8,35,4,128]{3,2,1,0:T(4,128)(2,1)S(1)}, u32[]{:S(2)}, u32[]{:S(2)}) async-start(bf16[8,35,4,128]{3,2,1,0:T(4,128)(2,1)} %shard_map.79), calls=%async_computation.1 | async-start | bytes 573440 | tf_op jit(solution)/shard_map/all_to_all | solution.py:62

commit v6 on v5

--- a/solution.py
+++ b/solution.py
@@ -103,6 +103,12 @@
     return jnp.where(place < plan.main, slot * plan.main + place, -1)
 
 
+def table_code(plan, slot, place, part):
+    tile = sum((place >= (index + 1) * TILE_ROWS).astype(jnp.int32) for index in range(plan.full))
+    inner = place - tile * TILE_ROWS + jnp.where(tile == plan.full, part * plan.tail, 0)
+    return (tile * plan.slots + slot) * TILE_ROWS + inner
+
+
 def tail_code(plan, slot, place, part):
     spot = slot * TILE_ROWS + place - plan.main + part * plan.tail
     return jnp.where(place < plan.main, -1, spot)
@@ -121,11 +127,15 @@
     return list(zip(lines[: plan.choices], lines[plan.choices :], strict=True))
 
 
-def pack_kernel(plan, warm_ref, slot_ref, ids_ref, tokens_ref, send_ref, found_ref):
+def route_kernel(plan, warm_ref, slot_ref, ids_ref, found_ref):
     found = route(plan, lax.axis_index("ep"), slot_ref[...], ids_ref[...])
     for k, (slot, place) in enumerate(found):
         found_ref[k : k + 1] = slot
         found_ref[plan.choices + k : plan.choices + k + 1] = place
+
+
+def pack_kernel(plan, found_ref, tokens_ref, send_ref):
+    found = read_found(plan, found_ref)
     if plan.full:
         line = iota((plan.main_rows, plan.tok), 0)
         hot = sum(jnp.where(line == main_code(plan, *pair), 1.0, 0.0) for pair in found)
@@ -160,14 +170,13 @@
     for k, (slot, place) in enumerate(read_found(plan, found_ref)):
         column_ref[:, k : k + 1] = to_column(gates_ref[k : k + 1])
         for part in range(plan.parts):
-            tail = plan.main_rows + tail_code(plan, slot, place, part)
-            code = jnp.where(place < plan.main, main_code(plan, slot, place), tail)
+            code = table_code(plan, slot, place, part)
             pick = jnp.where(to_column(code.astype(F32)) == lane, 1.0, 0.0)
             pick_ref[k * plan.parts + part] = pick.astype(BF16)
 
 
 def flat_tile(tile):
-    return tile.astype(F32).reshape(-1, LANES).astype(BF16)
+    return tile.reshape(-1, LANES)
 
 
 def unpack_rows(plan, packed_ref, rows_ref):
@@ -275,29 +284,21 @@
 
 
 def combine_kernel(plan, pick_ref, column_ref, packed_ref, out_ref):
-    for block in range(plan.blocks):
-        stack = []
-        if plan.full == 1:
-            stack.append(packed_ref[:, block].astype(F32).reshape(plan.main_rows, LANES))
-        elif plan.full:
-            tiles = [
-                packed_ref[:, index * plan.blocks + block].astype(F32)[:, None]
-                for index in range(plan.full)
-            ]
-            stack.append(jnp.concatenate(tiles, axis=1).reshape(plan.main_rows, LANES))
-        part = 0
-        if plan.tail:
-            index, part = divmod(block, plan.group)
-            tile = packed_ref[:, plan.full * plan.blocks + index]
-            stack.append(tile.astype(F32).reshape(plan.tail_wide, LANES))
-        table = jnp.concatenate(stack, axis=0).astype(BF16)
-        total = jnp.zeros((plan.tok, LANES), F32)
+    for part in range(plan.parts):
+        blocks = range(part, plan.blocks, plan.parts)
+        tables = []
+        for block in blocks:
+            tiles = [index * plan.blocks + block for index in range(plan.full)]
+            if plan.tail:
+                tiles.append(plan.full * plan.blocks + block // plan.group)
+            tables.append(jnp.concatenate([flat_tile(packed_ref[:, tile]) for tile in tiles], axis=0))
+        table = jnp.concatenate(tables, axis=1)
+        total = jnp.zeros((plan.tok, table.shape[1]), F32)
         for k in range(plan.choices):
-            picked = jnp.dot(
-                pick_ref[k * plan.parts + part], table, preferred_element_type=F32
-            )
+            picked = jnp.dot(pick_ref[k * plan.parts + part], table, preferred_element_type=F32)
             total = total + column_ref[:, k : k + 1] * picked
-        out_ref[:, lane_block(block)] = total.astype(BF16)
+        for index, block in enumerate(blocks):
+            out_ref[:, lane_block(block)] = total[:, lane_block(index)].astype(BF16)
 
 
 VMEM = pl.BlockSpec(memory_space=pltpu.VMEM)
@@ -342,14 +343,17 @@
         COVER_BYTES,
         1 * MIB,
     )()
-    send, found = call(
-        functools.partial(pack_kernel, plan),
-        [VMEM] * 4,
-        [packed, jax.ShapeDtypeStruct((2 * choices, tok), jnp.int32)],
-        COVER_FLOPS,
-        COVER_BYTES,
-        8 * MIB,
-    )(warm, slot_row, ids, tokens)
+    found = call(
+        functools.partial(route_kernel, plan),
+        [VMEM] * 3,
+        jax.ShapeDtypeStruct((2 * choices, tok), jnp.int32),
+        1 << 10,
+        1 << 10,
+        4 * MIB,
+    )(warm, slot_row, ids)
+    send = call(
+        functools.partial(pack_kernel, plan), [VMEM] * 2, packed, COVER_FLOPS, COVER_BYTES, 8 * MIB
+    )(found, tokens)
     arrived = exchange(send, slots)
     partner = lax.ppermute(arrived, "rep", swap)
     acc = call(

time: 35.6 us -> 35.4 us (level)
  no operation moved by 1% of the time
where the time goes in v6:
time: 35.4 us; the launch traced here: 35.2 us
  blocking collectives  15.3 us (43%)
  waiting for transfers between devices  8.46 us (24%)
  starting transfers between devices  6.46 us (18%)
  Pallas kernels  4.77 us (13%)
    all_to_all x1, blocking collectives, exchange(): lax.all_to_all(array, 'ep', split_axis=0, concat_axis=0, tiled=True, axis...  15.3 us
    all_to_all x1, waiting for transfers between devices, exchange(): lax.all_to_all(array, 'ep', split_axis=0, concat_axis=0, tiled=True, axis...  7.12 us
    all_to_all x1, starting transfers between devices, exchange(): lax.all_to_all(array, 'ep', split_axis=0, concat_axis=0, tiled=True, axis...  5.69 us
    pallas_call x1, Pallas kernels, body(): call(functools.partial(down_other_kernel, plan), [VMEM] * 3, packed, 2 *...  1.25 us
    pallas_call x1, Pallas kernels, body(): call(functools.partial(combine_kernel, plan), [VMEM, VMEM, VMEM], jax.Sha...  0.85 us
    pallas_call x1, Pallas kernels, body(): call(functools.partial(other_kernel, plan), [VMEM] * 4, jax.ShapeDtypeStr...  0.84 us
    pallas_call x1, Pallas kernels, body(): call(functools.partial(own_kernel, plan), [VMEM] * 4, jax.ShapeDtypeStruc...  0.83 us
    ppermute x1, waiting for transfers between devices, body(): partner = lax.ppermute(arrived, 'rep', swap)  0.72 us
  transfers between devices with their start and end apart: 4, of which 3 were waited for; matrix products, arithmetic and copies ran while one was open for 0% of the time, Pallas kernels for 8%

profile of v6, /device:TPU:0, one launch (start us, length us, event | category | flops | bytes accessed | tf_op | source)
XLA Modules:
  0.0 35.2 jit_solution(9751609040512383517)
XLA Ops:
  0.0 0.0 copy-start.3
  0.0 0.0 copy-start.4
  0.0 0.0 copy-start.5
  0.0 0.6 %collective-permute-start.2 = (bf16[512,3584]{1,0:T(8,128)(2,1)}, bf16[512,3584]{1,0:T(8,128)(2,1)S(1)}, u32[]{:S(2)}, u32[]{:S(2)}) collective-permute-start(bf16[512,3584]{1,0:T(8,128)(2,1)} %bitcast.10), channel_id=1, source_target_pairs={{0,1},{1,0},{2,3},{3,2},{4,5},{5,4},{6,7},{7,6},{8,9},{9,8},{10,11... | collective-permute-start | bytes 11010056 | tf_op jit(solution)/shard_map/ppermute | solution.py:337
  0.6 0.1 copy-done.3
  0.7 0.0 copy-done.4
  0.7 0.2 shard_map.74.found_ref
  0.8 0.1 copy-done.5
  0.9 0.0 copy-start
  0.9 0.0 copy-start.1
  0.9 0.0 copy-start.2
  0.9 0.2 shard_map.76
  1.2 15.3 %all_to_all.10.packed_ref = bf16[8,35,4,128]{3,2,1,0:T(4,128)(2,1)S(1)} all-to-all(bf16[8,35,4,128]{3,2,1,0:T(4,128)(2,1)S(1)} %shard_map.76), channel_id=1, replica_groups={{10,8,12,6,14,4,0,2},{11,9,13,7,15,5,1,3},{26,24,28,22,30,20,16,18},{27..., dimensions={0} | all-to-all | bytes 573440 | tf_op jit(solution)/shard_map/all_to_all | solution.py:62
  16.4 0.0 collective-permute-start
  16.4 0.0 copy-done
  16.4 0.0 copy-done.1
  16.4 0.0 copy-done.2
  16.5 0.8 %shard_map.77.acc_ref = f32[80,1024]{1,0:T(8,128)S(1)} custom-call(bf16[8,35,4,128]{3,2,1,0:T(4,128)(2,1)S(1)} %all_to_all.10.packed_ref, bf16[3584,512]{1,0:T(8,128)(2,1)S(1)} %bitcast.6, bf16[3584,512]{1,0:T(8,128)(2,1)S(1)} %bitcast.8, bf16[512,3584]{1,0:T(8,128)(2,1)S(1)} %bitcast.11), custom_call_target="tpu_custom_call" | custom-call | flops 1024 | bytes 1024 | tf_op jit(solution)/shard_map/pallas_call | solution.py:359
  17.3 0.7 %collective-permute-done.packed_ref = bf16[8,35,4,128]{3,2,1,0:T(4,128)(2,1)S(1)} collective-permute-done((bf16[8,35,4,128]{3,2,1,0:T(4,128)(2,1)S(1)}, bf16[8,35,4,128]{3,2,1,0:T(4,128)(2,1)S(1)}, u32[]{:S(2)}, u32[]{:S(2)}) %collective-permute-start) | collective-permute-done | bytes 286752 | tf_op jit(solution)/shard_map/ppermute | solution.py:358
  18.0 0.8 %shard_map.78.hidden_ref = bf16[80,512]{1,0:T(8,128)(2,1)S(1)} custom-call(bf16[8,35,4,128]{3,2,1,0:T(4,128)(2,1)S(1)} %collective-permute-done.packed_ref, f32[80,1024]{1,0:T(8,128)S(1)} %shard_map.77.acc_ref, bf16[3584,512]{1,0:T(8,128)(2,1)S(1)} %bitcast.7, bf16[3584,512]{1,0:T(8,128)(2,1)S(1)} %bitcast.9), custom_call_target="tpu_custom_call" | custom-call | flops 293601280 | bytes 614400 | tf_op jit(solution)/shard_map/pallas_call | solution.py:379
  18.8 0.2 collective-permute-start.1
  19.0 0.5 %shard_map.79.mine_ref = f32[96,1792]{1,0:T(8,128)S(1)} custom-call(bf16[80,512]{1,0:T(8,128)(2,1)S(1)} %shard_map.78.hidden_ref, bf16[512,3584]{1,0:T(8,128)(2,1)S(1)} %bitcast.12), custom_call_target="tpu_custom_call" | custom-call | flops 176160768 | bytes 573440 | tf_op jit(solution)/shard_map/pallas_call | solution.py:389
  19.6 0.0 copy-start.6
  19.6 0.6 %collective-permute-done.1.hidden_ref = bf16[80,512]{1,0:T(8,128)(2,1)S(1)} collective-permute-done((bf16[80,512]{1,0:T(8,128)(2,1)S(1)}, bf16[80,512]{1,0:T(8,128)(2,1)S(1)}, u32[]{:S(2)}, u32[]{:S(2)}) %collective-permute-start.1) | collective-permute-done | bytes 81952 | tf_op jit(solution)/shard_map/ppermute | solution.py:388
  20.2 0.0 collective-permute-done.2.down_ref
  20.2 1.3 %shard_map.80 = bf16[8,35,4,128]{3,2,1,0:T(4,128)(2,1)} custom-call(bf16[80,512]{1,0:T(8,128)(2,1)S(1)} %collective-permute-done.1.hidden_ref, bf16[512,3584]{1,0:T(8,128)(2,1)S(1)} %collective-permute-done.2.down_ref, f32[96,1792]{1,0:T(8,128)S(1)} %shard_map.79.mine_ref), custom_call_target="tpu_custom_call" | custom-call | flops 176160768 | bytes 573440 | tf_op jit(solution)/shard_map/pallas_call | solution.py:397
  21.4 5.7 %all-to-all-start.1 = ((bf16[8,35,4,128]{3,2,1,0:T(4,128)(2,1)}), bf16[8,35,4,128]{3,2,1,0:T(4,128)(2,1)S(1)}, u32[]{:S(2)}, u32[]{:S(2)}) async-start(bf16[8,35,4,128]{3,2,1,0:T(4,128)(2,1)} %shard_map.80), calls=%async_computation.1 | async-start | bytes 573440 | tf_op jit(solution)/shard_map/all_to_all | solution.py:62
  27.1 0.0 copy-done.6
  27.1 0.1 shard_map.75
  27.2 7.1 %all-to-all-done.1.packed_ref = bf16[8,35,4,128]{3,2,1,0:T(4,128)(2,1)S(1)} async-done(((bf16[8,35,4,128]{3,2,1,0:T(4,128)(2,1)}), bf16[8,35,4,128]{3,2,1,0:T(4,128)(2,1)S(1)}, u32[]{:S(2)}, u32[]{:S(2)}) %all-to-all-start.1) | async-done | bytes 286752 | tf_op jit(solution)/shard_map/all_to_all | solution.py:62
  34.4 0.8 %shard_map.81 = bf16[32,1792]{1,0:T(8,128)(2,1)} custom-call(bf16[2,32,96]{2,1,0:T(8,128)(2,1)S(1)} %get-tuple-element.7.pick_ref, f32[32,1]{1,0:T(8,128)S(1)} %get-tuple-element.8.column_ref, bf16[8,35,4,128]{3,2,1,0:T(4,128)(2,1)S(1)} %all-to-all-done.1.packed_ref), custom_call_target="tpu_custom_call" | custom-call | flops 11010048 | bytes 573440 | tf_op jit(solution)/shard_map/pallas_call | solution.py:406
  (1 shorter events, 0.0 us)
Async XLA Ops:
  0.0 0.7 %copy-start.3 = (s32[8]{0:T(128)S(1)}, s32[8]{0:T(128)}, u32[]{:S(2)}) copy-start(s32[8]{0:T(128)} %param.10) | copy-start | bytes 100
  0.0 0.7 %copy-start.4 = (s32[32,1]{0,1:T(1,128)S(1)}, s32[32,1]{0,1:T(1,128)}, u32[]{:S(2)}) copy-start(s32[32,1]{0,1:T(1,128)} %param.8) | copy-start | bytes 388
  0.0 0.9 %copy-start.5 = (bf16[32,1792]{1,0:T(8,128)(2,1)S(1)}, bf16[32,1792]{1,0:T(8,128)(2,1)}, u32[]{:S(2)}) copy-start(bf16[32,1792]{1,0:T(8,128)(2,1)} %tokens_ref.1) | copy-start | bytes 344068
  0.0 20.2 %collective-permute-start.2 = (bf16[512,3584]{1,0:T(8,128)(2,1)}, bf16[512,3584]{1,0:T(8,128)(2,1)S(1)}, u32[]{:S(2)}, u32[]{:S(2)}) collective-permute-start(bf16[512,3584]{1,0:T(8,128)(2,1)} %bitcast.10), channel_id=1, source_target_pairs={{0,1},{1,0},{2,3},{3,2},{4,5},{5,4},{6,7},{7,6},{8,9},{9,8},{10,11... | collective-permute-start | bytes 11010056 | tf_op jit(solution)/shard_map/ppermute | solution.py:337
  0.9 15.5 %copy-start = (bf16[1,3584,512]{2,1,0:T(8,128)(2,1)S(1)}, bf16[1,3584,512]{2,1,0:T(8,128)(2,1)}, u32[]{:S(2)}) copy-start(bf16[1,3584,512]{2,1,0:T(8,128)(2,1)} %param.11) | copy-start | bytes 11010052
  0.9 15.5 %copy-start.1 = (bf16[1,3584,512]{2,1,0:T(8,128)(2,1)S(1)}, bf16[1,3584,512]{2,1,0:T(8,128)(2,1)}, u32[]{:S(2)}) copy-start(bf16[1,3584,512]{2,1,0:T(8,128)(2,1)} %param.12) | copy-start | bytes 11010052
  0.9 15.5 %copy-start.2 = (bf16[1,512,3584]{2,1,0:T(8,128)(2,1)S(1)}, bf16[1,512,3584]{2,1,0:T(8,128)(2,1)}, u32[]{:S(2)}) copy-start(bf16[1,512,3584]{2,1,0:T(8,128)(2,1)} %param.13) | copy-start | bytes 11010052
  16.4 1.6 %collective-permute-start = (bf16[8,35,4,128]{3,2,1,0:T(4,128)(2,1)S(1)}, bf16[8,35,4,128]{3,2,1,0:T(4,128)(2,1)S(1)}, u32[]{:S(2)}, u32[]{:S(2)}) collective-permute-start(bf16[8,35,4,128]{3,2,1,0:T(4,128)(2,1)S(1)} %all_to_all.10.packed_ref), channel_id=1, source_target_pairs={{0,1},{1,0},{2,3},{3,2},{4,5},{5,4},{6,7},{7,6},{8,9},{9,8},{10,11... | collective-permute-start | bytes 860168 | tf_op jit(solution)/shard_map/ppermute | solution.py:358
  18.8 1.3 %collective-permute-start.1 = (bf16[80,512]{1,0:T(8,128)(2,1)S(1)}, bf16[80,512]{1,0:T(8,128)(2,1)S(1)}, u32[]{:S(2)}, u32[]{:S(2)}) collective-permute-start(bf16[80,512]{1,0:T(8,128)(2,1)S(1)} %shard_map.78.hidden_ref), channel_id=1, source_target_pairs={{0,1},{1,0},{2,3},{3,2},{4,5},{5,4},{6,7},{7,6},{8,9},{9,8},{10,11... | collective-permute-start | bytes 245768 | tf_op jit(solution)/shard_map/ppermute | solution.py:388
  19.6 7.6 %copy-start.6 = (f32[32,1]{0,1:T(1,128)S(1)}, f32[32,1]{0,1:T(1,128)}, u32[]{:S(2)}) copy-start(f32[32,1]{0,1:T(1,128)} %param.9) | copy-start | bytes 388
  21.4 12.9 %all-to-all-start.1 = ((bf16[8,35,4,128]{3,2,1,0:T(4,128)(2,1)}), bf16[8,35,4,128]{3,2,1,0:T(4,128)(2,1)S(1)}, u32[]{:S(2)}, u32[]{:S(2)}) async-start(bf16[8,35,4,128]{3,2,1,0:T(4,128)(2,1)} %shard_map.80), calls=%async_computation.1 | async-start | bytes 573440 | tf_op jit(solution)/shard_map/all_to_all | solution.py:62

commit v7 on v6

--- a/solution.py
+++ b/solution.py
@@ -229,17 +229,16 @@
         for index in range(plan.full):
             out_ref[:, index * plan.blocks + block] = tile[:, index].astype(out_ref.dtype)
     for index in range(plan.tail_tiles):
-        spot = iota((plan.tail_wide, LANES), 0)
-        spot = spot - floor_div(spot, TILE_ROWS) * TILE_ROWS
-        tile = jnp.zeros((plan.tail_wide, LANES), F32)
+        parts = []
         for part in range(plan.group):
             block = index * plan.group + part
             if block < plan.blocks:
-                here = (spot >= part * plan.tail) & (spot < (part + 1) * plan.tail)
-                tile = jnp.where(here, product[plan.main_rows :, lane_block(block)], tile)
-        out_ref[:, plan.full * plan.blocks + index] = tile.reshape(
-            plan.slots, TILE_ROWS, LANES
-        ).astype(out_ref.dtype)
+                piece = product[plan.main_rows :, lane_block(block)]
+                parts.append(piece.reshape(plan.slots, plan.tail, LANES))
+        while len(parts) * plan.tail < TILE_ROWS:
+            parts.append(jnp.zeros((plan.slots, min(plan.tail, TILE_ROWS - len(parts) * plan.tail), LANES), F32))
+        tile = jnp.concatenate(parts, axis=1)
+        out_ref[:, plan.full * plan.blocks + index] = tile.astype(out_ref.dtype)
 
 
 def other_kernel(plan, packed_ref, acc_ref, gate_ref, up_ref, hidden_ref, rows_ref):
@@ -257,21 +256,9 @@
 
 
 def down_product(plan, hidden_ref, down_ref):
-    rows = [hidden_ref[: plan.main_rows]] if plan.full else []
-    if plan.tail:
-        shape = (plan.tail_wide, plan.tail_rows)
-        line, col = iota(shape, 0), iota(shape, 1)
-        sender = floor_div(line, TILE_ROWS)
-        spot = line - sender * TILE_ROWS
-        spot = spot - floor_div(spot, plan.tail) * plan.tail
-        hot = jnp.where(sender * plan.tail + spot == col, 1.0, 0.0).astype(BF16)
-        tail = jnp.dot(hot, hidden_ref[plan.main_rows :], preferred_element_type=F32)
-        rows.append(tail.astype(BF16))
     first = pl.multiple_of(lax.axis_index("rep") * plan.feat, LANES)
     return jnp.dot(
-        jnp.concatenate(rows, axis=0),
-        down_ref[:, pl.ds(first, plan.feat)],
-        preferred_element_type=F32,
+        hidden_ref[...], down_ref[:, pl.ds(first, plan.feat)], preferred_element_type=F32
     )
 
 
@@ -389,7 +376,7 @@
     mine = call(
         functools.partial(down_own_kernel, plan),
         [VMEM] * 2,
-        jax.ShapeDtypeStruct((plan.wide, feat), F32),
+        jax.ShapeDtypeStruct((plan.rows, feat), F32),
         2 * plan.wide * hid * feat,
         2 * packed_bytes,
         8 * MIB,

time: 35.4 us -> 35.4 us (level)
  transfers between devices with their start and end apart: 4 -> 4, of which waited for: 3 -> 3; matrix products, arithmetic and copies ran while one was open for 0% -> 0% of each run, Pallas kernels for 8% -> 7%
where the time goes in v7:
time: 35.4 us; the launch traced here: 35.2 us
  blocking collectives  15.3 us (43%)
  waiting for transfers between devices  8.54 us (24%)
  starting transfers between devices  6.46 us (18%)
  Pallas kernels  4.64 us (13%)
    all_to_all x1, blocking collectives, exchange(): lax.all_to_all(array, 'ep', split_axis=0, concat_axis=0, tiled=True, axis...  15.3 us
    all_to_all x1, waiting for transfers between devices, exchange(): lax.all_to_all(array, 'ep', split_axis=0, concat_axis=0, tiled=True, axis...  7.13 us
    all_to_all x1, starting transfers between devices, exchange(): lax.all_to_all(array, 'ep', split_axis=0, concat_axis=0, tiled=True, axis...  5.69 us
    pallas_call x1, Pallas kernels, body(): call(functools.partial(down_other_kernel, plan), [VMEM] * 3, packed, 2 *...  1.19 us
    pallas_call x1, Pallas kernels, body(): call(functools.partial(combine_kernel, plan), [VMEM, VMEM, VMEM], jax.Sha...  0.85 us
    pallas_call x1, Pallas kernels, body(): call(functools.partial(other_kernel, plan), [VMEM] * 4, jax.ShapeDtypeStr...  0.84 us
    pallas_call x1, Pallas kernels, body(): call(functools.partial(own_kernel, plan), [VMEM] * 4, jax.ShapeDtypeStruc...  0.83 us
    ppermute x1, waiting for transfers between devices, body(): partner = lax.ppermute(arrived, 'rep', swap)  0.72 us
  transfers between devices with their start and end apart: 4, of which 3 were waited for; matrix products, arithmetic and copies ran while one was open for 0% of the time, Pallas kernels for 7%

profile of v7, /device:TPU:0, one launch (start us, length us, event | category | flops | bytes accessed | tf_op | source)
XLA Modules:
  0.0 35.2 jit_solution(6305488148203427277)
XLA Ops:
  0.0 0.0 copy-start.3
  0.0 0.0 copy-start.4
  0.0 0.0 copy-start.5
  0.0 0.6 %collective-permute-start.2 = (bf16[512,3584]{1,0:T(8,128)(2,1)}, bf16[512,3584]{1,0:T(8,128)(2,1)S(1)}, u32[]{:S(2)}, u32[]{:S(2)}) collective-permute-start(bf16[512,3584]{1,0:T(8,128)(2,1)} %bitcast.10), channel_id=1, source_target_pairs={{0,1},{1,0},{2,3},{3,2},{4,5},{5,4},{6,7},{7,6},{8,9},{9,8},{10,11... | collective-permute-start | bytes 11010056 | tf_op jit(solution)/shard_map/ppermute | solution.py:324
  0.6 0.1 copy-done.3
  0.7 0.0 copy-done.4
  0.7 0.2 shard_map.74.found_ref
  0.8 0.1 copy-done.5
  0.9 0.0 copy-start
  0.9 0.0 copy-start.1
  0.9 0.0 copy-start.2
  0.9 0.2 shard_map.76
  1.2 15.3 %all_to_all.10.packed_ref = bf16[8,35,4,128]{3,2,1,0:T(4,128)(2,1)S(1)} all-to-all(bf16[8,35,4,128]{3,2,1,0:T(4,128)(2,1)S(1)} %shard_map.76), channel_id=1, replica_groups={{10,8,12,6,14,4,0,2},{11,9,13,7,15,5,1,3},{26,24,28,22,30,20,16,18},{27..., dimensions={0} | all-to-all | bytes 573440 | tf_op jit(solution)/shard_map/all_to_all | solution.py:62
  16.4 0.0 collective-permute-start
  16.4 0.0 copy-done
  16.4 0.0 copy-done.1
  16.4 0.0 copy-done.2
  16.5 0.8 %shard_map.77.acc_ref = f32[80,1024]{1,0:T(8,128)S(1)} custom-call(bf16[8,35,4,128]{3,2,1,0:T(4,128)(2,1)S(1)} %all_to_all.10.packed_ref, bf16[3584,512]{1,0:T(8,128)(2,1)S(1)} %bitcast.6, bf16[3584,512]{1,0:T(8,128)(2,1)S(1)} %bitcast.8, bf16[512,3584]{1,0:T(8,128)(2,1)S(1)} %bitcast.11), custom_call_target="tpu_custom_call" | custom-call | flops 1024 | bytes 1024 | tf_op jit(solution)/shard_map/pallas_call | solution.py:346
  17.3 0.7 %collective-permute-done.packed_ref = bf16[8,35,4,128]{3,2,1,0:T(4,128)(2,1)S(1)} collective-permute-done((bf16[8,35,4,128]{3,2,1,0:T(4,128)(2,1)S(1)}, bf16[8,35,4,128]{3,2,1,0:T(4,128)(2,1)S(1)}, u32[]{:S(2)}, u32[]{:S(2)}) %collective-permute-start) | collective-permute-done | bytes 286752 | tf_op jit(solution)/shard_map/ppermute | solution.py:345
  18.0 0.8 %shard_map.78.hidden_ref = bf16[80,512]{1,0:T(8,128)(2,1)S(1)} custom-call(bf16[8,35,4,128]{3,2,1,0:T(4,128)(2,1)S(1)} %collective-permute-done.packed_ref, f32[80,1024]{1,0:T(8,128)S(1)} %shard_map.77.acc_ref, bf16[3584,512]{1,0:T(8,128)(2,1)S(1)} %bitcast.7, bf16[3584,512]{1,0:T(8,128)(2,1)S(1)} %bitcast.9), custom_call_target="tpu_custom_call" | custom-call | flops 293601280 | bytes 614400 | tf_op jit(solution)/shard_map/pallas_call | solution.py:366
  18.8 0.2 collective-permute-start.1
  19.0 0.4 %shard_map.79.mine_ref = f32[80,1792]{1,0:T(8,128)S(1)} custom-call(bf16[80,512]{1,0:T(8,128)(2,1)S(1)} %shard_map.78.hidden_ref, bf16[512,3584]{1,0:T(8,128)(2,1)S(1)} %bitcast.12), custom_call_target="tpu_custom_call" | custom-call | flops 176160768 | bytes 573440 | tf_op jit(solution)/shard_map/pallas_call | solution.py:376
  19.5 0.0 copy-start.6
  19.5 0.7 %collective-permute-done.1.hidden_ref = bf16[80,512]{1,0:T(8,128)(2,1)S(1)} collective-permute-done((bf16[80,512]{1,0:T(8,128)(2,1)S(1)}, bf16[80,512]{1,0:T(8,128)(2,1)S(1)}, u32[]{:S(2)}, u32[]{:S(2)}) %collective-permute-start.1) | collective-permute-done | bytes 81952 | tf_op jit(solution)/shard_map/ppermute | solution.py:375
  20.2 0.0 collective-permute-done.2.down_ref
  20.2 1.2 %shard_map.80 = bf16[8,35,4,128]{3,2,1,0:T(4,128)(2,1)} custom-call(bf16[80,512]{1,0:T(8,128)(2,1)S(1)} %collective-permute-done.1.hidden_ref, bf16[512,3584]{1,0:T(8,128)(2,1)S(1)} %collective-permute-done.2.down_ref, f32[80,1792]{1,0:T(8,128)S(1)} %shard_map.79.mine_ref), custom_call_target="tpu_custom_call" | custom-call | flops 176160768 | bytes 573440 | tf_op jit(solution)/shard_map/pallas_call | solution.py:384
  21.4 5.7 %all-to-all-start.1 = ((bf16[8,35,4,128]{3,2,1,0:T(4,128)(2,1)}), bf16[8,35,4,128]{3,2,1,0:T(4,128)(2,1)S(1)}, u32[]{:S(2)}, u32[]{:S(2)}) async-start(bf16[8,35,4,128]{3,2,1,0:T(4,128)(2,1)} %shard_map.80), calls=%async_computation.1 | async-start | bytes 573440 | tf_op jit(solution)/shard_map/all_to_all | solution.py:62
  27.1 0.0 copy-done.6
  27.1 0.1 shard_map.75
  27.2 7.1 %all-to-all-done.1.packed_ref = bf16[8,35,4,128]{3,2,1,0:T(4,128)(2,1)S(1)} async-done(((bf16[8,35,4,128]{3,2,1,0:T(4,128)(2,1)}), bf16[8,35,4,128]{3,2,1,0:T(4,128)(2,1)S(1)}, u32[]{:S(2)}, u32[]{:S(2)}) %all-to-all-start.1) | async-done | bytes 286752 | tf_op jit(solution)/shard_map/all_to_all | solution.py:62
  34.3 0.8 %shard_map.81 = bf16[32,1792]{1,0:T(8,128)(2,1)} custom-call(bf16[2,32,96]{2,1,0:T(8,128)(2,1)S(1)} %get-tuple-element.7.pick_ref, f32[32,1]{1,0:T(8,128)S(1)} %get-tuple-element.8.column_ref, bf16[8,35,4,128]{3,2,1,0:T(4,128)(2,1)S(1)} %all-to-all-done.1.packed_ref), custom_call_target="tpu_custom_call" | custom-call | flops 11010048 | bytes 573440 | tf_op jit(solution)/shard_map/pallas_call | solution.py:393
  (1 shorter events, 0.0 us)
Async XLA Ops:
  0.0 0.7 %copy-start.3 = (s32[8]{0:T(128)S(1)}, s32[8]{0:T(128)}, u32[]{:S(2)}) copy-start(s32[8]{0:T(128)} %param.10) | copy-start | bytes 100
  0.0 0.7 %copy-start.4 = (s32[32,1]{0,1:T(1,128)S(1)}, s32[32,1]{0,1:T(1,128)}, u32[]{:S(2)}) copy-start(s32[32,1]{0,1:T(1,128)} %param.8) | copy-start | bytes 388
  0.0 0.9 %copy-start.5 = (bf16[32,1792]{1,0:T(8,128)(2,1)S(1)}, bf16[32,1792]{1,0:T(8,128)(2,1)}, u32[]{:S(2)}) copy-start(bf16[32,1792]{1,0:T(8,128)(2,1)} %tokens_ref.1) | copy-start | bytes 344068
  0.0 20.2 %collective-permute-start.2 = (bf16[512,3584]{1,0:T(8,128)(2,1)}, bf16[512,3584]{1,0:T(8,128)(2,1)S(1)}, u32[]{:S(2)}, u32[]{:S(2)}) collective-permute-start(bf16[512,3584]{1,0:T(8,128)(2,1)} %bitcast.10), channel_id=1, source_target_pairs={{0,1},{1,0},{2,3},{3,2},{4,5},{5,4},{6,7},{7,6},{8,9},{9,8},{10,11... | collective-permute-start | bytes 11010056 | tf_op jit(solution)/shard_map/ppermute | solution.py:324
  0.9 15.5 %copy-start = (bf16[1,3584,512]{2,1,0:T(8,128)(2,1)S(1)}, bf16[1,3584,512]{2,1,0:T(8,128)(2,1)}, u32[]{:S(2)}) copy-start(bf16[1,3584,512]{2,1,0:T(8,128)(2,1)} %param.11) | copy-start | bytes 11010052
  0.9 15.5 %copy-start.1 = (bf16[1,3584,512]{2,1,0:T(8,128)(2,1)S(1)}, bf16[1,3584,512]{2,1,0:T(8,128)(2,1)}, u32[]{:S(2)}) copy-start(bf16[1,3584,512]{2,1,0:T(8,128)(2,1)} %param.12) | copy-start | bytes 11010052
  0.9 15.5 %copy-start.2 = (bf16[1,512,3584]{2,1,0:T(8,128)(2,1)S(1)}, bf16[1,512,3584]{2,1,0:T(8,128)(2,1)}, u32[]{:S(2)}) copy-start(bf16[1,512,3584]{2,1,0:T(8,128)(2,1)} %param.13) | copy-start | bytes 11010052
  16.4 1.6 %collective-permute-start = (bf16[8,35,4,128]{3,2,1,0:T(4,128)(2,1)S(1)}, bf16[8,35,4,128]{3,2,1,0:T(4,128)(2,1)S(1)}, u32[]{:S(2)}, u32[]{:S(2)}) collective-permute-start(bf16[8,35,4,128]{3,2,1,0:T(4,128)(2,1)S(1)} %all_to_all.10.packed_ref), channel_id=1, source_target_pairs={{0,1},{1,0},{2,3},{3,2},{4,5},{5,4},{6,7},{7,6},{8,9},{9,8},{10,11... | collective-permute-start | bytes 860168 | tf_op jit(solution)/shard_map/ppermute | solution.py:345
  18.8 1.3 %collective-permute-start.1 = (bf16[80,512]{1,0:T(8,128)(2,1)S(1)}, bf16[80,512]{1,0:T(8,128)(2,1)S(1)}, u32[]{:S(2)}, u32[]{:S(2)}) collective-permute-start(bf16[80,512]{1,0:T(8,128)(2,1)S(1)} %shard_map.78.hidden_ref), channel_id=1, source_target_pairs={{0,1},{1,0},{2,3},{3,2},{4,5},{5,4},{6,7},{7,6},{8,9},{9,8},{10,11... | collective-permute-start | bytes 245768 | tf_op jit(solution)/shard_map/ppermute | solution.py:375
  19.5 7.6 %copy-start.6 = (f32[32,1]{0,1:T(1,128)S(1)}, f32[32,1]{0,1:T(1,128)}, u32[]{:S(2)}) copy-start(f32[32,1]{0,1:T(1,128)} %param.9) | copy-start | bytes 388
  21.4 12.9 %all-to-all-start.1 = ((bf16[8,35,4,128]{3,2,1,0:T(4,128)(2,1)}), bf16[8,35,4,128]{3,2,1,0:T(4,128)(2,1)S(1)}, u32[]{:S(2)}, u32[]{:S(2)}) async-start(bf16[8,35,4,128]{3,2,1,0:T(4,128)(2,1)} %shard_map.80), calls=%async_computation.1 | async-start | bytes 573440 | tf_op jit(solution)/shard_map/all_to_all | solution.py:62

commit v8 on v7

--- a/solution.py
+++ b/solution.py
@@ -41,10 +41,6 @@
 
 def iota(shape, dim):
     return lax.broadcasted_iota(jnp.int32, shape, dim)
-
-
-def floor_div(values, divisor):
-    return jnp.floor((values.astype(F32) + 0.5) * (1.0 / divisor)).astype(jnp.int32)
 
 
 def exchange_place(index, members):
@@ -189,23 +185,14 @@
                 for sender in range(plan.slots):
                     first = sender * plan.main + index * TILE_ROWS
                     rows_ref[first : first + TILE_ROWS, lane_block(block)] = tile[sender]
-    if plan.tail:
-        shape = (plan.group * plan.tail_rows, plan.tail_wide)
-        line = iota(shape, 0)
-        part = floor_div(line, plan.tail_rows)
-        inner = line - part * plan.tail_rows
-        sender = floor_div(inner, plan.tail)
-        spot = sender * TILE_ROWS + part * plan.tail + inner - sender * plan.tail
-        hot = jnp.where(spot == iota(shape, 1), 1.0, 0.0).astype(BF16)
-        for index in range(plan.tail_tiles):
-            tile = flat_tile(packed_ref[:, plan.full * plan.blocks + index])
-            moved = jnp.dot(hot, tile, preferred_element_type=F32).astype(BF16)
-            for part in range(plan.group):
-                block = index * plan.group + part
-                if block < plan.blocks:
-                    rows_ref[plan.main_rows : plan.rows, lane_block(block)] = moved[
-                        part * plan.tail_rows : (part + 1) * plan.tail_rows
-                    ]
+    for index in range(plan.tail_tiles):
+        tile = packed_ref[:, plan.full * plan.blocks + index]
+        for part in range(plan.group):
+            block = index * plan.group + part
+            if block < plan.blocks:
+                piece = tile.astype(F32)[:, part * plan.tail : (part + 1) * plan.tail]
+                piece = piece.reshape(plan.tail_rows, LANES).astype(BF16)
+                rows_ref[plan.main_rows : plan.rows, lane_block(block)] = piece
 
 
 def own_kernel(plan, packed_ref, gate_ref, up_ref, down_ref, acc_ref, rows_ref):

time: 35.4 us -> 35.4 us (level)
  no operation moved by 1% of the time
where the time goes in v8:
time: 35.4 us; the launch traced here: 35.1 us
  blocking collectives  15.3 us (43%)
  waiting for transfers between devices  8.59 us (24%)
  starting transfers between devices  6.46 us (18%)
  Pallas kernels  4.56 us (13%)
    all_to_all x1, blocking collectives, exchange(): lax.all_to_all(array, 'ep', split_axis=0, concat_axis=0, tiled=True, axis...  15.3 us
    all_to_all x1, waiting for transfers between devices, exchange(): lax.all_to_all(array, 'ep', split_axis=0, concat_axis=0, tiled=True, axis...  7.13 us
    all_to_all x1, starting transfers between devices, exchange(): lax.all_to_all(array, 'ep', split_axis=0, concat_axis=0, tiled=True, axis...  5.69 us
    pallas_call x1, Pallas kernels, body(): call(functools.partial(down_other_kernel, plan), [VMEM] * 3, packed, 2 *...  1.19 us
    pallas_call x1, Pallas kernels, body(): call(functools.partial(combine_kernel, plan), [VMEM, VMEM, VMEM], jax.Sha...  0.85 us
    pallas_call x1, Pallas kernels, body(): call(functools.partial(other_kernel, plan), [VMEM] * 4, jax.ShapeDtypeStr...  0.81 us
    pallas_call x1, Pallas kernels, body(): call(functools.partial(own_kernel, plan), [VMEM] * 4, jax.ShapeDtypeStruc...  0.79 us
    ppermute x1, waiting for transfers between devices, body(): partner = lax.ppermute(arrived, 'rep', swap)  0.76 us
  transfers between devices with their start and end apart: 4, of which 3 were waited for; matrix products, arithmetic and copies ran while one was open for 0% of the time, Pallas kernels for 7%

profile of v8, /device:TPU:0, one launch (start us, length us, event | category | flops | bytes accessed | tf_op | source)
XLA Modules:
  0.0 35.1 jit_solution(3168941881970596091)
XLA Ops:
  0.0 0.0 copy-start.3
  0.0 0.0 copy-start.4
  0.0 0.0 copy-start.5
  0.0 0.6 %collective-permute-start.2 = (bf16[512,3584]{1,0:T(8,128)(2,1)}, bf16[512,3584]{1,0:T(8,128)(2,1)S(1)}, u32[]{:S(2)}, u32[]{:S(2)}) collective-permute-start(bf16[512,3584]{1,0:T(8,128)(2,1)} %bitcast.10), channel_id=1, source_target_pairs={{0,1},{1,0},{2,3},{3,2},{4,5},{5,4},{6,7},{7,6},{8,9},{9,8},{10,11... | collective-permute-start | bytes 11010056 | tf_op jit(solution)/shard_map/ppermute | solution.py:311
  0.6 0.1 copy-done.3
  0.7 0.0 copy-done.4
  0.7 0.2 shard_map.74.found_ref
  0.8 0.1 copy-done.5
  0.9 0.0 copy-start
  0.9 0.0 copy-start.1
  0.9 0.0 copy-start.2
  0.9 0.2 shard_map.76
  1.2 15.3 %all_to_all.10.packed_ref = bf16[8,35,4,128]{3,2,1,0:T(4,128)(2,1)S(1)} all-to-all(bf16[8,35,4,128]{3,2,1,0:T(4,128)(2,1)S(1)} %shard_map.76), channel_id=1, replica_groups={{10,8,12,6,14,4,0,2},{11,9,13,7,15,5,1,3},{26,24,28,22,30,20,16,18},{27..., dimensions={0} | all-to-all | bytes 573440 | tf_op jit(solution)/shard_map/all_to_all | solution.py:58
  16.4 0.0 collective-permute-start
  16.4 0.0 copy-done
  16.4 0.0 copy-done.1
  16.4 0.0 copy-done.2
  16.5 0.8 %shard_map.77.acc_ref = f32[80,1024]{1,0:T(8,128)S(1)} custom-call(bf16[8,35,4,128]{3,2,1,0:T(4,128)(2,1)S(1)} %all_to_all.10.packed_ref, bf16[3584,512]{1,0:T(8,128)(2,1)S(1)} %bitcast.6, bf16[3584,512]{1,0:T(8,128)(2,1)S(1)} %bitcast.8, bf16[512,3584]{1,0:T(8,128)(2,1)S(1)} %bitcast.11), custom_call_target="tpu_custom_call" | custom-call | flops 1024 | bytes 1024 | tf_op jit(solution)/shard_map/pallas_call | solution.py:333
  17.2 0.8 %collective-permute-done.packed_ref = bf16[8,35,4,128]{3,2,1,0:T(4,128)(2,1)S(1)} collective-permute-done((bf16[8,35,4,128]{3,2,1,0:T(4,128)(2,1)S(1)}, bf16[8,35,4,128]{3,2,1,0:T(4,128)(2,1)S(1)}, u32[]{:S(2)}, u32[]{:S(2)}) %collective-permute-start) | collective-permute-done | bytes 286752 | tf_op jit(solution)/shard_map/ppermute | solution.py:332
  18.0 0.8 %shard_map.78.hidden_ref = bf16[80,512]{1,0:T(8,128)(2,1)S(1)} custom-call(bf16[8,35,4,128]{3,2,1,0:T(4,128)(2,1)S(1)} %collective-permute-done.packed_ref, f32[80,1024]{1,0:T(8,128)S(1)} %shard_map.77.acc_ref, bf16[3584,512]{1,0:T(8,128)(2,1)S(1)} %bitcast.7, bf16[3584,512]{1,0:T(8,128)(2,1)S(1)} %bitcast.9), custom_call_target="tpu_custom_call" | custom-call | flops 293601280 | bytes 614400 | tf_op jit(solution)/shard_map/pallas_call | solution.py:353
  18.8 0.2 collective-permute-start.1
  19.0 0.4 %shard_map.79.mine_ref = f32[80,1792]{1,0:T(8,128)S(1)} custom-call(bf16[80,512]{1,0:T(8,128)(2,1)S(1)} %shard_map.78.hidden_ref, bf16[512,3584]{1,0:T(8,128)(2,1)S(1)} %bitcast.12), custom_call_target="tpu_custom_call" | custom-call | flops 176160768 | bytes 573440 | tf_op jit(solution)/shard_map/pallas_call | solution.py:363
  19.5 0.0 copy-start.6
  19.5 0.7 %collective-permute-done.1.hidden_ref = bf16[80,512]{1,0:T(8,128)(2,1)S(1)} collective-permute-done((bf16[80,512]{1,0:T(8,128)(2,1)S(1)}, bf16[80,512]{1,0:T(8,128)(2,1)S(1)}, u32[]{:S(2)}, u32[]{:S(2)}) %collective-permute-start.1) | collective-permute-done | bytes 81952 | tf_op jit(solution)/shard_map/ppermute | solution.py:362
  20.2 0.0 collective-permute-done.2.down_ref
  20.2 1.2 %shard_map.80 = bf16[8,35,4,128]{3,2,1,0:T(4,128)(2,1)} custom-call(bf16[80,512]{1,0:T(8,128)(2,1)S(1)} %collective-permute-done.1.hidden_ref, bf16[512,3584]{1,0:T(8,128)(2,1)S(1)} %collective-permute-done.2.down_ref, f32[80,1792]{1,0:T(8,128)S(1)} %shard_map.79.mine_ref), custom_call_target="tpu_custom_call" | custom-call | flops 176160768 | bytes 573440 | tf_op jit(solution)/shard_map/pallas_call | solution.py:371
  21.4 5.7 %all-to-all-start.1 = ((bf16[8,35,4,128]{3,2,1,0:T(4,128)(2,1)}), bf16[8,35,4,128]{3,2,1,0:T(4,128)(2,1)S(1)}, u32[]{:S(2)}, u32[]{:S(2)}) async-start(bf16[8,35,4,128]{3,2,1,0:T(4,128)(2,1)} %shard_map.80), calls=%async_computation.1 | async-start | bytes 573440 | tf_op jit(solution)/shard_map/all_to_all | solution.py:58
  27.0 0.0 copy-done.6
  27.1 0.1 shard_map.75
  27.1 7.1 %all-to-all-done.1.packed_ref = bf16[8,35,4,128]{3,2,1,0:T(4,128)(2,1)S(1)} async-done(((bf16[8,35,4,128]{3,2,1,0:T(4,128)(2,1)}), bf16[8,35,4,128]{3,2,1,0:T(4,128)(2,1)S(1)}, u32[]{:S(2)}, u32[]{:S(2)}) %all-to-all-start.1) | async-done | bytes 286752 | tf_op jit(solution)/shard_map/all_to_all | solution.py:58
  34.3 0.8 %shard_map.81 = bf16[32,1792]{1,0:T(8,128)(2,1)} custom-call(bf16[2,32,96]{2,1,0:T(8,128)(2,1)S(1)} %get-tuple-element.7.pick_ref, f32[32,1]{1,0:T(8,128)S(1)} %get-tuple-element.8.column_ref, bf16[8,35,4,128]{3,2,1,0:T(4,128)(2,1)S(1)} %all-to-all-done.1.packed_ref), custom_call_target="tpu_custom_call" | custom-call | flops 11010048 | bytes 573440 | tf_op jit(solution)/shard_map/pallas_call | solution.py:380
  (1 shorter events, 0.0 us)
Async XLA Ops:
  0.0 0.7 %copy-start.3 = (s32[8]{0:T(128)S(1)}, s32[8]{0:T(128)}, u32[]{:S(2)}) copy-start(s32[8]{0:T(128)} %param.10) | copy-start | bytes 100
  0.0 0.7 %copy-start.4 = (s32[32,1]{0,1:T(1,128)S(1)}, s32[32,1]{0,1:T(1,128)}, u32[]{:S(2)}) copy-start(s32[32,1]{0,1:T(1,128)} %param.8) | copy-start | bytes 388
  0.0 0.9 %copy-start.5 = (bf16[32,1792]{1,0:T(8,128)(2,1)S(1)}, bf16[32,1792]{1,0:T(8,128)(2,1)}, u32[]{:S(2)}) copy-start(bf16[32,1792]{1,0:T(8,128)(2,1)} %tokens_ref.1) | copy-start | bytes 344068
  0.0 20.2 %collective-permute-start.2 = (bf16[512,3584]{1,0:T(8,128)(2,1)}, bf16[512,3584]{1,0:T(8,128)(2,1)S(1)}, u32[]{:S(2)}, u32[]{:S(2)}) collective-permute-start(bf16[512,3584]{1,0:T(8,128)(2,1)} %bitcast.10), channel_id=1, source_target_pairs={{0,1},{1,0},{2,3},{3,2},{4,5},{5,4},{6,7},{7,6},{8,9},{9,8},{10,11... | collective-permute-start | bytes 11010056 | tf_op jit(solution)/shard_map/ppermute | solution.py:311
  0.9 15.5 %copy-start = (bf16[1,3584,512]{2,1,0:T(8,128)(2,1)S(1)}, bf16[1,3584,512]{2,1,0:T(8,128)(2,1)}, u32[]{:S(2)}) copy-start(bf16[1,3584,512]{2,1,0:T(8,128)(2,1)} %param.11) | copy-start | bytes 11010052
  0.9 15.5 %copy-start.1 = (bf16[1,3584,512]{2,1,0:T(8,128)(2,1)S(1)}, bf16[1,3584,512]{2,1,0:T(8,128)(2,1)}, u32[]{:S(2)}) copy-start(bf16[1,3584,512]{2,1,0:T(8,128)(2,1)} %param.12) | copy-start | bytes 11010052
  0.9 15.5 %copy-start.2 = (bf16[1,512,3584]{2,1,0:T(8,128)(2,1)S(1)}, bf16[1,512,3584]{2,1,0:T(8,128)(2,1)}, u32[]{:S(2)}) copy-start(bf16[1,512,3584]{2,1,0:T(8,128)(2,1)} %param.13) | copy-start | bytes 11010052
  16.4 1.6 %collective-permute-start = (bf16[8,35,4,128]{3,2,1,0:T(4,128)(2,1)S(1)}, bf16[8,35,4,128]{3,2,1,0:T(4,128)(2,1)S(1)}, u32[]{:S(2)}, u32[]{:S(2)}) collective-permute-start(bf16[8,35,4,128]{3,2,1,0:T(4,128)(2,1)S(1)} %all_to_all.10.packed_ref), channel_id=1, source_target_pairs={{0,1},{1,0},{2,3},{3,2},{4,5},{5,4},{6,7},{7,6},{8,9},{9,8},{10,11... | collective-permute-start | bytes 860168 | tf_op jit(solution)/shard_map/ppermute | solution.py:332
  18.8 1.3 %collective-permute-start.1 = (bf16[80,512]{1,0:T(8,128)(2,1)S(1)}, bf16[80,512]{1,0:T(8,128)(2,1)S(1)}, u32[]{:S(2)}, u32[]{:S(2)}) collective-permute-start(bf16[80,512]{1,0:T(8,128)(2,1)S(1)} %shard_map.78.hidden_ref), channel_id=1, source_target_pairs={{0,1},{1,0},{2,3},{3,2},{4,5},{5,4},{6,7},{7,6},{8,9},{9,8},{10,11... | collective-permute-start | bytes 245768 | tf_op jit(solution)/shard_map/ppermute | solution.py:362
  19.5 7.6 %copy-start.6 = (f32[32,1]{0,1:T(1,128)S(1)}, f32[32,1]{0,1:T(1,128)}, u32[]{:S(2)}) copy-start(f32[32,1]{0,1:T(1,128)} %param.9) | copy-start | bytes 388
  21.4 12.9 %all-to-all-start.1 = ((bf16[8,35,4,128]{3,2,1,0:T(4,128)(2,1)}), bf16[8,35,4,128]{3,2,1,0:T(4,128)(2,1)S(1)}, u32[]{:S(2)}, u32[]{:S(2)}) async-start(bf16[8,35,4,128]{3,2,1,0:T(4,128)(2,1)} %shard_map.80), calls=%async_computation.1 | async-start | bytes 573440 | tf_op jit(solution)/shard_map/all_to_all | solution.py:58

commit v9 on v8

--- a/solution.py
+++ b/solution.py
@@ -254,7 +254,17 @@
 
 
 def down_other_kernel(plan, hidden_ref, down_ref, mine_ref, out_ref):
-    emit_packed(plan, mine_ref[...] + down_product(plan, hidden_ref, down_ref), out_ref)
+    first = pl.multiple_of(lax.axis_index("rep") * plan.feat, LANES)
+    half = (plan.blocks + 1) // 2 * LANES
+    parts = []
+    for start, size in ((0, half), (half, plan.feat - half)):
+        if size:
+            offset = pl.multiple_of(first + start, LANES)
+            piece = jnp.dot(
+                hidden_ref[...], down_ref[:, pl.ds(offset, size)], preferred_element_type=F32
+            )
+            parts.append(mine_ref[:, start : start + size] + piece)
+    emit_packed(plan, jnp.concatenate(parts, axis=1), out_ref)
 
 
 def combine_kernel(plan, pick_ref, column_ref, packed_ref, out_ref):

time: 35.4 us -> 35.3 us (level)
  no operation moved by 1% of the time
where the time goes in v9:
time: 35.3 us; the launch traced here: 35.1 us
  blocking collectives  15.3 us (43%)
  waiting for transfers between devices  8.58 us (24%)
  starting transfers between devices  6.45 us (18%)
  Pallas kernels  4.54 us (13%)
    all_to_all x1, blocking collectives, exchange(): lax.all_to_all(array, 'ep', split_axis=0, concat_axis=0, tiled=True, axis...  15.3 us
    all_to_all x1, waiting for transfers between devices, exchange(): lax.all_to_all(array, 'ep', split_axis=0, concat_axis=0, tiled=True, axis...  7.13 us
    all_to_all x1, starting transfers between devices, exchange(): lax.all_to_all(array, 'ep', split_axis=0, concat_axis=0, tiled=True, axis...  5.69 us
    pallas_call x1, Pallas kernels, body(): call(functools.partial(down_other_kernel, plan), [VMEM] * 3, packed, 2 *...  1.17 us
    pallas_call x1, Pallas kernels, body(): call(functools.partial(combine_kernel, plan), [VMEM, VMEM, VMEM], jax.Sha...  0.85 us
    pallas_call x1, Pallas kernels, body(): call(functools.partial(other_kernel, plan), [VMEM] * 4, jax.ShapeDtypeStr...  0.81 us
    pallas_call x1, Pallas kernels, body(): call(functools.partial(own_kernel, plan), [VMEM] * 4, jax.ShapeDtypeStruc...  0.79 us
    ppermute x1, waiting for transfers between devices, body(): partner = lax.ppermute(arrived, 'rep', swap)  0.76 us
  transfers between devices with their start and end apart: 4, of which 3 were waited for; matrix products, arithmetic and copies ran while one was open for 0% of the time, Pallas kernels for 7%

profile of v9, /device:TPU:0, one launch (start us, length us, event | category | flops | bytes accessed | tf_op | source)
XLA Modules:
  0.0 35.1 jit_solution(16603920841520235461)
XLA Ops:
  0.0 0.0 copy-start.3
  0.0 0.0 copy-start.4
  0.0 0.0 copy-start.5
  0.0 0.6 %collective-permute-start.2 = (bf16[512,3584]{1,0:T(8,128)(2,1)}, bf16[512,3584]{1,0:T(8,128)(2,1)S(1)}, u32[]{:S(2)}, u32[]{:S(2)}) collective-permute-start(bf16[512,3584]{1,0:T(8,128)(2,1)} %bitcast.10), channel_id=1, source_target_pairs={{0,1},{1,0},{2,3},{3,2},{4,5},{5,4},{6,7},{7,6},{8,9},{9,8},{10,11... | collective-permute-start | bytes 11010056 | tf_op jit(solution)/shard_map/ppermute | solution.py:321
  0.6 0.1 copy-done.3
  0.7 0.0 copy-done.4
  0.7 0.2 shard_map.74.found_ref
  0.8 0.1 copy-done.5
  0.9 0.0 copy-start
  0.9 0.0 copy-start.1
  0.9 0.0 copy-start.2
  0.9 0.2 shard_map.76
  1.2 15.3 %all_to_all.10.packed_ref = bf16[8,35,4,128]{3,2,1,0:T(4,128)(2,1)S(1)} all-to-all(bf16[8,35,4,128]{3,2,1,0:T(4,128)(2,1)S(1)} %shard_map.76), channel_id=1, replica_groups={{10,8,12,6,14,4,0,2},{11,9,13,7,15,5,1,3},{26,24,28,22,30,20,16,18},{27..., dimensions={0} | all-to-all | bytes 573440 | tf_op jit(solution)/shard_map/all_to_all | solution.py:58
  16.4 0.0 collective-permute-start
  16.4 0.0 copy-done
  16.4 0.0 copy-done.1
  16.4 0.0 copy-done.2
  16.5 0.8 %shard_map.77.acc_ref = f32[80,1024]{1,0:T(8,128)S(1)} custom-call(bf16[8,35,4,128]{3,2,1,0:T(4,128)(2,1)S(1)} %all_to_all.10.packed_ref, bf16[3584,512]{1,0:T(8,128)(2,1)S(1)} %bitcast.6, bf16[3584,512]{1,0:T(8,128)(2,1)S(1)} %bitcast.8, bf16[512,3584]{1,0:T(8,128)(2,1)S(1)} %bitcast.11), custom_call_target="tpu_custom_call" | custom-call | flops 1024 | bytes 1024 | tf_op jit(solution)/shard_map/pallas_call | solution.py:343
  17.2 0.8 %collective-permute-done.packed_ref = bf16[8,35,4,128]{3,2,1,0:T(4,128)(2,1)S(1)} collective-permute-done((bf16[8,35,4,128]{3,2,1,0:T(4,128)(2,1)S(1)}, bf16[8,35,4,128]{3,2,1,0:T(4,128)(2,1)S(1)}, u32[]{:S(2)}, u32[]{:S(2)}) %collective-permute-start) | collective-permute-done | bytes 286752 | tf_op jit(solution)/shard_map/ppermute | solution.py:342
  18.0 0.8 %shard_map.78.hidden_ref = bf16[80,512]{1,0:T(8,128)(2,1)S(1)} custom-call(bf16[8,35,4,128]{3,2,1,0:T(4,128)(2,1)S(1)} %collective-permute-done.packed_ref, f32[80,1024]{1,0:T(8,128)S(1)} %shard_map.77.acc_ref, bf16[3584,512]{1,0:T(8,128)(2,1)S(1)} %bitcast.7, bf16[3584,512]{1,0:T(8,128)(2,1)S(1)} %bitcast.9), custom_call_target="tpu_custom_call" | custom-call | flops 293601280 | bytes 614400 | tf_op jit(solution)/shard_map/pallas_call | solution.py:363
  18.8 0.2 collective-permute-start.1
  19.0 0.4 %shard_map.79.mine_ref = f32[80,1792]{1,0:T(8,128)S(1)} custom-call(bf16[80,512]{1,0:T(8,128)(2,1)S(1)} %shard_map.78.hidden_ref, bf16[512,3584]{1,0:T(8,128)(2,1)S(1)} %bitcast.12), custom_call_target="tpu_custom_call" | custom-call | flops 176160768 | bytes 573440 | tf_op jit(solution)/shard_map/pallas_call | solution.py:373
  19.5 0.0 copy-start.6
  19.5 0.7 %collective-permute-done.1.hidden_ref = bf16[80,512]{1,0:T(8,128)(2,1)S(1)} collective-permute-done((bf16[80,512]{1,0:T(8,128)(2,1)S(1)}, bf16[80,512]{1,0:T(8,128)(2,1)S(1)}, u32[]{:S(2)}, u32[]{:S(2)}) %collective-permute-start.1) | collective-permute-done | bytes 81952 | tf_op jit(solution)/shard_map/ppermute | solution.py:372
  20.2 0.0 collective-permute-done.2.down_ref
  20.2 1.2 %shard_map.80 = bf16[8,35,4,128]{3,2,1,0:T(4,128)(2,1)} custom-call(bf16[80,512]{1,0:T(8,128)(2,1)S(1)} %collective-permute-done.1.hidden_ref, bf16[512,3584]{1,0:T(8,128)(2,1)S(1)} %collective-permute-done.2.down_ref, f32[80,1792]{1,0:T(8,128)S(1)} %shard_map.79.mine_ref), custom_call_target="tpu_custom_call" | custom-call | flops 176160768 | bytes 573440 | tf_op jit(solution)/shard_map/pallas_call | solution.py:381
  21.3 5.7 %all-to-all-start.1 = ((bf16[8,35,4,128]{3,2,1,0:T(4,128)(2,1)}), bf16[8,35,4,128]{3,2,1,0:T(4,128)(2,1)S(1)}, u32[]{:S(2)}, u32[]{:S(2)}) async-start(bf16[8,35,4,128]{3,2,1,0:T(4,128)(2,1)} %shard_map.80), calls=%async_computation.1 | async-start | bytes 573440 | tf_op jit(solution)/shard_map/all_to_all | solution.py:58
  27.0 0.0 copy-done.6
  27.0 0.1 shard_map.75
  27.1 7.1 %all-to-all-done.1.packed_ref = bf16[8,35,4,128]{3,2,1,0:T(4,128)(2,1)S(1)} async-done(((bf16[8,35,4,128]{3,2,1,0:T(4,128)(2,1)}), bf16[8,35,4,128]{3,2,1,0:T(4,128)(2,1)S(1)}, u32[]{:S(2)}, u32[]{:S(2)}) %all-to-all-start.1) | async-done | bytes 286752 | tf_op jit(solution)/shard_map/all_to_all | solution.py:58
  34.3 0.8 %shard_map.81 = bf16[32,1792]{1,0:T(8,128)(2,1)} custom-call(bf16[2,32,96]{2,1,0:T(8,128)(2,1)S(1)} %get-tuple-element.7.pick_ref, f32[32,1]{1,0:T(8,128)S(1)} %get-tuple-element.8.column_ref, bf16[8,35,4,128]{3,2,1,0:T(4,128)(2,1)S(1)} %all-to-all-done.1.packed_ref), custom_call_target="tpu_custom_call" | custom-call | flops 11010048 | bytes 573440 | tf_op jit(solution)/shard_map/pallas_call | solution.py:390
  (1 shorter events, 0.0 us)
Async XLA Ops:
  0.0 0.7 %copy-start.3 = (s32[8]{0:T(128)S(1)}, s32[8]{0:T(128)}, u32[]{:S(2)}) copy-start(s32[8]{0:T(128)} %param.10) | copy-start | bytes 100
  0.0 0.7 %copy-start.4 = (s32[32,1]{0,1:T(1,128)S(1)}, s32[32,1]{0,1:T(1,128)}, u32[]{:S(2)}) copy-start(s32[32,1]{0,1:T(1,128)} %param.8) | copy-start | bytes 388
  0.0 0.9 %copy-start.5 = (bf16[32,1792]{1,0:T(8,128)(2,1)S(1)}, bf16[32,1792]{1,0:T(8,128)(2,1)}, u32[]{:S(2)}) copy-start(bf16[32,1792]{1,0:T(8,128)(2,1)} %tokens_ref.1) | copy-start | bytes 344068
  0.0 20.2 %collective-permute-start.2 = (bf16[512,3584]{1,0:T(8,128)(2,1)}, bf16[512,3584]{1,0:T(8,128)(2,1)S(1)}, u32[]{:S(2)}, u32[]{:S(2)}) collective-permute-start(bf16[512,3584]{1,0:T(8,128)(2,1)} %bitcast.10), channel_id=1, source_target_pairs={{0,1},{1,0},{2,3},{3,2},{4,5},{5,4},{6,7},{7,6},{8,9},{9,8},{10,11... | collective-permute-start | bytes 11010056 | tf_op jit(solution)/shard_map/ppermute | solution.py:321
  0.9 15.5 %copy-start = (bf16[1,3584,512]{2,1,0:T(8,128)(2,1)S(1)}, bf16[1,3584,512]{2,1,0:T(8,128)(2,1)}, u32[]{:S(2)}) copy-start(bf16[1,3584,512]{2,1,0:T(8,128)(2,1)} %param.11) | copy-start | bytes 11010052
  0.9 15.5 %copy-start.1 = (bf16[1,3584,512]{2,1,0:T(8,128)(2,1)S(1)}, bf16[1,3584,512]{2,1,0:T(8,128)(2,1)}, u32[]{:S(2)}) copy-start(bf16[1,3584,512]{2,1,0:T(8,128)(2,1)} %param.12) | copy-start | bytes 11010052
  0.9 15.5 %copy-start.2 = (bf16[1,512,3584]{2,1,0:T(8,128)(2,1)S(1)}, bf16[1,512,3584]{2,1,0:T(8,128)(2,1)}, u32[]{:S(2)}) copy-start(bf16[1,512,3584]{2,1,0:T(8,128)(2,1)} %param.13) | copy-start | bytes 11010052
  16.4 1.6 %collective-permute-start = (bf16[8,35,4,128]{3,2,1,0:T(4,128)(2,1)S(1)}, bf16[8,35,4,128]{3,2,1,0:T(4,128)(2,1)S(1)}, u32[]{:S(2)}, u32[]{:S(2)}) collective-permute-start(bf16[8,35,4,128]{3,2,1,0:T(4,128)(2,1)S(1)} %all_to_all.10.packed_ref), channel_id=1, source_target_pairs={{0,1},{1,0},{2,3},{3,2},{4,5},{5,4},{6,7},{7,6},{8,9},{9,8},{10,11... | collective-permute-start | bytes 860168 | tf_op jit(solution)/shard_map/ppermute | solution.py:342
  18.8 1.3 %collective-permute-start.1 = (bf16[80,512]{1,0:T(8,128)(2,1)S(1)}, bf16[80,512]{1,0:T(8,128)(2,1)S(1)}, u32[]{:S(2)}, u32[]{:S(2)}) collective-permute-start(bf16[80,512]{1,0:T(8,128)(2,1)S(1)} %shard_map.78.hidden_ref), channel_id=1, source_target_pairs={{0,1},{1,0},{2,3},{3,2},{4,5},{5,4},{6,7},{7,6},{8,9},{9,8},{10,11... | collective-permute-start | bytes 245768 | tf_op jit(solution)/shard_map/ppermute | solution.py:372
  19.5 7.6 %copy-start.6 = (f32[32,1]{0,1:T(1,128)S(1)}, f32[32,1]{0,1:T(1,128)}, u32[]{:S(2)}) copy-start(f32[32,1]{0,1:T(1,128)} %param.9) | copy-start | bytes 388
  21.3 12.9 %all-to-all-start.1 = ((bf16[8,35,4,128]{3,2,1,0:T(4,128)(2,1)}), bf16[8,35,4,128]{3,2,1,0:T(4,128)(2,1)S(1)}, u32[]{:S(2)}, u32[]{:S(2)}) async-start(bf16[8,35,4,128]{3,2,1,0:T(4,128)(2,1)} %shard_map.80), calls=%async_computation.1 | async-start | bytes 573440 | tf_op jit(solution)/shard_map/all_to_all | solution.py:58
